TPU v7x, 512 devices: a whole 4x4x16 slice. The times are simulated.
512 devices in a mesh: ctx: 64 (over x, z), head: 8 (over y, core).
Axes of the slice: x: 4, y: 4, z: 16, core: 2. Of those that a mesh axis runs over, the one named last changes fastest.
Arguments:
- queries: bfloat16 [32768, 4096], P('ctx', 'head'), may hold values from -6 to 6
- key_rows: bfloat16 [32768, 4096], P('ctx', 'head'), may hold values from -6 to 6
- value_rows: bfloat16 [32768, 4096], P('ctx', 'head'), may hold values from -6 to 6
- decay_rates: float32 [32], P('head'), as said below
- norm_gain: float32 [4096], P('head'), may hold values from 0.5 to 1.5
- out_grad: bfloat16 [32768, 4096], P('ctx', 'head'), may hold values from -6 to 6
Outputs:
- normed_out: bfloat16 [32768, 4096], P('ctx', 'head')
- query_grad: bfloat16 [32768, 4096], P('ctx', 'head')
- key_grad: bfloat16 [32768, 4096], P('ctx', 'head')
- value_grad: bfloat16 [32768, 4096], P('ctx', 'head')
Inputs may be any that keep to these rules, and one draw needn't show every extreme that they name: `decay_rates`: each head's decay factor per token is exp(-rate).
All inputs are finite; a program needn't handle non-finite values.
Results may differ from a plain program's by a relative error of at most 0.005.
Values sent between devices are 32-bit elements; how exact they have to be, the bound alone decides.
No kernel may reach another device: no remote copies, remote signals or barrier semaphores. Data moves between devices by JAX's collectives and lax.ppermute only.
A program may use at most 64 MiB of HBM per device.

v0:
```python
import jax
import jax.numpy as jnp
from jax import lax
from jax.sharding import Mesh
from jax.sharding import PartitionSpec as P

BLOCK = 256
CTX = ("ctx_0", "ctx_1")


highest = lax.Precision.HIGHEST
epsilon = 1e-06


def filled_with(array, identity):
    return jax.tree.map(
        lambda part, zero: jnp.zeros_like(part) + jnp.asarray(zero, part.dtype), array, identity
    )


def prefix_by_axis(array, axes, combine, identity, reverse):
    before = start = filled_with(array, identity)
    running = array
    for axis in reversed(axes):
        length, position = (lax.axis_size(axis), lax.axis_index(axis))
        pieces = jax.tree.map(lambda part: lax.all_gather(part, axis), running)
        inside, running = (start, start)
        for k in reversed(range(length)) if reverse else range(length):
            passed = k > position if reverse else k < position
            running = combine(running, jax.tree.map(lambda part: part[k], pieces))
            inside = jax.tree.map(lambda new, old: jnp.where(passed, new, old), running, inside)
        before = combine(inside, before)
    return before


def low_product(form, left, right):
    return jnp.einsum(form, left, right, preferred_element_type=jnp.float32)


def exact_product(form, left, right):
    return jnp.einsum(form, left, right, precision=highest)


def decay_tables(decay_rates, length):
    position = jnp.arange(length, dtype=jnp.float32)
    spacing = position[:, None] - position[None, :]
    weights = jnp.where(
        spacing[None] >= 0,
        jnp.exp(-decay_rates[:, None, None] * jnp.maximum(spacing, 0.0)[None]),
        0.0,
    )
    leading = jnp.exp(-decay_rates[None, :] * (position[:, None] + 1.0))
    trailing = jnp.exp(-decay_rates[None, :] * (length - 1.0 - position[:, None]))
    after_end = jnp.exp(-decay_rates[None, :] * (length - position[:, None]))
    from_start = jnp.exp(-decay_rates[None, :] * position[:, None])
    return (weights, leading, trailing, after_end, from_start)


def combine(earlier, latter):
    return (earlier[0] * latter[0], latter[0][:, None, None] * earlier[1] + latter[1])


def local_forward(query_blocks, key_blocks, value_blocks, decay_rates):
    head_width = query_blocks.shape[3]
    weights, leading, trailing, _, _ = decay_tables(decay_rates, query_blocks.shape[1])
    full_decay = jnp.exp(-decay_rates * query_blocks.shape[1])[:, None, None]

    def advance(memory, blocks):
        query_rows, key_part, value_part = blocks
        scores = low_product("ihd,jhd->hij", query_rows, key_part)
        attn_probs = (scores * weights).astype(jnp.bfloat16)
        inside = low_product("hij,jhd->ihd", attn_probs, value_part)
        carried = (
            exact_product("iha,hac->ihc", query_rows.astype(jnp.float32), memory)
            * leading[:, :, None]
        )
        update = exact_product(
            "jha,jhc->hac",
            key_part.astype(jnp.float32) * trailing[:, :, None],
            value_part.astype(jnp.float32),
        )
        return (full_decay * memory + update, (inside + carried, memory))

    initial = jnp.zeros((decay_rates.shape[0], head_width, head_width), jnp.float32)
    return lax.scan(advance, initial, (query_blocks, key_blocks, value_blocks))


def local_backward(query_blocks, key_blocks, value_blocks, grad_blocks, entering, decay_rates):
    head_width = query_blocks.shape[3]
    weights, leading, _, after_end, from_start = decay_tables(decay_rates, query_blocks.shape[1])
    full_decay = jnp.exp(-decay_rates * query_blocks.shape[1])[:, None, None]

    def retreat(backlog, blocks):
        query_rows, key_part, value_part, grad_rows, memory = blocks
        scores = low_product("ihd,jhd->hij", query_rows, key_part)
        attn_probs = (scores * weights).astype(jnp.bfloat16)
        grad_scores = low_product("ihc,jhc->hij", grad_rows, value_part)
        grad_probs = (grad_scores * weights).astype(jnp.bfloat16)
        grad_wide = grad_rows.astype(jnp.float32)
        query_out = low_product("hij,jha->iha", grad_probs, key_part)
        query_out = (
            query_out + exact_product("ihc,hac->iha", grad_wide, memory) * leading[:, :, None]
        )
        key_out = low_product("hij,iha->jha", grad_probs, query_rows)
        key_out = (
            key_out
            + exact_product("jhc,hac->jha", value_part.astype(jnp.float32), backlog)
            * after_end[:, :, None]
        )
        value_out = low_product("hij,ihc->jhc", attn_probs, grad_rows)
        value_out = (
            value_out
            + exact_product("jha,hac->jhc", key_part.astype(jnp.float32), backlog)
            * after_end[:, :, None]
        )
        gathered = exact_product(
            "iha,ihc->hac", query_rows.astype(jnp.float32) * from_start[:, :, None], grad_wide
        )
        return (full_decay * backlog + gathered, (query_out, key_out, value_out))

    initial = jnp.zeros((decay_rates.shape[0], head_width, head_width), jnp.float32)
    return lax.scan(
        retreat,
        initial,
        (query_blocks, key_blocks, value_blocks, grad_blocks, entering),
        reverse=True,
    )


def on_device(queries, key_rows, value_rows, decay_rates, norm_gain, out_grad):
    token_count = queries.shape[0]
    head_count = decay_rates.shape[0]
    head_width = queries.shape[1] // head_count
    block_count = token_count // BLOCK

    def blocked(array):
        return array.reshape(block_count, BLOCK, head_count, head_width)

    query_blocks = blocked(queries)
    key_blocks = blocked(key_rows)
    value_blocks = blocked(value_rows)
    memory_end, (local_out, local_enter) = local_forward(
        query_blocks, key_blocks, value_blocks, decay_rates
    )
    device_decay = jnp.exp(-decay_rates * token_count)
    identity = (
        jnp.ones((head_count,), jnp.float32),
        jnp.zeros((head_count, head_width, head_width), jnp.float32),
    )
    memory_in = prefix_by_axis((device_decay, memory_end), CTX, combine, identity, False)[1]
    position = jnp.arange(token_count, dtype=jnp.float32)
    lead_device = jnp.exp(-decay_rates[None, :] * (position[:, None] + 1.0))
    query_flat = queries.reshape(token_count, head_count, head_width)
    attention = local_out.reshape(token_count, head_count, head_width)
    attention = (
        attention
        + exact_product("iha,hac->ihc", query_flat.astype(jnp.float32), memory_in)
        * lead_device[:, :, None]
    )
    block_start = jnp.arange(block_count, dtype=jnp.float32) * BLOCK
    entering = (
        jnp.exp(-decay_rates[None, :] * block_start[:, None])[:, :, None, None] * memory_in[None]
        + local_enter
    )
    flat = attention.reshape(token_count, head_count * head_width)
    features = float(norm_gain.shape[0] * lax.axis_size("head"))
    grad_normed = out_grad.astype(jnp.float32) * norm_gain[None, :]
    local_squares = jnp.sum(flat * flat, axis=1)
    local_projection = jnp.sum(grad_normed * flat, axis=1)
    total_squares, total_projection = lax.psum((local_squares, local_projection), "head")
    scale = lax.rsqrt(total_squares / features + epsilon)
    normed = flat * scale[:, None]
    normed_out = (normed * norm_gain[None, :]).astype(jnp.bfloat16)
    coeff = scale * total_projection / features
    grad_attn = (scale[:, None] * (grad_normed - normed * coeff[:, None])).astype(jnp.bfloat16)
    backlog_end, (query_part, key_part, value_part) = local_backward(
        query_blocks, key_blocks, value_blocks, blocked(grad_attn), entering, decay_rates
    )
    identity_back = (
        jnp.ones((head_count,), jnp.float32),
        jnp.zeros((head_count, head_width, head_width), jnp.float32),
    )
    backlog_after = prefix_by_axis((device_decay, backlog_end), CTX, combine, identity_back, True)[
        1
    ]
    tail_device = jnp.exp(-decay_rates[None, :] * (token_count - position[:, None]))[:, :, None]
    value_flat = value_rows.reshape(token_count, head_count, head_width).astype(jnp.float32)
    key_flat = key_rows.reshape(token_count, head_count, head_width).astype(jnp.float32)
    key_grad = (
        key_part.reshape(token_count, head_count, head_width)
        + exact_product("jhc,hac->jha", value_flat, backlog_after) * tail_device
    )
    value_grad = (
        value_part.reshape(token_count, head_count, head_width)
        + exact_product("jha,hac->jhc", key_flat, backlog_after) * tail_device
    )
    query_grad = query_part.reshape(token_count, head_count * head_width).astype(jnp.bfloat16)
    key_out = key_grad.reshape(token_count, head_count * head_width).astype(jnp.bfloat16)
    value_out = value_grad.reshape(token_count, head_count * head_width).astype(jnp.bfloat16)
    return (normed_out, query_grad, key_out, value_out)


def solution(mesh):
    split = Mesh(mesh.devices.reshape(4, 16, mesh.shape["head"]), ("ctx_0", "ctx_1", "head"))
    placed = (P(CTX, "head"), P(CTX, "head"), P(CTX, "head"), P("head"), P("head"), P(CTX, "head"))
    return jax.shard_map(
        on_device,
        mesh=split,
        in_specs=placed,
        out_specs=(P(CTX, "head"), P(CTX, "head"), P(CTX, "head"), P(CTX, "head")),
        check_vma=False,
    )
```

profile of v0, /device:TPU:8, one launch (start us, length us, event | category | flops | bytes accessed | tf_op | source)
XLA Modules:
  0.0 378.6 jit_solution(16742063409671422481)
XLA Ops:
  7.2 0.8 fusion.177
  8.1 1.2 reshape.412
  9.4 2.0 reshape.411
  11.3 1.2 reshape.413
  12.5 1.3 dynamic-slice
  14.8 25.1 %while.40 = (s32[]{:T(128)}, f32[4,128,128]{2,1,0:T(8,128)S(1)}, f32[2,256,4,128]{1,0,3,2:T(2,128)S(1)}, f32[2,4,128,128]{3,2,1,0:T(8,128)}, f32[4,1,1]{0,2,1:T(...) while((s32[]{:T(128)}, f32[4,128,128]{2,1,0:T(8,128)S(1)}, ...), condition=%wide.region_1.2_spmd.clone.clone.clone, body=%wide.region_0.1_spmd.clone.clone.clone.sunk | while | flops 538773504 | bytes 7950009 | solution.py:85
  14.8 1.1 constant_dynamic-slice_fusion.8
  16.0 1.5 convolution_bitcast_fusion.15
  18.5 7.3 %dynamic_update_slice.58 = f32[2,256,4,128]{1,0,3,2:T(2,128)S(1)} dynamic-update-slice(f32[2,256,4,128]{1,0,3,2:T(2,128)S(1)} %get-tuple-element.1065, f32[1,256,4,128]{1,0,3,2:T(1,128)S(1)} %copy.162, s32[]{:T(128)} %get-tuple-element.1063, s32[]{:T(128)} %constant.97.clone.1..sunk, s32[]{:T(128)} %constant.97.clone.1..sunk, s32[]{:T(128)} %constant.97.clone.1..sunk) | dynamic-update-slice | bytes 1048580 | tf_op jit(solution)/shard_map/while/body/jit(dynamic_update_index_in_dim)/dynamic_update_slice | solution.py:85
  25.8 0.7 bitcast_dynamic-update-slice_fusion.2
  26.6 0.8 convolution_add_fusion.4
  27.4 1.1 constant_dynamic-slice_fusion.8
  28.5 1.5 convolution_bitcast_fusion.15
  31.1 7.3 %dynamic_update_slice.58 = f32[2,256,4,128]{1,0,3,2:T(2,128)S(1)} dynamic-update-slice(f32[2,256,4,128]{1,0,3,2:T(2,128)S(1)} %get-tuple-element.1065, f32[1,256,4,128]{1,0,3,2:T(1,128)S(1)} %copy.162, s32[]{:T(128)} %get-tuple-element.1063, s32[]{:T(128)} %constant.97.clone.1..sunk, s32[]{:T(128)} %constant.97.clone.1..sunk, s32[]{:T(128)} %constant.97.clone.1..sunk) | dynamic-update-slice | bytes 1048580 | tf_op jit(solution)/shard_map/while/body/jit(dynamic_update_index_in_dim)/dynamic_update_slice | solution.py:85
  38.4 0.7 bitcast_dynamic-update-slice_fusion.2
  39.1 0.8 convolution_add_fusion.4
  40.0 0.7 copy-done
  40.7 36.5 %all-reduce = f32[64]{0:T(128)S(1)} all-reduce(f32[64]{0:T(128)S(1)} %get-tuple-element.845), channel_id=2, replica_groups=mesh['ctx_0'=4,'ctx_1'=16,'head'=8] {'ctx_1'}, use_global_device_ids=true, to_apply=%add | all-reduce | flops 64 | bytes 512
  77.3 0.6 fusion.257
  77.9 45.4 %all-gather.14.cloned.1.call-done = f32[64,128,128]{2,1,0:T(8,128)} async-done(((f32[4,128,128]{2,1,0:T(8,128)}), f32[64,128,128]{2,1,0:T(8,128)}) %all-gather.14.cloned.1.call-update) | async-done | bytes 4194320 | tf_op jit(solution)/shard_map/all_gather | solution.py:26
  123.3 3.3 bitcast_add_fusion.20
  126.8 9.4 %all-gather.3 = f32[4,1,4]{2,1,0:T(1,128)S(1)} all-gather(f32[1,1,4]{2,1,0:T(1,128)S(1)} %fusion.246), channel_id=1, replica_groups=mesh['ctx_0'=4,'ctx_1'=16,'head'=8] {'ctx_0'}, dimensions={0}, use_global_device_ids=true | all-gather | bytes 80 | tf_op jit(solution)/shard_map/all_gather | solution.py:26
  136.2 0.8 reshape.414
  137.2 0.7 multiply_exponential_fusion.7
  138.0 16.5 %all-gather.10.cloned.1.call-done = f32[4,4,128,128]{3,2,1,0:T(8,128)} async-done(((f32[1,4,128,128]{3,2,1,0:T(8,128)}), f32[4,4,128,128]{3,2,1,0:T(8,128)}) %all-gather.10.cloned.1.call-update) | async-done | bytes 1048592 | tf_op jit(solution)/shard_map/all_gather | solution.py:26
  154.5 5.6 %multiply_reduce_fusion.1 = (f32[512]{0:T(512)}, f32[512,4,128]{0,2,1:T(8,128)}) fusion(f32[512,4,128]{0,2,1:T(8,128)S(1)} %reshape.414, f32[512,4]{0,1:T(4,128)S(1)} %get-tuple-element.826, f32[4,4,128,128]{3,2,1,0:T(8,128)} %all-gather.10.cloned.1.call-done, f32[64,128,128]{2,1,0:T(8,128)} %all-gather.14.cloned.1.call-done, f32[4]{0:T(128)} %copy-done.19, ...), kind=kOutput, calls=%fused_computation.118 | convolution fusion | flops 407633408 | bytes 7874916 | tf_op jit(solution)/shard_map/iha,hac->ihc/dot_general | solution.py:41
  160.1 1.6 copy.72
  161.7 0.9 multiply_reduce_fusion
  162.6 10.9 %all-reduce.1 = (f32[512]{0:T(512)}, f32[512]{0:T(512)}) all-reduce(f32[512]{0:T(512)} %get-tuple-element.848, f32[512]{0:T(512)S(1)} %multiply_reduce_fusion), channel_id=1, replica_groups=mesh['ctx_0'=4,'ctx_1'=16,'head'=8] {'head'}, use_global_device_ids=true, to_apply=%region_3.4 | all-reduce | flops 1024 | bytes 8192 | tf_op jit(solution)/shard_map/psum | solution.py:170
  173.5 0.7 multiply_multiply_fusion
  174.2 2.0 multiply_convert_fusion
  176.2 2.0 reshape.417
  178.2 3.1 add_bitcast_fusion
  181.4 0.9 multiply_add_fusion
  182.3 1.3 broadcast.371.clone
  183.5 1.2 broadcast.371.clone2.1
  184.8 0.8 broadcast.371
  185.6 65.4 %while.41 = (s32[]{:T(128)}, f32[4,128,128]{2,1,0:T(8,128)S(1)}, bf16[2,256,4,128]{1,3,2,0:T(8,128)(2,1)}, f32[2,256,4,128]{1,0,3,2:T(2,128)}, f32[2,256,4,128]{...) while((s32[]{:T(128)}, f32[4,128,128]{2,1,0:T(8,128)S(1)}, ...), condition=%wide.region_7.8_spmd.clone.clone.clone, body=%wide.region_6.7_spmd.clone.clone.clone.sunk | while | flops 1144327168 | bytes 18251524 | solution.py:122
  185.6 1.2 constant_dynamic-slice_fusion.10
  186.8 1.3 fusion.305
  189.7 11.5 %dynamic_update_slice.60 = f32[2,256,4,128]{1,0,3,2:T(2,128)} dynamic-update-slice(f32[2,256,4,128]{1,0,3,2:T(2,128)} %get-tuple-element.1114, f32[1,256,4,128]{1,0,3,2:T(1,128)S(1)} %copy.169, s32[]{:T(128)S(6)} %sub.112, s32[]{:T(128)} %constant.97.clone.1..sunk.1, s32[]{:T(128)} %constant.97.clone.1..sunk.1, s32[]{:T(128)} %constant.97.clone.1..sunk.1) | dynamic-update-slice | bytes 1048580 | tf_op jit(solution)/shard_map/while/body/jit(dynamic_update_index_in_dim)/dynamic_update_slice | solution.py:85
  201.4 1.5 convolution_bitcast_fusion.18
  203.9 11.5 %dynamic_update_slice.61 = f32[2,256,4,128]{1,0,3,2:T(2,128)} dynamic-update-slice(f32[2,256,4,128]{1,0,3,2:T(2,128)} %get-tuple-element.1115, f32[1,256,4,128]{1,0,3,2:T(1,128)S(1)} %copy.170, s32[]{:T(128)S(6)} %sub.112, s32[]{:T(128)} %constant.97.clone.1..sunk.1, s32[]{:T(128)} %constant.97.clone.1..sunk.1, s32[]{:T(128)} %constant.97.clone.1..sunk.1) | dynamic-update-slice | bytes 1048580 | tf_op jit(solution)/shard_map/while/body/jit(dynamic_update_index_in_dim)/dynamic_update_slice | solution.py:85
  215.8 2.1 fusion.306
  218.3 1.2 constant_dynamic-slice_fusion.10
  219.5 1.3 fusion.305
  222.4 11.5 %dynamic_update_slice.60 = f32[2,256,4,128]{1,0,3,2:T(2,128)} dynamic-update-slice(f32[2,256,4,128]{1,0,3,2:T(2,128)} %get-tuple-element.1114, f32[1,256,4,128]{1,0,3,2:T(1,128)S(1)} %copy.169, s32[]{:T(128)S(6)} %sub.112, s32[]{:T(128)} %constant.97.clone.1..sunk.1, s32[]{:T(128)} %constant.97.clone.1..sunk.1, s32[]{:T(128)} %constant.97.clone.1..sunk.1) | dynamic-update-slice | bytes 1048580 | tf_op jit(solution)/shard_map/while/body/jit(dynamic_update_index_in_dim)/dynamic_update_slice | solution.py:85
  234.1 1.5 convolution_bitcast_fusion.18
  236.6 11.5 %dynamic_update_slice.61 = f32[2,256,4,128]{1,0,3,2:T(2,128)} dynamic-update-slice(f32[2,256,4,128]{1,0,3,2:T(2,128)} %get-tuple-element.1115, f32[1,256,4,128]{1,0,3,2:T(1,128)S(1)} %copy.170, s32[]{:T(128)S(6)} %sub.112, s32[]{:T(128)} %constant.97.clone.1..sunk.1, s32[]{:T(128)} %constant.97.clone.1..sunk.1, s32[]{:T(128)} %constant.97.clone.1..sunk.1) | dynamic-update-slice | bytes 1048580 | tf_op jit(solution)/shard_map/while/body/jit(dynamic_update_index_in_dim)/dynamic_update_slice | solution.py:85
  248.5 2.1 fusion.306
  251.0 0.7 copy-done.1
  251.8 79.1 %all-gather.16.cloned.1.call-done = f32[64,128,128]{2,1,0:T(8,128)} async-done(((f32[4,128,128]{2,1,0:T(8,128)}), f32[64,128,128]{2,1,0:T(8,128)}) %all-gather.16.cloned.1.call-update) | async-done | bytes 4194320 | tf_op jit(solution)/shard_map/all_gather | solution.py:26
  330.9 3.2 bitcast_add_fusion
  334.3 9.9 %all-gather.4 = f32[4,1,4]{2,1,0:T(1,128)S(1)} all-gather(f32[1,1,4]{2,1,0:T(1,128)S(1)} %fusion.255), channel_id=1, replica_groups=mesh['ctx_0'=4,'ctx_1'=16,'head'=8] {'ctx_0'}, dimensions={0}, use_global_device_ids=true | all-gather | bytes 80 | tf_op jit(solution)/shard_map/all_gather | solution.py:26
  344.3 0.8 reshape.420
  345.1 0.8 reshape.418
  346.0 1.4 copy.78
  347.4 0.9 copy.144
  348.3 14.3 %all-gather.12.cloned.1.call-done = f32[4,4,128,128]{3,2,1,0:T(8,128)} async-done(((f32[1,4,128,128]{3,2,1,0:T(8,128)}), f32[4,4,128,128]{3,2,1,0:T(8,128)}) %all-gather.12.cloned.1.call-update) | async-done | bytes 1048592 | tf_op jit(solution)/shard_map/all_gather | solution.py:26
  362.6 3.3 fusion.101
  365.9 1.4 fusion.91
  367.3 2.0 copy.85
  369.4 1.6 fusion.90
  371.0 1.0 copy.84
  (109 shorter events, 10.2 us)
Async XLA Ops:
  7.2 7.3 %copy-start.27 = (f32[4]{0:T(128)S(1)}, f32[4]{0:T(128)}, u32[]{:S(2)}) copy-start(f32[4]{0:T(128)} %param.13) | copy-start | bytes 52
  7.2 116.2 %all-gather.14.cloned.1.call-start = ((), (), s32[]{:S(2)}) async-start(), calls=%async_computation.2 | async-start | bytes 4456448 | tf_op jit(solution)/shard_map/all_gather | solution.py:26
  39.9 0.7 copy-start
  40.7 113.8 %all-gather.10.cloned.1.call-start = ((), (), s32[]{:S(2)}) async-start(), calls=%async_computation | async-start | bytes 1310720 | tf_op jit(solution)/shard_map/all_gather | solution.py:26
  77.9 48.8 %copy-start.19 = (f32[4]{0:T(128)}, f32[4]{0:T(128)S(1)}, u32[]{:S(2)}) copy-start(f32[4]{0:T(128)S(1)} %get-tuple-element.828) | copy-start | bytes 52
  77.9 59.1 %copy-start.15 = (f32[4]{0:T(128)}, f32[4]{0:T(128)S(1)}, u32[]{:S(2)}) copy-start(f32[4]{0:T(128)S(1)} %get-tuple-element.840) | copy-start | bytes 52
  77.9 60.0 %copy-start.21 = (f32[4]{0:T(128)}, f32[4]{0:T(128)S(1)}, u32[]{:S(2)}) copy-start(f32[4]{0:T(128)S(1)} %get-tuple-element.843) | copy-start | bytes 52
  77.9 82.1 %copy-start.11 = (f32[4]{0:T(128)}, f32[4]{0:T(128)S(1)}, u32[]{:S(2)}) copy-start(f32[4]{0:T(128)S(1)} %get-tuple-element.832) | copy-start | bytes 52
  77.9 82.1 %copy-start.13 = (f32[4]{0:T(128)}, f32[4]{0:T(128)S(1)}, u32[]{:S(2)}) copy-start(f32[4]{0:T(128)S(1)} %get-tuple-element.836) | copy-start | bytes 52
  77.9 100.3 %copy-start.9 = (f32[4]{0:T(128)}, f32[4]{0:T(128)S(1)}, u32[]{:S(2)}) copy-start(f32[4]{0:T(128)S(1)} %get-tuple-element.844) | copy-start | bytes 52
  126.6 204.2 %all-gather.16.cloned.1.call-start = ((), (), s32[]{:S(2)}) async-start(), calls=%async_computation.3 | async-start | bytes 4456448 | tf_op jit(solution)/shard_map/all_gather | solution.py:26
  137.2 17.3 %copy-start.22 = (f32[4]{0:T(128)}, f32[4]{0:T(128)S(1)}, u32[]{:S(2)}) copy-start(f32[4]{0:T(128)S(1)} %broadcast_select_fusion.31) | copy-start | bytes 52
  137.9 16.6 %copy-start.23 = (f32[4]{0:T(128)}, f32[4]{0:T(128)S(1)}, u32[]{:S(2)}) copy-start(f32[4]{0:T(128)S(1)} %get-tuple-element.821) | copy-start | bytes 52
  137.9 16.6 %copy-start.24 = (f32[4]{0:T(128)}, f32[4]{0:T(128)S(1)}, u32[]{:S(2)}) copy-start(f32[4]{0:T(128)S(1)} %get-tuple-element.822) | copy-start | bytes 52
  137.9 16.6 %copy-start.25 = (f32[4]{0:T(128)}, f32[4]{0:T(128)S(1)}, u32[]{:S(2)}) copy-start(f32[4]{0:T(128)S(1)} %get-tuple-element.823) | copy-start | bytes 52
  137.9 16.6 %copy-start.26 = (f32[4]{0:T(128)}, f32[4]{0:T(128)S(1)}, u32[]{:S(2)}) copy-start(f32[4]{0:T(128)S(1)} %get-tuple-element.824) | copy-start | bytes 52
  154.5 7.2 %copy-start.5 = (bf16[512,512]{1,0:T(8,128)(2,1)S(1)}, bf16[512,512]{1,0:T(8,128)(2,1)}, u32[]{:S(2)}) copy-start(bf16[512,512]{1,0:T(8,128)(2,1)} %param.15) | copy-start | bytes 1572868
  160.0 18.2 %copy-start.4 = (f32[1,4,128,128]{3,2,1,0:T(8,128)S(1)}, f32[1,4,128,128]{3,2,1,0:T(8,128)}, u32[]{:S(2)}) copy-start(f32[1,4,128,128]{3,2,1,0:T(8,128)} %get-tuple-element.800) | copy-start | bytes 786436
  160.1 18.2 %copy-start.7 = (f32[1,4,128,128]{3,2,1,0:T(8,128)S(1)}, f32[1,4,128,128]{3,2,1,0:T(8,128)}, u32[]{:S(2)}) copy-start(f32[1,4,128,128]{3,2,1,0:T(8,128)} %get-tuple-element.801) | copy-start | bytes 786436
  176.2 5.2 %copy-start.8 = (f32[2,4,128,128]{3,2,1,0:T(8,128)S(1)}, f32[2,4,128,128]{3,2,1,0:T(8,128)}, u32[]{:S(2)}) copy-start(f32[2,4,128,128]{3,2,1,0:T(8,128)} %get-tuple-element.361) | copy-start | bytes 1572868
  176.2 5.2 %copy-start.20 = (f32[2,4]{1,0:T(2,128)S(1)}, f32[2,4]{1,0:T(2,128)}, u32[]{:S(2)}) copy-start(f32[2,4]{1,0:T(2,128)} %multiply_exponential_fusion.7) | copy-start | bytes 100
  251.0 0.7 copy-start.1
  251.0 93.3 %copy-start.3 = (f32[2,256,4,128]{1,0,3,2:T(2,128)S(1)}, f32[2,256,4,128]{1,0,3,2:T(2,128)}, u32[]{:S(2)}) copy-start(f32[2,256,4,128]{1,0,3,2:T(2,128)} %get-tuple-element.365) | copy-start | bytes 3145732
  251.0 94.1 %copy-start.2 = (f32[2,256,4,128]{1,0,3,2:T(2,128)S(1)}, f32[2,256,4,128]{1,0,3,2:T(2,128)}, u32[]{:S(2)}) copy-start(f32[2,256,4,128]{1,0,3,2:T(2,128)} %get-tuple-element.363) | copy-start | bytes 3145732
  251.7 110.8 %all-gather.12.cloned.1.call-start = ((), (), s32[]{:S(2)}) async-start(), calls=%async_computation.1 | async-start | bytes 1310720 | tf_op jit(solution)/shard_map/all_gather | solution.py:26
  334.1 28.4 %copy-start.10 = (f32[4]{0:T(128)S(1)}, f32[4]{0:T(128)}, u32[]{:S(2)}) copy-start(f32[4]{0:T(128)} %copy-done.9) | copy-start | bytes 52
  334.1 28.4 %copy-start.12 = (f32[4]{0:T(128)S(1)}, f32[4]{0:T(128)}, u32[]{:S(2)}) copy-start(f32[4]{0:T(128)} %copy-done.11) | copy-start | bytes 52
  334.1 28.4 %copy-start.14 = (f32[4]{0:T(128)S(1)}, f32[4]{0:T(128)}, u32[]{:S(2)}) copy-start(f32[4]{0:T(128)} %copy-done.13) | copy-start | bytes 52
  334.1 28.4 %copy-start.16 = (f32[4]{0:T(128)S(1)}, f32[4]{0:T(128)}, u32[]{:S(2)}) copy-start(f32[4]{0:T(128)} %copy-done.15) | copy-start | bytes 52
  334.1 28.4 %copy-start.17 = (f32[4]{0:T(128)S(1)}, f32[4]{0:T(128)}, u32[]{:S(2)}) copy-start(f32[4]{0:T(128)} %get-tuple-element.827) | copy-start | bytes 52
  334.2 28.4 %copy-start.18 = (f32[4]{0:T(128)S(1)}, f32[4]{0:T(128)}, u32[]{:S(2)}) copy-start(f32[4]{0:T(128)} %get-tuple-element.829) | copy-start | bytes 52
  346.0 19.9 %copy-start.6 = (bf16[512,512]{1,0:T(8,128)(2,1)S(1)}, bf16[512,512]{1,0:T(8,128)(2,1)}, u32[]{:S(2)}) copy-start(bf16[512,512]{1,0:T(8,128)(2,1)} %param.11) | copy-start | bytes 1572868
Sparse Core Ops, SparseCore 0:
  40.8 82.4 all-gather.13
  126.7 27.6 all-gather.9
  251.8 78.9 all-gather.15
  334.3 28.1 all-gather.11
where the time goes:
time: 382 us; the launch traced here: 379 us
  waiting for transfers between devices  155 us (41%)
  local copies, waits for them, and re-layouts  91.7 us (24%)
  blocking collectives  66.7 us (17%)
  matrix products  27.5 us (7%)
  other arithmetic  21.9 us (6%)
  between operations  14.9 us (4%)
    all_gather x4, waiting for transfers between devices, prefix_by_axis(): pieces = jax.tree.map(lambda part: lax.all_gather(part, axis), running)  155 us
    dynamic_update_slice x12, local copies, waits for them, and re-layouts, local_forward(): return lax.scan(advance, initial, (query_blocks, key_blocks, value_blocks))  63.9 us
    unnamed x1, blocking collectives  36.5 us
    all_gather x2, blocking collectives, prefix_by_axis(): pieces = jax.tree.map(lambda part: lax.all_gather(part, axis), running)  19.3 us
    dot_general x15, matrix products, exact_product(): return jnp.einsum(form, left, right, precision=highest)  17.7 us
    psum x1, blocking collectives, on_device(): lax.psum((local_squares, local_projection), 'head')  10.9 us
    add x3, other arithmetic, combine(): latter[0][:, None, None] * earlier[1] + latter[1]  9.82 us
    dot_general x10, matrix products, low_product(): return jnp.einsum(form, left, right, preferred_element_type=jnp.float32)  9.74 us
  transfers between devices with their start and end apart: 4, of which 4 were waited for; matrix products, arithmetic and copies ran while one was open for 2% of the time, Pallas kernels for 0%

commit v1 on v0

v1 whole, which is shorter than its diff:
```python
import functools

import jax
import jax.numpy as jnp
from jax import lax
from jax.experimental import pallas as pl
from jax.experimental.pallas import tpu as pltpu
from jax.sharding import Mesh
from jax.sharding import PartitionSpec as P

BLOCK = 256
LINE = ("ctx_0", "ctx_1")
EPSILON = 1e-06
F32 = jnp.float32
BF16 = jnp.bfloat16
SMEM = pl.BlockSpec(memory_space=pltpu.SMEM)
VMEM = pl.BlockSpec(memory_space=pltpu.VMEM)


def dot(left, right, left_dim, right_dim):
    return lax.dot_general(
        left, right, (((left_dim,), (right_dim,)), ((), ())), preferred_element_type=F32
    )


def halves(wide):
    high = wide.astype(BF16)
    return high, (wide - high.astype(F32)).astype(BF16)


def dot_wide_right(left, right, left_dim, right_dim):
    high, low = halves(right)
    return dot(left, high, left_dim, right_dim) + dot(left, low, left_dim, right_dim)


def dot_wide_left(left, right, left_dim, right_dim):
    high, low = halves(left)
    return dot(high, right, left_dim, right_dim) + dot(low, right, left_dim, right_dim)


def rows_of(shape):
    return lax.broadcasted_iota(jnp.int32, shape, 0).astype(F32)


def decay_weights(rate):
    shape = (BLOCK, BLOCK)
    spacing = rows_of(shape) - lax.broadcasted_iota(jnp.int32, shape, 1).astype(F32)
    return jnp.where(spacing >= 0, jnp.exp(-rate * jnp.maximum(spacing, 0.0)), 0.0)


def block_rows(block):
    return slice(block * BLOCK, (block + 1) * BLOCK)


def memory_kernel(rates, keys, values, end, first):
    rate = rates[pl.program_id(0)]
    trailing = jnp.exp(-rate * (BLOCK - 1.0 - rows_of((BLOCK, 128))))
    full = jnp.exp(jnp.full((128, 128), -BLOCK * rate, F32))
    memory = None
    for block in range(2):
        rows = block_rows(block)
        update = dot_wide_left(keys[rows, :].astype(F32) * trailing, values[rows, :], 0, 0)
        memory = update if memory is None else full * memory + update
        if block == 0:
            first[0] = memory
    end[0] = memory


def inside_kernel(rates, queries, keys, values, probs, inside):
    weights = decay_weights(rates[pl.program_id(0)])
    for block in range(2):
        rows = block_rows(block)
        scores = dot(queries[rows, :], keys[rows, :], 1, 1)
        low = (scores * weights).astype(BF16)
        probs[0, block] = low
        inside[rows, :] = dot(low, values[rows, :], 1, 0)


def carried_kernel(
    rates, queries, entering, first, inside, gain, out_grad, attention, sums, squares, projection
):
    head = pl.program_id(0)
    rate = rates[head]
    leading = jnp.exp(-rate * (rows_of((BLOCK, 128)) + 1.0))
    full = jnp.exp(jnp.full((128, 128), -BLOCK * rate, F32))
    memory = entering[0]
    for block in range(2):
        rows = block_rows(block)
        carried = dot_wide_right(queries[rows, :], memory, 1, 0) * leading
        out = inside[rows, :] + carried
        attention[rows, :] = out
        grad = out_grad[rows, :].astype(F32) * gain[...]
        square, product = out * out, grad * out

        @pl.when(head == 0)
        def _():
            squares[rows, :] = square
            projection[rows, :] = product

        @pl.when(head > 0)
        def _():
            squares[rows, :] += square
            projection[rows, :] += product

        memory = full * memory + first[0]

    @pl.when(head == pl.num_programs(0) - 1)
    def _():
        flat = []
        for part in (squares, projection):
            for tile in range(4):
                turned = part[tile * 128 : (tile + 1) * 128, :].T
                flat.append(jnp.sum(turned, axis=0, keepdims=True))
        sums[...] = jnp.concatenate(flat, axis=0)


def grad_kernel(
    features, rates, sums, queries, attention, gain, out_grad, grad_out, normed_out, end, second, scale, coeff
):
    head = pl.program_id(0)
    rate = rates[head]
    @pl.when(head == 0)
    def _():
        scale_row = lax.rsqrt(sums[0:4] / features + EPSILON)
        coeff_row = scale_row * sums[4:8] / features
        for tile in range(4):
            rows = slice(tile * 128, (tile + 1) * 128)
            scale[rows, :] = jnp.broadcast_to(scale_row[tile : tile + 1], (128, 128)).T
            coeff[rows, :] = jnp.broadcast_to(coeff_row[tile : tile + 1], (128, 128)).T

    start = jnp.exp(-rate * rows_of((BLOCK, 128)))
    full = jnp.exp(jnp.full((128, 128), -BLOCK * rate, F32))
    backlog = None
    for block in (1, 0):
        rows = block_rows(block)
        by = scale[rows, :]
        normed = attention[rows, :] * by
        normed_out[rows, :] = (normed * gain[...]).astype(BF16)
        grad = out_grad[rows, :].astype(F32) * gain[...]
        low = (by * (grad - normed * coeff[rows, :])).astype(BF16)
        grad_out[rows, :] = low
        gathered = dot_wide_left(queries[rows, :].astype(F32) * start, low, 0, 0)
        backlog = gathered if backlog is None else full * backlog + gathered
        if block == 1:
            second[0] = backlog
    end[0] = backlog


def local_kernel(
    rates, queries, keys, values, grads, probs, entering, first, query_grad, key_part, value_part
):
    rate = rates[pl.program_id(0)]
    weights = decay_weights(rate)
    leading = jnp.exp(-rate * (rows_of((BLOCK, 128)) + 1.0))
    full = jnp.exp(jnp.full((128, 128), -BLOCK * rate, F32))
    memory = entering[0]
    for block in range(2):
        rows = block_rows(block)
        grad = grads[rows, :]
        low = (dot(grad, values[rows, :], 1, 1) * weights).astype(BF16)
        carried = dot_wide_right(grad, memory, 1, 1) * leading
        query_grad[rows, :] = (dot(low, keys[rows, :], 1, 0) + carried).astype(BF16)
        key_part[rows, :] = dot(low, queries[rows, :], 0, 0)
        value_part[rows, :] = dot(probs[0, block], grad, 0, 0)
        memory = full * memory + first[0]


def finish_kernel(rates, keys, values, key_part, value_part, after, second, key_grad, value_grad):
    rate = rates[pl.program_id(0)]
    ending = jnp.exp(-rate * (BLOCK - rows_of((BLOCK, 128))))
    full = jnp.exp(jnp.full((128, 128), -BLOCK * rate, F32))
    backlog = after[0]
    for block in (1, 0):
        rows = block_rows(block)
        key_more = dot_wide_right(values[rows, :], backlog, 1, 1) * ending
        value_more = dot_wide_right(keys[rows, :], backlog, 1, 0) * ending
        key_grad[rows, :] = (key_part[rows, :] + key_more).astype(BF16)
        value_grad[rows, :] = (value_part[rows, :] + value_more).astype(BF16)
        backlog = full * backlog + second[0]


def shape(*dims, dtype=F32):
    return jax.ShapeDtypeStruct(dims, dtype)


COLS = pl.BlockSpec((512, 128), lambda h: (0, h))
GAIN = pl.BlockSpec((1, 128), lambda h: (0, h))
STATE = pl.BlockSpec((1, 128, 128), lambda h: (h, 0, 0))
PROBS = pl.BlockSpec((1, 2, BLOCK, BLOCK), lambda h: (h, 0, 0, 0))


def whole(*dims):
    return pl.BlockSpec(dims, lambda h: (0,) * len(dims))


def per_head(kernel, name, in_specs, outs, out_specs, scratch=(), flops=50_000_000):
    return pl.pallas_call(
        kernel,
        grid=(4,),
        in_specs=[SMEM] + in_specs,
        out_specs=out_specs,
        out_shape=outs,
        scratch_shapes=scratch,
        name=name,
        cost_estimate=pl.CostEstimate(flops=flops, bytes_accessed=4_000_000, transcendentals=300_000),
        compiler_params=pltpu.CompilerParams(dimension_semantics=("arbitrary",)),
    )


def scan_total(table, pieces, reverse):
    count, rows, lanes = pieces.shape

    def kernel(table_ref, piece_ref, total_ref):
        order = range(count - 1, -1, -1) if reverse else range(count)
        running = None
        for k in order:
            piece = piece_ref[k]
            running = piece if running is None else running * table_ref[0] + piece
        for peer in range(total_ref.shape[0]):
            total_ref[peer] = running

    return pl.pallas_call(
        kernel,
        in_specs=[SMEM, VMEM],
        out_specs=VMEM,
        out_shape=shape(lax.axis_size(LINE[0]), rows, lanes),
        name="scan_total",
    )(table, pieces)


def scan_prefix(table, pieces, totals, reverse):
    count, rows, lanes = pieces.shape
    first = 5 if reverse else 1

    def kernel(table_ref, piece_ref, total_ref, prefix_ref):
        order = list(range(count - 1, -1, -1) if reverse else range(count))
        running = total_ref[0] * table_ref[first]
        for peer in range(1, total_ref.shape[0]):
            running = running + total_ref[peer] * table_ref[first + peer]
        for k in order:
            prefix_ref[k] = running
            if k != order[-1]:
                running = running * table_ref[0] + piece_ref[k]

    return pl.pallas_call(
        kernel,
        in_specs=[SMEM, VMEM, VMEM],
        out_specs=VMEM,
        out_shape=shape(count, rows, lanes),
        name="scan_prefix",
    )(table, pieces, totals)


def line_table(decay_rates, token_count):
    far, near = lax.axis_index(LINE[0]), lax.axis_index(LINE[1])
    far_size, near_size = lax.axis_size(LINE[0]), lax.axis_size(LINE[1])
    rate = lax.dynamic_index_in_dim(
        decay_rates, near * decay_rates.shape[0] // near_size, 0, keepdims=False
    )
    slot = jnp.arange(1 + 2 * far_size)
    earlier = far - slot
    later = slot - 1 - far_size - far - 1
    steps = jnp.where(slot > far_size, later, earlier) * near_size
    steps = jnp.where(slot == 0, 1, steps)
    weights = jnp.exp(-rate * token_count * jnp.maximum(steps, 0).astype(F32))
    return jnp.where(steps >= 0, weights, 0.0)


def along_context(table, state, reverse):
    near_size, far_size = lax.axis_size(LINE[1]), lax.axis_size(LINE[0])
    lanes = state.shape[-1]
    pieces = lax.all_to_all(state.reshape(near_size, -1, lanes), LINE[1], 0, 0)
    totals = lax.all_to_all(scan_total(table, pieces, reverse), LINE[0], 0, 0)
    prefix = scan_prefix(table, pieces, totals, reverse)
    return lax.all_to_all(prefix, LINE[1], 0, 0).reshape(state.shape)


def on_device(queries, key_rows, value_rows, decay_rates, norm_gain, out_grad):
    tokens, width = queries.shape
    heads = decay_rates.shape[0]
    features = float(width * lax.axis_size("head"))
    gain = norm_gain[None, :]
    table = line_table(decay_rates, tokens)
    state = shape(heads, 128, 128)
    wide, narrow = shape(tokens, width), shape(tokens, width, dtype=BF16)
    memory_end, memory_first = per_head(
        memory_kernel, "memory", [COLS, COLS], (state, state), (STATE, STATE)
    )(decay_rates, key_rows, value_rows)
    probs, inside = per_head(
        inside_kernel,
        "inside",
        [COLS, COLS, COLS],
        (shape(heads, 2, BLOCK, BLOCK, dtype=BF16), wide),
        (PROBS, COLS),
    )(decay_rates, queries, key_rows, value_rows)
    entering = along_context(table, memory_end, False)
    attention, sums = per_head(
        carried_kernel,
        "carried",
        [COLS, STATE, STATE, COLS, GAIN, COLS],
        (wide, shape(8, 128)),
        (COLS, whole(8, 128)),
        [pltpu.VMEM((tokens, 128), F32), pltpu.VMEM((tokens, 128), F32)],
    )(decay_rates, queries, entering, memory_first, inside, gain, out_grad)
    sums = lax.psum(sums, "head")
    grads, normed_out, backlog_end, backlog_second = per_head(
        functools.partial(grad_kernel, features),
        "grad",
        [whole(8, 128), COLS, COLS, GAIN, COLS],
        (narrow, narrow, state, state),
        (COLS, COLS, STATE, STATE),
        [pltpu.VMEM((tokens, 128), F32), pltpu.VMEM((tokens, 128), F32)],
    )(decay_rates, sums, queries, attention, gain, out_grad)
    query_grad, key_part, value_part = per_head(
        local_kernel,
        "local",
        [COLS, COLS, COLS, COLS, PROBS, STATE, STATE],
        (narrow, wide, wide),
        (COLS, COLS, COLS),
    )(decay_rates, queries, key_rows, value_rows, grads, probs, entering, memory_first)
    after = along_context(table, backlog_end, True)
    key_grad, value_grad = per_head(
        finish_kernel,
        "finish",
        [COLS, COLS, COLS, COLS, STATE, STATE],
        (narrow, narrow),
        (COLS, COLS),
    )(decay_rates, key_rows, value_rows, key_part, value_part, after, backlog_second)
    return (normed_out, query_grad, key_grad, value_grad)


def solution(mesh):
    split = Mesh(mesh.devices.reshape(4, 16, mesh.shape["head"]), LINE + ("head",))
    rows = P(LINE, "head")
    return jax.shard_map(
        on_device,
        mesh=split,
        in_specs=(rows, rows, rows, P("head"), P("head"), rows),
        out_specs=(rows, rows, rows, rows),
        check_vma=False,
    )
```

time: 382 us -> 163 us (0.43)
  the two profiles are of different devices: /device:TPU:8 before, /device:TPU:24 now
where the time goes in v1:
time: 163 us; the launch traced here: 162 us
  blocking collectives  55.1 us (34%)
  waiting for transfers between devices  40.2 us (25%)
  Pallas kernels  34.8 us (21%)
  starting transfers between devices  26.8 us (16%)
  local copies, waits for them, and re-layouts  3.34 us (2%)
    all_to_all x1, blocking collectives, along_context(): pieces = lax.all_to_all(state.reshape(near_size, -1, lanes), LINE[1], 0, 0)  24.8 us
    all_to_all x2, waiting for transfers between devices, along_context(): return lax.all_to_all(prefix, LINE[1], 0, 0).reshape(state.shape)  24.2 us
    all_to_all x2, blocking collectives, along_context(): totals = lax.all_to_all(scan_total(table, pieces, reverse), LINE[0], 0, 0)  19.6 us
    all_to_all x1, waiting for transfers between devices, along_context(): pieces = lax.all_to_all(state.reshape(near_size, -1, lanes), LINE[1], 0, 0)  15.9 us
    all_to_all x1, starting transfers between devices, along_context(): pieces = lax.all_to_all(state.reshape(near_size, -1, lanes), LINE[1], 0, 0)  15.2 us
    all_to_all x2, starting transfers between devices, along_context(): return lax.all_to_all(prefix, LINE[1], 0, 0).reshape(state.shape)  11.6 us
    psum x1, blocking collectives, on_device(): sums = lax.psum(sums, 'head')  10.7 us
    pallas_call x1, Pallas kernels, on_device(): per_head(local_kernel, 'local', [COLS, COLS, COLS, COLS, PROBS, STATE, ST...  6.02 us
  transfers between devices with their start and end apart: 3, of which 3 were waited for; matrix products, arithmetic and copies ran while one was open for 1% of the time, Pallas kernels for 7%

profile of v1, /device:TPU:24, one launch (start us, length us, event | category | flops | bytes accessed | tf_op | source)
XLA Modules:
  0.0 162.2 jit_solution(18330496758906236425)
XLA Ops:
  0.6 3.9 %memory.1 = (f32[4,128,128]{2,1,0:T(8,128)}, f32[4,128,128]{2,1,0:T(8,128)}) custom-call(f32[4]{0:T(128)} %rates.11, bf16[512,512]{1,0:T(8,128)(2,1)} %keys.7, bf16[512,512]{1,0:T(8,128)(2,1)} %values.7), custom_call_target="tpu_custom_call" | custom-call | flops 50000000 | bytes 4000000 | tf_op jit(solution)/shard_map/memory/pallas_call | solution.py:286
  4.5 15.2 %all-to-all-start = ((f32[16,32,128]{2,1,0:T(8,128)}), f32[16,32,128]{2,1,0:T(8,128)S(1)}, u32[]{:S(2)}, u32[]{:S(2)}) async-start(f32[16,32,128]{2,1,0:T(8,128)} %bitcast.9), calls=%async_computation | async-start | bytes 524288 | tf_op jit(solution)/shard_map/all_to_all | solution.py:272
  19.7 0.0 copy-start.3
  19.7 0.6 copy-done.3
  20.4 0.6 dynamic_slice.4
  21.6 0.6 compare_select_fusion.table_ref
  22.2 15.9 %all-to-all-done.piece_ref = f32[16,32,128]{2,1,0:T(8,128)S(1)} async-done(((f32[16,32,128]{2,1,0:T(8,128)}), f32[16,32,128]{2,1,0:T(8,128)S(1)}, u32[]{:S(2)}, u32[]{:S(2)}) %all-to-all-start) | async-done | bytes 262176 | tf_op jit(solution)/shard_map/all_to_all | solution.py:272
  38.1 0.0 copy-start
  38.1 0.7 copy-done
  38.8 1.6 %scan_total.2 = f32[4,32,128]{2,1,0:T(8,128)} custom-call(f32[9]{0:T(128)} %compare_select_fusion.table_ref, f32[16,32,128]{2,1,0:T(8,128)} %copy-done), custom_call_target="tpu_custom_call" | custom-call | tf_op jit(solution)/shard_map/scan_total/pallas_call | solution.py:222
  40.4 10.0 %all_to_all.30.total_ref = f32[4,32,128]{2,1,0:T(8,128)} all-to-all(f32[4,32,128]{2,1,0:T(8,128)} %scan_total.2), channel_id=1, replica_groups=mesh['ctx_0'=4,'ctx_1'=16,'head'=8] {'ctx_0'}, dimensions={0} | all-to-all | bytes 131072 | tf_op jit(solution)/shard_map/all_to_all | solution.py:273
  50.4 1.7 %scan_prefix.2 = f32[16,32,128]{2,1,0:T(8,128)} custom-call(f32[9]{0:T(128)} %compare_select_fusion.table_ref, f32[16,32,128]{2,1,0:T(8,128)} %copy-done, f32[4,32,128]{2,1,0:T(8,128)} %all_to_all.30.total_ref), custom_call_target="tpu_custom_call" | custom-call | tf_op jit(solution)/shard_map/scan_prefix/pallas_call | solution.py:245
  52.1 5.8 %all-to-all-start.2 = ((f32[16,32,128]{2,1,0:T(8,128)}), f32[16,32,128]{2,1,0:T(8,128)S(1)}, u32[]{:S(2)}, u32[]{:S(2)}) async-start(f32[16,32,128]{2,1,0:T(8,128)} %scan_prefix.2), calls=%async_computation.2 | async-start | bytes 524288 | tf_op jit(solution)/shard_map/all_to_all | solution.py:275
  57.9 4.7 %inside.1 = (bf16[4,2,256,256]{3,2,1,0:T(8,128)(2,1)}, f32[512,512]{1,0:T(8,128)}) custom-call(f32[4]{0:T(128)} %rates.11, bf16[512,512]{1,0:T(8,128)(2,1)} %queries.7, bf16[512,512]{1,0:T(8,128)(2,1)} %keys.7, bf16[512,512]{1,0:T(8,128)(2,1)} %values.7), custom_call_target="tpu_custom_call" | custom-call | flops 50000000 | bytes 4000000 | tf_op jit(solution)/shard_map/inside/pallas_call | solution.py:289
  62.6 12.5 %all-to-all-done.2 = f32[16,32,128]{2,1,0:T(8,128)S(1)} async-done(((f32[16,32,128]{2,1,0:T(8,128)}), f32[16,32,128]{2,1,0:T(8,128)S(1)}, u32[]{:S(2)}, u32[]{:S(2)}) %all-to-all-start.2) | async-done | bytes 262176 | tf_op jit(solution)/shard_map/all_to_all | solution.py:275
  75.1 0.0 copy-start.1
  75.1 0.7 copy-done.1
  75.8 4.9 %carried.1 = (f32[512,512]{1,0:T(8,128)}, f32[8,128]{1,0:T(8,128)}) custom-call(f32[4]{0:T(128)} %rates.11, bf16[512,512]{1,0:T(8,128)(2,1)} %queries.7, f32[4,128,128]{2,1,0:T(8,128)} %bitcast.6, f32[4,128,128]{2,1,0:T(8,128)} %get-tuple-element.20.first, f32[512,512]{1,0:T(8,128)} %get-tuple-element.21.inside, f32[1,512]{1,0:T(1,128)} %bitcast.11, ...), custom_call_target="tpu_custom_call" | custom-call | flops 50000000 | bytes 4000000 | tf_op jit(solution)/shard_map/carried/pallas_call | solution.py:297
  80.7 10.7 %psum.7.sums = f32[8,128]{1,0:T(8,128)} all-reduce(f32[8,128]{1,0:T(8,128)} %get-tuple-element.22), channel_id=1, replica_groups=mesh['ctx_0'=4,'ctx_1'=16,'head'=8] {'head'}, use_global_device_ids=true, to_apply=%region_0.1 | all-reduce | flops 1024 | bytes 8192 | tf_op jit(solution)/shard_map/psum | solution.py:305
  91.4 4.3 %grad.1 = (bf16[512,512]{1,0:T(8,128)(2,1)}, bf16[512,512]{1,0:T(8,128)(2,1)}, f32[4,128,128]{2,1,0:T(8,128)}, f32[4,128,128]{2,1,0:T(8,128)}) custom-call(f32[4]{0:T(128)} %rates.11, f32[8,128]{1,0:T(8,128)} %psum.7.sums, bf16[512,512]{1,0:T(8,128)(2,1)} %queries.7, f32[512,512]{1,0:T(8,128)} %get-tuple-element.23.attention, f32[1,512]{1,0:T(1,128)} %bitcast.12, ...), custom_call_target="tpu_custom_call" | custom-call | flops 50000000 | bytes 4000000 | tf_op jit(solution)/shard_map/grad/pallas_call | solution.py:306
  95.7 24.8 %all_to_all.31.piece_ref = f32[16,32,128]{2,1,0:T(8,128)} all-to-all(f32[16,32,128]{2,1,0:T(8,128)} %bitcast.10), channel_id=1, replica_groups=mesh['ctx_0'=4,'ctx_1'=16,'head'=8] {'ctx_1'}, dimensions={0} | all-to-all | bytes 524288 | tf_op jit(solution)/shard_map/all_to_all | solution.py:272
  120.5 1.6 %scan_total.3 = f32[4,32,128]{2,1,0:T(8,128)} custom-call(f32[9]{0:T(128)} %compare_select_fusion.table_ref, f32[16,32,128]{2,1,0:T(8,128)} %all_to_all.31.piece_ref), custom_call_target="tpu_custom_call" | custom-call | tf_op jit(solution)/shard_map/scan_total/pallas_call | solution.py:222
  122.2 9.6 %all_to_all.32.total_ref = f32[4,32,128]{2,1,0:T(8,128)} all-to-all(f32[4,32,128]{2,1,0:T(8,128)} %scan_total.3), channel_id=1, replica_groups=mesh['ctx_0'=4,'ctx_1'=16,'head'=8] {'ctx_0'}, dimensions={0} | all-to-all | bytes 131072 | tf_op jit(solution)/shard_map/all_to_all | solution.py:273
  131.8 1.7 %scan_prefix.3 = f32[16,32,128]{2,1,0:T(8,128)} custom-call(f32[9]{0:T(128)} %compare_select_fusion.table_ref, f32[16,32,128]{2,1,0:T(8,128)} %all_to_all.31.piece_ref, f32[4,32,128]{2,1,0:T(8,128)} %all_to_all.32.total_ref), custom_call_target="tpu_custom_call" | custom-call | tf_op jit(solution)/shard_map/scan_prefix/pallas_call | solution.py:245
  133.5 5.9 %all-to-all-start.5 = ((f32[16,32,128]{2,1,0:T(8,128)}), f32[16,32,128]{2,1,0:T(8,128)S(1)}, u32[]{:S(2)}, u32[]{:S(2)}) async-start(f32[16,32,128]{2,1,0:T(8,128)} %scan_prefix.3), calls=%async_computation.5 | async-start | bytes 524288 | tf_op jit(solution)/shard_map/all_to_all | solution.py:275
  139.4 6.0 %local.1 = (bf16[512,512]{1,0:T(8,128)(2,1)}, f32[512,512]{1,0:T(8,128)}, f32[512,512]{1,0:T(8,128)}) custom-call(f32[4]{0:T(128)} %rates.11, bf16[512,512]{1,0:T(8,128)(2,1)} %queries.7, bf16[512,512]{1,0:T(8,128)(2,1)} %keys.7, bf16[512,512]{1,0:T(8,128)(2,1)} %values.7, bf16[512,512]{1,0:T(8,128)(2,1)} %get-tuple-element.25.grads, ...), custom_call_target="tpu_custom_call" | custom-call | flops 50000000 | bytes 4000000 | tf_op jit(solution)/shard_map/local/pallas_call | solution.py:314
  145.4 11.7 %all-to-all-done.5 = f32[16,32,128]{2,1,0:T(8,128)S(1)} async-done(((f32[16,32,128]{2,1,0:T(8,128)}), f32[16,32,128]{2,1,0:T(8,128)S(1)}, u32[]{:S(2)}, u32[]{:S(2)}) %all-to-all-start.5) | async-done | bytes 262176 | tf_op jit(solution)/shard_map/all_to_all | solution.py:275
  157.1 0.0 copy-start.2
  157.1 0.7 copy-done.2
  157.8 4.4 %finish.1 = (bf16[512,512]{1,0:T(8,128)(2,1)}, bf16[512,512]{1,0:T(8,128)(2,1)}) custom-call(f32[4]{0:T(128)} %rates.11, bf16[512,512]{1,0:T(8,128)(2,1)} %keys.7, bf16[512,512]{1,0:T(8,128)(2,1)} %values.7, f32[512,512]{1,0:T(8,128)} %get-tuple-element.28.key_part, f32[512,512]{1,0:T(8,128)} %get-tuple-element.29.value_part, f32[4,128,128]{2,1,0:T(8,128)} %bitcast.8, ...), custom_call_target="tpu_custom_call" | custom-call | flops 50000000 | bytes 4000000 | tf_op jit(solution)/shard_map/finish/pallas_call | solution.py:322
Async XLA Ops:
  4.5 33.6 %all-to-all-start = ((f32[16,32,128]{2,1,0:T(8,128)}), f32[16,32,128]{2,1,0:T(8,128)S(1)}, u32[]{:S(2)}, u32[]{:S(2)}) async-start(f32[16,32,128]{2,1,0:T(8,128)} %bitcast.9), calls=%async_computation | async-start | bytes 524288 | tf_op jit(solution)/shard_map/all_to_all | solution.py:272
  19.7 0.7 copy-start.3
  38.1 0.7 copy-start
  52.1 23.0 %all-to-all-start.2 = ((f32[16,32,128]{2,1,0:T(8,128)}), f32[16,32,128]{2,1,0:T(8,128)S(1)}, u32[]{:S(2)}, u32[]{:S(2)}) async-start(f32[16,32,128]{2,1,0:T(8,128)} %scan_prefix.2), calls=%async_computation.2 | async-start | bytes 524288 | tf_op jit(solution)/shard_map/all_to_all | solution.py:275
  75.1 0.7 copy-start.1
  133.5 23.6 %all-to-all-start.5 = ((f32[16,32,128]{2,1,0:T(8,128)}), f32[16,32,128]{2,1,0:T(8,128)S(1)}, u32[]{:S(2)}, u32[]{:S(2)}) async-start(f32[16,32,128]{2,1,0:T(8,128)} %scan_prefix.3), calls=%async_computation.5 | async-start | bytes 524288 | tf_op jit(solution)/shard_map/all_to_all | solution.py:275
  157.1 0.7 copy-start.2

commit v2 on v1

v2 whole, which is shorter than its diff:
```python
import dataclasses
import functools

import jax
import jax.numpy as jnp
from jax import lax
from jax.experimental import pallas as pl
from jax.experimental.pallas import tpu as pltpu
from jax.sharding import Mesh
from jax.sharding import PartitionSpec as P

BLOCK = 256
LINE = ("ctx_0", "ctx_1")
SIDE = ("row", "core")
EPSILON = 1e-06
GRANT = 12 << 20
F32 = jnp.float32
BF16 = jnp.bfloat16
SMEM = pl.BlockSpec(memory_space=pltpu.SMEM)
VMEM = pl.BlockSpec(memory_space=pltpu.VMEM)


def dot(left, right, left_dim, right_dim):
    return lax.dot_general(
        left, right, (((left_dim,), (right_dim,)), ((), ())), preferred_element_type=F32
    )


def halves(wide):
    high = wide.astype(BF16)
    return high, (wide - high.astype(F32)).astype(BF16)


def dot_wide_right(left, right, left_dim, right_dim):
    high, low = halves(right)
    return dot(left, high, left_dim, right_dim) + dot(left, low, left_dim, right_dim)


def dot_wide_left(left, right, left_dim, right_dim):
    high, low = halves(left)
    return dot(high, right, left_dim, right_dim) + dot(low, right, left_dim, right_dim)


def rows_of(shape):
    return lax.broadcasted_iota(jnp.int32, shape, 0).astype(F32)


def decay_weights(rate):
    shape = (BLOCK, BLOCK)
    spacing = rows_of(shape) - lax.broadcasted_iota(jnp.int32, shape, 1).astype(F32)
    return jnp.where(spacing >= 0, jnp.exp(-rate * jnp.maximum(spacing, 0.0)), 0.0)


def block_rows(block):
    return slice(block * BLOCK, (block + 1) * BLOCK)


@dataclasses.dataclass
class Streamed:
    array: object


def cols_of(head):
    return slice(head * 128, (head + 1) * 128)


def memory_kernel(rates, keys, values, end, first):
    rows_in = rows_of((BLOCK, 128))
    for head in range(4):
        cols = cols_of(head)
        trailing = jnp.exp(-rates[head] * (BLOCK - 1.0 - rows_in))
        full = jnp.exp(jnp.full((128, 128), -BLOCK * rates[head], F32))
        updates = []
        for block in range(2):
            rows = block_rows(block)
            wide = keys[rows, cols].astype(F32) * trailing
            updates.append(dot_wide_left(wide, values[rows, cols], 0, 0))
        first[head] = updates[0]
        end[head] = full * updates[0] + updates[1]


def inside_kernel(rates, queries, keys, values, probs, inside):
    for head in range(4):
        cols = cols_of(head)
        weights = decay_weights(rates[head])
        for block in range(2):
            rows = block_rows(block)
            scores = dot(queries[rows, cols], keys[rows, cols], 1, 1)
            low = (scores * weights).astype(BF16)
            probs[head, block] = low
            inside[rows, cols] = dot(low, values[rows, cols], 1, 0)


def carried_kernel(rates, queries, entering, first, inside, gain, out_grad, attention, sums):
    after_start = rows_of((BLOCK, 128)) + 1.0
    squares, products = [], []
    for block in range(2):
        rows = block_rows(block)
        square = product = None
        for head in range(4):
            cols = cols_of(head)
            memory = entering[head]
            if block == 1:
                full = jnp.exp(jnp.full((128, 128), -BLOCK * rates[head], F32))
                memory = full * memory + first[head]
            leading = jnp.exp(-rates[head] * after_start)
            carried = dot_wide_right(queries[rows, cols], memory, 1, 0) * leading
            out = inside[rows, cols] + carried
            attention[rows, cols] = out
            grad = out_grad[rows, cols].astype(F32) * gain[:, cols]
            square = out * out if square is None else square + out * out
            product = grad * out if product is None else product + grad * out
        for part, flat in ((square, squares), (product, products)):
            for tile in range(2):
                turned = part[tile * 128 : (tile + 1) * 128, :].T
                flat.append(jnp.sum(turned, axis=0, keepdims=True))
    sums[...] = jnp.concatenate(squares + products, axis=0)


def per_token(row):
    return jnp.broadcast_to(row, (128, 128)).T


def scales_of(features, sums, block):
    scale = lax.rsqrt(sums[0:4] / features + EPSILON)
    coeff = scale * sums[4:8] / features
    tiles = (2 * block, 2 * block + 1)
    return tuple(
        jnp.concatenate([per_token(part[tile : tile + 1]) for tile in tiles], axis=0)
        for part in (scale, coeff)
    )


def attention_grad(attention, out_grad, gain, scale, coeff):
    normed = attention * scale
    grad = out_grad.astype(F32) * gain
    return normed, (scale * (grad - normed * coeff)).astype(BF16)


def grad_kernel(features, rates, sums, queries, attention, gain, out_grad, end, second):
    from_start = rows_of((BLOCK, 128))
    for block in (1, 0):
        rows = block_rows(block)
        scale, coeff = scales_of(features, sums, block)
        for head in range(4):
            cols = cols_of(head)
            _, low = attention_grad(
                attention[rows, cols], out_grad[rows, cols], gain[:, cols], scale, coeff
            )
            start = jnp.exp(-rates[head] * from_start)
            gathered = dot_wide_left(queries[rows, cols].astype(F32) * start, low, 0, 0)
            if block == 1:
                second[head] = gathered
            else:
                full = jnp.exp(jnp.full((128, 128), -BLOCK * rates[head], F32))
                end[head] = full * second[head] + gathered


def local_kernel(
    features,
    rates,
    queries,
    keys,
    values,
    out_grad,
    probs,
    entering,
    first,
    sums,
    attention,
    gain,
    query_grad,
    normed_out,
    key_part,
    value_part,
):
    after_start = rows_of((BLOCK, 128)) + 1.0
    for block in range(2):
        rows = block_rows(block)
        scale, coeff = scales_of(features, sums, block)
        for head in range(4):
            cols = cols_of(head)
            weights = decay_weights(rates[head])
            memory = entering[head]
            if block == 1:
                full = jnp.exp(jnp.full((128, 128), -BLOCK * rates[head], F32))
                memory = full * memory + first[head]
            leading = jnp.exp(-rates[head] * after_start)
            normed, grad = attention_grad(
                attention[rows, cols], out_grad[rows, cols], gain[:, cols], scale, coeff
            )
            normed_out[rows, cols] = (normed * gain[:, cols]).astype(BF16)
            low = (dot(grad, values[rows, cols], 1, 1) * weights).astype(BF16)
            carried = dot_wide_right(grad, memory, 1, 1) * leading
            query_grad[rows, cols] = (dot(low, keys[rows, cols], 1, 0) + carried).astype(BF16)
            key_part[rows, cols] = dot(low, queries[rows, cols], 0, 0)
            value_part[rows, cols] = dot(probs[head, block], grad, 0, 0)


def finish_kernel(
    rates, keys, values, key_part, value_part, after, second, key_grad, value_grad
):
    tile = pl.program_id(0)
    to_end = BLOCK - rows_of((128, 128)) - 128.0 * (tile % 2).astype(F32)
    for head in range(4):
        cols = cols_of(head)
        ending = jnp.exp(-rates[head] * to_end)
        full = jnp.exp(jnp.full((128, 128), -BLOCK * rates[head], F32))
        backlog = jnp.where(tile < 2, full * after[head] + second[head], after[head])
        key_more = dot_wide_right(values[:, cols], backlog, 1, 1) * ending
        value_more = dot_wide_right(keys[:, cols], backlog, 1, 0) * ending
        key_grad[:, cols] = (key_part[:, cols] + key_more).astype(BF16)
        value_grad[:, cols] = (value_part[:, cols] + value_more).astype(BF16)


def shape(*dims, dtype=F32):
    return jax.ShapeDtypeStruct(dims, dtype)


def near(array):
    return pltpu.with_memory_space_constraint(array, pltpu.VMEM)


def call(kernel, name, outs, *operands, grant=GRANT):
    rates, *rest = operands
    streamed = [isinstance(array, Streamed) for array in rest]
    arrays = [array.array if isinstance(array, Streamed) else array for array in rest]
    far = pl.BlockSpec()
    return pl.pallas_call(
        kernel,
        in_specs=[SMEM] + [far if flag else VMEM for flag in streamed],
        out_specs=tuple(far if isinstance(out, Streamed) else VMEM for out in outs),
        out_shape=tuple(out.array if isinstance(out, Streamed) else out for out in outs),
        name=name,
        cost_estimate=pl.CostEstimate(
            flops=400_000_000, bytes_accessed=4_000_000, transcendentals=300_000
        ),
        compiler_params=pltpu.CompilerParams(vmem_limit_bytes=grant),
    )(rates, *arrays)


def scan_total(table, pieces, reverse):
    count, rows, lanes = pieces.shape

    def kernel(table_ref, piece_ref, total_ref):
        order = range(count - 1, -1, -1) if reverse else range(count)
        running = None
        for k in order:
            piece = piece_ref[k]
            running = piece if running is None else running * table_ref[0] + piece
        for peer in range(total_ref.shape[0]):
            total_ref[peer] = running

    return pl.pallas_call(
        kernel,
        in_specs=[SMEM, VMEM],
        out_specs=VMEM,
        out_shape=pltpu.VMEM((lax.axis_size(LINE[0]), rows, lanes), F32),
        name="scan_total",
        compiler_params=pltpu.CompilerParams(vmem_limit_bytes=GRANT),
    )(table, near(pieces))


def scan_prefix(table, pieces, totals, reverse):
    count, rows, lanes = pieces.shape
    first = 5 if reverse else 1

    def kernel(table_ref, piece_ref, total_ref, prefix_ref):
        order = list(range(count - 1, -1, -1) if reverse else range(count))
        running = total_ref[0] * table_ref[first]
        for peer in range(1, total_ref.shape[0]):
            running = running + total_ref[peer] * table_ref[first + peer]
        for k in order:
            prefix_ref[k] = running
            if k != order[-1]:
                running = running * table_ref[0] + piece_ref[k]

    return pl.pallas_call(
        kernel,
        in_specs=[SMEM, VMEM, VMEM],
        out_specs=VMEM,
        out_shape=pltpu.VMEM((count, rows, lanes), F32),
        name="scan_prefix",
        compiler_params=pltpu.CompilerParams(vmem_limit_bytes=GRANT),
    )(table, near(pieces), near(totals))


def line_table(decay_rates, token_count):
    far, near = lax.axis_index(LINE[0]), lax.axis_index(LINE[1])
    far_size, near_size = lax.axis_size(LINE[0]), lax.axis_size(LINE[1])
    rate = lax.dynamic_index_in_dim(
        decay_rates, near * decay_rates.shape[0] // near_size, 0, keepdims=False
    )
    slot = jnp.arange(1 + 2 * far_size)
    earlier = far - slot
    later = slot - 1 - far_size - far - 1
    steps = jnp.where(slot > far_size, later, earlier) * near_size
    steps = jnp.where(slot == 0, 1, steps)
    weights = jnp.exp(-rate * token_count * jnp.maximum(steps, 0).astype(F32))
    return jnp.where(steps >= 0, weights, 0.0)


def along_context(table, state, reverse):
    near_size, far_size = lax.axis_size(LINE[1]), lax.axis_size(LINE[0])
    lanes = state.shape[-1]
    pieces = lax.all_to_all(state.reshape(near_size, -1, lanes), LINE[1], 0, 0)
    totals = lax.all_to_all(scan_total(table, pieces, reverse), LINE[0], 0, 0)
    prefix = scan_prefix(table, pieces, totals, reverse)
    return lax.all_to_all(prefix, LINE[1], 0, 0).reshape(state.shape)


def on_device(queries, key_rows, value_rows, decay_rates, norm_gain, out_grad):
    tokens, width = queries.shape
    heads = decay_rates.shape[0]
    features = float(width * lax.axis_size(SIDE))
    gain = norm_gain[None, :]
    table = line_table(decay_rates, tokens)
    state = shape(heads, 128, 128)
    wide, narrow = shape(tokens, width), shape(tokens, width, dtype=BF16)
    tables = shape(heads, 2, BLOCK, BLOCK, dtype=BF16)
    state_near, wide_near = pltpu.VMEM(state.shape, F32), pltpu.VMEM(wide.shape, F32)
    far_q, far_k, far_v, far_grad = map(Streamed, (queries, key_rows, value_rows, out_grad))
    memory_end, memory_first = call(
        memory_kernel,
        "memory",
        (state_near, state_near),
        decay_rates,
        near(key_rows),
        near(value_rows),
    )
    probs, inside = call(
        inside_kernel,
        "inside",
        (Streamed(tables), wide_near),
        decay_rates,
        far_q,
        far_k,
        far_v,
        grant=None,
    )
    entering = along_context(table, memory_end, False)
    attention, sums = call(
        carried_kernel,
        "carried",
        (wide_near, pltpu.VMEM((8, 128), F32)),
        decay_rates,
        near(queries),
        near(entering),
        near(memory_first),
        near(inside),
        near(gain),
        near(out_grad),
    )
    sums = lax.psum(lax.psum(sums, "core"), "row")
    backlog_end, backlog_second = call(
        functools.partial(grad_kernel, features),
        "grad",
        (state_near, state_near),
        decay_rates,
        near(sums),
        near(queries),
        near(attention),
        near(gain),
        near(out_grad),
    )
    query_grad, normed_out, key_part, value_part = call(
        functools.partial(local_kernel, features),
        "local",
        (Streamed(narrow), Streamed(narrow), Streamed(wide), Streamed(wide)),
        decay_rates,
        far_q,
        far_k,
        far_v,
        far_grad,
        Streamed(probs),
        near(entering),
        near(memory_first),
        near(sums),
        near(attention),
        near(gain),
        grant=None,
    )
    after = along_context(table, backlog_end, True)
    tile_rows = pl.BlockSpec((128, width), lambda tile: (tile, 0))
    key_grad, value_grad = pl.pallas_call(
        finish_kernel,
        grid=(tokens // 128,),
        in_specs=[SMEM] + [tile_rows] * 4 + [VMEM] * 2,
        out_specs=(tile_rows, tile_rows),
        out_shape=(narrow, narrow),
        name="finish",
    )(
        decay_rates,
        key_rows,
        value_rows,
        key_part,
        value_part,
        near(after),
        near(backlog_second),
    )
    return (normed_out, query_grad, key_grad, value_grad)


def solution(mesh):
    split = Mesh(mesh.devices.reshape(4, 16, 4, 2), LINE + SIDE)
    rows = P(LINE, SIDE)
    return jax.shard_map(
        on_device,
        mesh=split,
        in_specs=(rows, rows, rows, P(SIDE), P(SIDE), rows),
        out_specs=(rows, rows, rows, rows),
        check_vma=False,
    )
```

time: 163 us -> 152 us (0.933)
  the two profiles are of different devices: /device:TPU:24 before, /device:TPU:32 now
where the time goes in v2:
time: 152 us; the launch traced here: 151 us
  blocking collectives  53.2 us (35%)
  waiting for transfers between devices  40.6 us (27%)
  starting transfers between devices  26.5 us (17%)
  Pallas kernels  22.1 us (15%)
  local copies, waits for them, and re-layouts  6.88 us (5%)
    all_to_all x2, waiting for transfers between devices, along_context(): return lax.all_to_all(prefix, LINE[1], 0, 0).reshape(state.shape)  24.6 us
    all_to_all x1, blocking collectives, along_context(): pieces = lax.all_to_all(state.reshape(near_size, -1, lanes), LINE[1], 0, 0)  22.4 us
    all_to_all x2, blocking collectives, along_context(): totals = lax.all_to_all(scan_total(table, pieces, reverse), LINE[0], 0, 0)  17.7 us
    all_to_all x1, waiting for transfers between devices, along_context(): pieces = lax.all_to_all(state.reshape(near_size, -1, lanes), LINE[1], 0, 0)  16 us
    all_to_all x1, starting transfers between devices, along_context(): pieces = lax.all_to_all(state.reshape(near_size, -1, lanes), LINE[1], 0, 0)  15.2 us
    pallas_call x5, Pallas kernels, call(): pl.pallas_call(kernel, in_specs=[SMEM] + [far if flag else VMEM for flag...  13.8 us
    psum x2, blocking collectives, on_device(): sums = lax.psum(lax.psum(sums, 'core'), 'row')  13.2 us
    all_to_all x2, starting transfers between devices, along_context(): return lax.all_to_all(prefix, LINE[1], 0, 0).reshape(state.shape)  11.3 us
  transfers between devices with their start and end apart: 3, of which 3 were waited for; matrix products, arithmetic and copies ran while one was open for 0% of the time, Pallas kernels for 6%

profile of v2, /device:TPU:32, one launch (start us, length us, event | category | flops | bytes accessed | tf_op | source)
XLA Modules:
  0.0 150.7 jit_solution(8130673114364150616)
XLA Ops:
  0.6 0.0 copy-start.2
  0.6 1.0 copy-done.2
  1.7 0.0 copy-start.3
  1.7 1.0 copy-done.3
  2.7 0.0 copy-start.9
  2.7 0.7 copy-done.9
  3.4 1.8 %memory.1 = (f32[4,128,128]{2,1,0:T(8,128)}, f32[4,128,128]{2,1,0:T(8,128)S(1)}) custom-call(f32[4]{0:T(128)S(1)} %copy-done.9, bf16[512,512]{1,0:T(8,128)(2,1)S(1)} %copy-done.2, bf16[512,512]{1,0:T(8,128)(2,1)S(1)} %copy-done.3), custom_call_target="tpu_custom_call" | custom-call | flops 400000000 | bytes 4000000 | tf_op jit(solution)/shard_map/memory/pallas_call | solution.py:229
  5.2 15.2 %all-to-all-start = ((f32[16,32,128]{2,1,0:T(8,128)}), f32[16,32,128]{2,1,0:T(8,128)S(1)}, u32[]{:S(2)}, u32[]{:S(2)}) async-start(f32[16,32,128]{2,1,0:T(8,128)} %bitcast.1), calls=%async_computation | async-start | bytes 524288 | tf_op jit(solution)/shard_map/all_to_all | solution.py:306
  20.4 0.0 copy-start.10
  20.4 0.6 copy-done.10
  21.0 0.6 dynamic_slice.4
  22.3 16.0 %all-to-all-done.piece_ref = f32[16,32,128]{2,1,0:T(8,128)S(1)} async-done(((f32[16,32,128]{2,1,0:T(8,128)}), f32[16,32,128]{2,1,0:T(8,128)S(1)}, u32[]{:S(2)}, u32[]{:S(2)}) %all-to-all-start) | async-done | bytes 262176 | tf_op jit(solution)/shard_map/all_to_all | solution.py:306
  38.3 0.6 scan_total.2
  38.9 9.7 %all_to_all.30.total_ref = f32[4,32,128]{2,1,0:T(8,128)S(1)} all-to-all(f32[4,32,128]{2,1,0:T(8,128)S(1)} %scan_total.2), channel_id=1, replica_groups=mesh['ctx_0'=4,'ctx_1'=16,'row'=4,'core'=2] {'ctx_0'}, dimensions={0} | all-to-all | bytes 131072 | tf_op jit(solution)/shard_map/all_to_all | solution.py:307
  48.6 1.3 scan_prefix.2
  49.9 6.2 %all-to-all-start.2 = ((f32[16,32,128]{2,1,0:T(8,128)}), f32[16,32,128]{2,1,0:T(8,128)S(1)}, u32[]{:S(2)}, u32[]{:S(2)}) async-start(f32[16,32,128]{2,1,0:T(8,128)} %scan_prefix.2), calls=%async_computation.2 | async-start | bytes 524288 | tf_op jit(solution)/shard_map/all_to_all | solution.py:309
  56.1 0.0 copy-start
  56.1 0.0 copy-start.1
  56.1 3.3 %inside.1 = (bf16[4,2,256,256]{3,2,1,0:T(8,128)(2,1)}, f32[512,512]{1,0:T(8,128)S(1)}) custom-call(f32[4]{0:T(128)} %rates.11, bf16[512,512]{1,0:T(8,128)(2,1)} %queries.7, bf16[512,512]{1,0:T(8,128)(2,1)} %keys.7, bf16[512,512]{1,0:T(8,128)(2,1)} %values.7), custom_call_target="tpu_custom_call" | custom-call | flops 400000000 | bytes 4000000 | tf_op jit(solution)/shard_map/inside/pallas_call | solution.py:229
  59.4 0.0 copy-start.6
  59.4 1.0 copy-done.6
  60.4 13.4 %all-to-all-done.2 = f32[16,32,128]{2,1,0:T(8,128)S(1)} async-done(((f32[16,32,128]{2,1,0:T(8,128)}), f32[16,32,128]{2,1,0:T(8,128)S(1)}, u32[]{:S(2)}, u32[]{:S(2)}) %all-to-all-start.2) | async-done | bytes 262176 | tf_op jit(solution)/shard_map/all_to_all | solution.py:309
  73.8 0.0 copy-start.8
  73.8 0.0 copy-start.11
  73.8 0.0 copy-done
  73.8 0.0 copy-done.1
  73.8 0.7 copy-done.8
  74.5 0.0 copy-done.11
  74.5 0.0 copy-start.7
  74.5 1.2 copy-done.7
  75.7 1.3 carried.1
  77.0 0.0 copy-start.4
  77.0 2.5 %psum.14 = f32[8,128]{1,0:T(8,128)S(1)} all-reduce(f32[8,128]{1,0:T(8,128)S(1)} %get-tuple-element.22), channel_id=1, replica_groups=mesh['ctx_0'=4,'ctx_1'=16,'row'=4,'core'=2] {'core'}, use_global_device_ids=true, to_apply=%region_0.1 | all-reduce | flops 1024 | bytes 8192 | tf_op jit(solution)/shard_map/psum | solution.py:354
  79.4 10.7 %psum.15.sums = f32[8,128]{1,0:T(8,128)S(1)} all-reduce(f32[8,128]{1,0:T(8,128)S(1)} %psum.14), channel_id=1, replica_groups=mesh['ctx_0'=4,'ctx_1'=16,'row'=4,'core'=2] {'row'}, use_global_device_ids=true, to_apply=%region_1.2 | all-reduce | flops 1024 | bytes 8192 | tf_op jit(solution)/shard_map/psum | solution.py:354
  90.1 1.5 grad.1
  91.6 0.0 copy-done.4
  91.6 0.0 copy-start.5
  91.6 22.4 %all_to_all.31.piece_ref = f32[16,32,128]{2,1,0:T(8,128)S(1)} all-to-all(f32[16,32,128]{2,1,0:T(8,128)S(1)} %bitcast.9), channel_id=1, replica_groups=mesh['ctx_0'=4,'ctx_1'=16,'row'=4,'core'=2] {'ctx_1'}, dimensions={0} | all-to-all | bytes 524288 | tf_op jit(solution)/shard_map/all_to_all | solution.py:306
  114.0 0.6 scan_total.3
  114.6 8.0 %all_to_all.32.total_ref = f32[4,32,128]{2,1,0:T(8,128)S(1)} all-to-all(f32[4,32,128]{2,1,0:T(8,128)S(1)} %scan_total.3), channel_id=1, replica_groups=mesh['ctx_0'=4,'ctx_1'=16,'row'=4,'core'=2] {'ctx_0'}, dimensions={0} | all-to-all | bytes 131072 | tf_op jit(solution)/shard_map/all_to_all | solution.py:307
  122.6 1.3 scan_prefix.3
  123.8 5.0 %all-to-all-start.5 = ((f32[16,32,128]{2,1,0:T(8,128)}), f32[16,32,128]{2,1,0:T(8,128)S(1)}, u32[]{:S(2)}, u32[]{:S(2)}) async-start(f32[16,32,128]{2,1,0:T(8,128)} %scan_prefix.3), calls=%async_computation.5 | async-start | bytes 524288 | tf_op jit(solution)/shard_map/all_to_all | solution.py:309
  128.9 0.0 copy-done.5
  128.9 6.0 %local.1 = (bf16[512,512]{1,0:T(8,128)(2,1)}, bf16[512,512]{1,0:T(8,128)(2,1)}, f32[512,512]{1,0:T(8,128)}, f32[512,512]{1,0:T(8,128)}) custom-call(f32[4]{0:T(128)} %rates.11, bf16[512,512]{1,0:T(8,128)(2,1)} %queries.7, bf16[512,512]{1,0:T(8,128)(2,1)} %keys.7, bf16[512,512]{1,0:T(8,128)(2,1)} %values.7, bf16[512,512]{1,0:T(8,128)(2,1)} %out_grad.5, ...), custom_call_target="tpu_custom_call" | custom-call | flops 400000000 | bytes 4000000 | tf_op jit(solution)/shard_map/local/pallas_call | solution.py:229
  134.9 11.2 %all-to-all-done.5 = f32[16,32,128]{2,1,0:T(8,128)S(1)} async-done(((f32[16,32,128]{2,1,0:T(8,128)}), f32[16,32,128]{2,1,0:T(8,128)S(1)}, u32[]{:S(2)}, u32[]{:S(2)}) %all-to-all-start.5) | async-done | bytes 262176 | tf_op jit(solution)/shard_map/all_to_all | solution.py:309
  146.1 4.5 %finish.1 = (bf16[512,512]{1,0:T(8,128)(2,1)}, bf16[512,512]{1,0:T(8,128)(2,1)}) custom-call(f32[4]{0:T(128)} %rates.11, bf16[512,512]{1,0:T(8,128)(2,1)} %keys.7, bf16[512,512]{1,0:T(8,128)(2,1)} %values.7, f32[512,512]{1,0:T(8,128)} %get-tuple-element.26.key_part, f32[512,512]{1,0:T(8,128)} %get-tuple-element.27.value_part, f32[4,128,128]{2,1,0:T(8,128)S(1)} %bitcast.8, ...), custom_call_target="tpu_custom_call" | custom-call | tf_op jit(solution)/shard_map/finish/pallas_call | solution.py:385
  (1 shorter events, 0.0 us)
Async XLA Ops:
  0.6 1.0 copy-start.2
  1.7 1.0 copy-start.3
  2.7 0.7 copy-start.9
  5.2 33.1 %all-to-all-start = ((f32[16,32,128]{2,1,0:T(8,128)}), f32[16,32,128]{2,1,0:T(8,128)S(1)}, u32[]{:S(2)}, u32[]{:S(2)}) async-start(f32[16,32,128]{2,1,0:T(8,128)} %bitcast.1), calls=%async_computation | async-start | bytes 524288 | tf_op jit(solution)/shard_map/all_to_all | solution.py:306
  20.4 0.7 copy-start.10
  49.9 23.9 %all-to-all-start.2 = ((f32[16,32,128]{2,1,0:T(8,128)}), f32[16,32,128]{2,1,0:T(8,128)S(1)}, u32[]{:S(2)}, u32[]{:S(2)}) async-start(f32[16,32,128]{2,1,0:T(8,128)} %scan_prefix.2), calls=%async_computation.2 | async-start | bytes 524288 | tf_op jit(solution)/shard_map/all_to_all | solution.py:309
  56.1 17.7 %copy-start = (bf16[512,512]{1,0:T(8,128)(2,1)S(1)}, bf16[512,512]{1,0:T(8,128)(2,1)}, u32[]{:S(2)}) copy-start(bf16[512,512]{1,0:T(8,128)(2,1)} %queries.7) | copy-start | bytes 1572868
  56.1 17.7 %copy-start.1 = (bf16[512,512]{1,0:T(8,128)(2,1)S(1)}, bf16[512,512]{1,0:T(8,128)(2,1)}, u32[]{:S(2)}) copy-start(bf16[512,512]{1,0:T(8,128)(2,1)} %out_grad.5) | copy-start | bytes 1572868
  59.4 1.0 copy-start.6
  73.8 0.7 copy-start.8
  73.8 0.7 copy-start.11
  74.5 1.2 copy-start.7
  77.0 14.7 %copy-start.4 = (f32[512,512]{1,0:T(8,128)}, f32[512,512]{1,0:T(8,128)S(1)}, u32[]{:S(2)}) copy-start(f32[512,512]{1,0:T(8,128)S(1)} %get-tuple-element.23.attention) | copy-start | bytes 3145732
  91.6 37.2 %copy-start.5 = (f32[512,512]{1,0:T(8,128)S(1)}, f32[512,512]{1,0:T(8,128)}, u32[]{:S(2)}) copy-start(f32[512,512]{1,0:T(8,128)} %copy-done.4) | copy-start | bytes 3145732
  123.8 22.3 %all-to-all-start.5 = ((f32[16,32,128]{2,1,0:T(8,128)}), f32[16,32,128]{2,1,0:T(8,128)S(1)}, u32[]{:S(2)}, u32[]{:S(2)}) async-start(f32[16,32,128]{2,1,0:T(8,128)} %scan_prefix.3), calls=%async_computation.5 | async-start | bytes 524288 | tf_op jit(solution)/shard_map/all_to_all | solution.py:309

commit v3 on v2

--- a/solution.py
+++ b/solution.py
@@ -60,26 +60,41 @@
     array: object
 
 
+@dataclasses.dataclass
+class Far:
+    array: object
+
+
 def cols_of(head):
     return slice(head * 128, (head + 1) * 128)
 
 
 def memory_kernel(rates, keys, values, end, first):
-    rows_in = rows_of((BLOCK, 128))
+    block = pl.program_id(0)
+    to_last = BLOCK - 1.0 - rows_of((BLOCK, 128))
     for head in range(4):
         cols = cols_of(head)
-        trailing = jnp.exp(-rates[head] * (BLOCK - 1.0 - rows_in))
+        wide = keys[:, cols].astype(F32) * jnp.exp(-rates[head] * to_last)
+        update = dot_wide_left(wide, values[:, cols], 0, 0)
         full = jnp.exp(jnp.full((128, 128), -BLOCK * rates[head], F32))
-        updates = []
-        for block in range(2):
-            rows = block_rows(block)
-            wide = keys[rows, cols].astype(F32) * trailing
-            updates.append(dot_wide_left(wide, values[rows, cols], 0, 0))
-        first[head] = updates[0]
-        end[head] = full * updates[0] + updates[1]
-
-
-def inside_kernel(rates, queries, keys, values, probs, inside):
+
+        @pl.when(block == 0)
+        def _():
+            first[head] = update
+
+        @pl.when(block > 0)
+        def _():
+            end[head] = full * first[head] + update
+
+
+def rate_row(table, head):
+    return table[1 + head : 2 + head, 0:128]
+
+
+def inside_kernel(rates, queries, keys, values, gain, probs, inside, table):
+    table[0:1, :] = gain[...]
+    for head in range(4):
+        table[1 + head : 2 + head, :] = jnp.full((1, table.shape[1]), rates[head], F32)
     for head in range(4):
         cols = cols_of(head)
         weights = decay_weights(rates[head])
@@ -91,23 +106,36 @@
             inside[rows, cols] = dot(low, values[rows, cols], 1, 0)
 
 
-def carried_kernel(rates, queries, entering, first, inside, gain, out_grad, attention, sums):
+def carried_kernel(
+    table, queries, entering, first, far_inside, out_grad, attention, sums, inside, ready
+):
+    loads = []
+    for block in range(2):
+        rows = block_rows(block)
+        load = pltpu.make_async_copy(
+            far_inside.at[rows, :], inside.at[rows, :], ready.at[block]
+        )
+        load.start()
+        loads.append(load)
     after_start = rows_of((BLOCK, 128)) + 1.0
     squares, products = [], []
     for block in range(2):
         rows = block_rows(block)
-        square = product = None
         for head in range(4):
             cols = cols_of(head)
             memory = entering[head]
             if block == 1:
-                full = jnp.exp(jnp.full((128, 128), -BLOCK * rates[head], F32))
-                memory = full * memory + first[head]
-            leading = jnp.exp(-rates[head] * after_start)
-            carried = dot_wide_right(queries[rows, cols], memory, 1, 0) * leading
-            out = inside[rows, cols] + carried
+                memory = jnp.exp(-BLOCK * rate_row(table, head)) * memory + first[head]
+            leading = jnp.exp(-rate_row(table, head) * after_start)
+            carried = dot_wide_right(queries[rows, cols], memory, 1, 0)
+            attention[rows, cols] = carried * leading
+        loads[block].wait()
+        square = product = None
+        for head in range(4):
+            cols = cols_of(head)
+            out = inside[rows, cols] + attention[rows, cols]
             attention[rows, cols] = out
-            grad = out_grad[rows, cols].astype(F32) * gain[:, cols]
+            grad = out_grad[rows, cols].astype(F32) * table[0:1, cols]
             square = out * out if square is None else square + out * out
             product = grad * out if product is None else product + grad * out
         for part, flat in ((square, squares), (product, products)):
@@ -137,7 +165,7 @@
     return normed, (scale * (grad - normed * coeff)).astype(BF16)
 
 
-def grad_kernel(features, rates, sums, queries, attention, gain, out_grad, end, second):
+def grad_kernel(features, table, sums, queries, attention, out_grad, end):
     from_start = rows_of((BLOCK, 128))
     for block in (1, 0):
         rows = block_rows(block)
@@ -145,15 +173,14 @@
         for head in range(4):
             cols = cols_of(head)
             _, low = attention_grad(
-                attention[rows, cols], out_grad[rows, cols], gain[:, cols], scale, coeff
+                attention[rows, cols], out_grad[rows, cols], table[0:1, cols], scale, coeff
             )
-            start = jnp.exp(-rates[head] * from_start)
+            start = jnp.exp(-rate_row(table, head) * from_start)
             gathered = dot_wide_left(queries[rows, cols].astype(F32) * start, low, 0, 0)
             if block == 1:
-                second[head] = gathered
+                end[head] = gathered
             else:
-                full = jnp.exp(jnp.full((128, 128), -BLOCK * rates[head], F32))
-                end[head] = full * second[head] + gathered
+                end[head] = jnp.exp(-BLOCK * rate_row(table, head)) * end[head] + gathered
 
 
 def local_kernel(
@@ -173,6 +200,7 @@
     normed_out,
     key_part,
     value_part,
+    second,
 ):
     after_start = rows_of((BLOCK, 128)) + 1.0
     for block in range(2):
@@ -195,20 +223,24 @@
             query_grad[rows, cols] = (dot(low, keys[rows, cols], 1, 0) + carried).astype(BF16)
             key_part[rows, cols] = dot(low, queries[rows, cols], 0, 0)
             value_part[rows, cols] = dot(probs[head, block], grad, 0, 0)
+            if block == 1:
+                start = jnp.exp(-rates[head] * (after_start - 1.0))
+                second[head] = dot_wide_left(queries[rows, cols].astype(F32) * start, grad, 0, 0)
 
 
 def finish_kernel(
     rates, keys, values, key_part, value_part, after, second, key_grad, value_grad
 ):
     tile = pl.program_id(0)
+    rows = pl.ds(tile * 128, 128)
     to_end = BLOCK - rows_of((128, 128)) - 128.0 * (tile % 2).astype(F32)
     for head in range(4):
         cols = cols_of(head)
         ending = jnp.exp(-rates[head] * to_end)
         full = jnp.exp(jnp.full((128, 128), -BLOCK * rates[head], F32))
         backlog = jnp.where(tile < 2, full * after[head] + second[head], after[head])
-        key_more = dot_wide_right(values[:, cols], backlog, 1, 1) * ending
-        value_more = dot_wide_right(keys[:, cols], backlog, 1, 0) * ending
+        key_more = dot_wide_right(values[rows, cols], backlog, 1, 1) * ending
+        value_more = dot_wide_right(keys[rows, cols], backlog, 1, 0) * ending
         key_grad[:, cols] = (key_part[:, cols] + key_more).astype(BF16)
         value_grad[:, cols] = (value_part[:, cols] + value_more).astype(BF16)
 
@@ -221,22 +253,30 @@
     return pltpu.with_memory_space_constraint(array, pltpu.VMEM)
 
 
-def call(kernel, name, outs, *operands, grant=GRANT):
-    rates, *rest = operands
-    streamed = [isinstance(array, Streamed) for array in rest]
-    arrays = [array.array if isinstance(array, Streamed) else array for array in rest]
-    far = pl.BlockSpec()
+def place_of(item):
+    if isinstance(item, Far):
+        return pl.BlockSpec(memory_space=pltpu.HBM)
+    return pl.BlockSpec() if isinstance(item, Streamed) else VMEM
+
+
+def bare(item):
+    return item.array if isinstance(item, (Far, Streamed)) else item
+
+
+def call(kernel, name, outs, *operands, grant=GRANT, rates=None, scratch=()):
+    small = [] if rates is None else [rates]
     return pl.pallas_call(
         kernel,
-        in_specs=[SMEM] + [far if flag else VMEM for flag in streamed],
-        out_specs=tuple(far if isinstance(out, Streamed) else VMEM for out in outs),
-        out_shape=tuple(out.array if isinstance(out, Streamed) else out for out in outs),
+        in_specs=[SMEM] * len(small) + [place_of(item) for item in operands],
+        out_specs=tuple(place_of(item) for item in outs),
+        out_shape=tuple(bare(item) for item in outs),
+        scratch_shapes=scratch,
         name=name,
         cost_estimate=pl.CostEstimate(
             flops=400_000_000, bytes_accessed=4_000_000, transcendentals=300_000
         ),
         compiler_params=pltpu.CompilerParams(vmem_limit_bytes=grant),
-    )(rates, *arrays)
+    )(*small, *map(bare, operands))
 
 
 def scan_total(table, pieces, reverse):
@@ -320,54 +360,56 @@
     tables = shape(heads, 2, BLOCK, BLOCK, dtype=BF16)
     state_near, wide_near = pltpu.VMEM(state.shape, F32), pltpu.VMEM(wide.shape, F32)
     far_q, far_k, far_v, far_grad = map(Streamed, (queries, key_rows, value_rows, out_grad))
-    memory_end, memory_first = call(
+    block_rows_spec = pl.BlockSpec((BLOCK, width), lambda block: (block, 0))
+    states = pl.BlockSpec(state.shape, lambda block: (0, 0, 0))
+    memory_end, memory_first = pl.pallas_call(
         memory_kernel,
-        "memory",
-        (state_near, state_near),
-        decay_rates,
-        near(key_rows),
-        near(value_rows),
-    )
-    probs, inside = call(
+        grid=(tokens // BLOCK,),
+        in_specs=[SMEM, block_rows_spec, block_rows_spec],
+        out_specs=(states, states),
+        out_shape=(state, state),
+        name="memory",
+    )(decay_rates, key_rows, value_rows)
+    probs, inside, aux = call(
         inside_kernel,
         "inside",
-        (Streamed(tables), wide_near),
-        decay_rates,
+        (Streamed(tables), Streamed(wide), pltpu.VMEM((8, width), F32)),
         far_q,
         far_k,
         far_v,
+        Streamed(gain),
         grant=None,
+        rates=decay_rates,
     )
     entering = along_context(table, memory_end, False)
     attention, sums = call(
         carried_kernel,
         "carried",
         (wide_near, pltpu.VMEM((8, 128), F32)),
-        decay_rates,
+        near(aux),
         near(queries),
         near(entering),
         near(memory_first),
-        near(inside),
-        near(gain),
+        Far(inside),
         near(out_grad),
+        grant=None,
+        scratch=(wide_near, pltpu.SemaphoreType.DMA((2,))),
     )
     sums = lax.psum(lax.psum(sums, "core"), "row")
-    backlog_end, backlog_second = call(
+    (backlog_end,) = call(
         functools.partial(grad_kernel, features),
         "grad",
-        (state_near, state_near),
-        decay_rates,
+        (state_near,),
+        near(aux),
         near(sums),
         near(queries),
         near(attention),
-        near(gain),
         near(out_grad),
     )
-    query_grad, normed_out, key_part, value_part = call(
+    query_grad, normed_out, key_part, value_part, backlog_second = call(
         functools.partial(local_kernel, features),
         "local",
-        (Streamed(narrow), Streamed(narrow), Streamed(wide), Streamed(wide)),
-        decay_rates,
+        (Streamed(narrow), Streamed(narrow), Streamed(wide), Streamed(wide), state_near),
         far_q,
         far_k,
         far_v,
@@ -377,22 +419,23 @@
         near(memory_first),
         near(sums),
         near(attention),
-        near(gain),
+        Streamed(gain),
         grant=None,
+        rates=decay_rates,
     )
     after = along_context(table, backlog_end, True)
     tile_rows = pl.BlockSpec((128, width), lambda tile: (tile, 0))
     key_grad, value_grad = pl.pallas_call(
         finish_kernel,
         grid=(tokens // 128,),
-        in_specs=[SMEM] + [tile_rows] * 4 + [VMEM] * 2,
+        in_specs=[SMEM] + [VMEM] * 2 + [tile_rows] * 2 + [VMEM] * 2,
         out_specs=(tile_rows, tile_rows),
         out_shape=(narrow, narrow),
         name="finish",
     )(
         decay_rates,
-        key_rows,
-        value_rows,
+        near(key_rows),
+        near(value_rows),
         key_part,
         value_part,
         near(after),

time: 152 us -> 149 us (0.980)
  local copies, waits for them, and re-layouts: 6.88 us -> 1.27 us
  Pallas kernels: 22.1 us -> 24.1 us
    unnamed x24 -> x18, local copies, waits for them, and re-layouts: 6.29 us -> 0.69 us
    pallas_call x6, Pallas kernels: 18.3 us -> 20.4 us  [the longest x4 12.2 us: call(): pl.pallas_call(kernel, in_specs=[SMEM] * len(small) + [place_of(item) for...]
  transfers between devices with their start and end apart: 3 -> 3, of which waited for: 3 -> 3; matrix products, arithmetic and copies ran while one was open for 0% -> 0% of each run, Pallas kernels for 6% -> 7%
where the time goes in v3:
time: 149 us; the launch traced here: 148 us
  blocking collectives  53.2 us (36%)
  waiting for transfers between devices  41.2 us (28%)
  starting transfers between devices  26.6 us (18%)
  Pallas kernels  24.1 us (16%)
    all_to_all x2, waiting for transfers between devices, along_context(): return lax.all_to_all(prefix, LINE[1], 0, 0).reshape(state.shape)  25.2 us
    all_to_all x1, blocking collectives, along_context(): pieces = lax.all_to_all(state.reshape(near_size, -1, lanes), LINE[1], 0, 0)  22.4 us
    all_to_all x2, blocking collectives, along_context(): totals = lax.all_to_all(scan_total(table, pieces, reverse), LINE[0], 0, 0)  17.7 us
    all_to_all x1, waiting for transfers between devices, along_context(): pieces = lax.all_to_all(state.reshape(near_size, -1, lanes), LINE[1], 0, 0)  16 us
    all_to_all x1, starting transfers between devices, along_context(): pieces = lax.all_to_all(state.reshape(near_size, -1, lanes), LINE[1], 0, 0)  15.2 us
    psum x2, blocking collectives, on_device(): sums = lax.psum(lax.psum(sums, 'core'), 'row')  13.2 us
    pallas_call x4, Pallas kernels, call(): pl.pallas_call(kernel, in_specs=[SMEM] * len(small) + [place_of(item) for...  12.2 us
    all_to_all x2, starting transfers between devices, along_context(): return lax.all_to_all(prefix, LINE[1], 0, 0).reshape(state.shape)  11.4 us
  transfers between devices with their start and end apart: 3, of which 3 were waited for; matrix products, arithmetic and copies ran while one was open for 0% of the time, Pallas kernels for 7%

profile of v3, /device:TPU:32, one launch (start us, length us, event | category | flops | bytes accessed | tf_op | source)
XLA Modules:
  0.0 147.9 jit_solution(11221728424212053762)
XLA Ops:
  0.6 3.9 %memory.1 = (f32[4,128,128]{2,1,0:T(8,128)}, f32[4,128,128]{2,1,0:T(8,128)}) custom-call(f32[4]{0:T(128)} %rates.7, bf16[512,512]{1,0:T(8,128)(2,1)} %keys.7, bf16[512,512]{1,0:T(8,128)(2,1)} %values.7), custom_call_target="tpu_custom_call" | custom-call | tf_op jit(solution)/shard_map/memory/pallas_call | solution.py:365
  4.5 15.2 %all-to-all-start = ((f32[16,32,128]{2,1,0:T(8,128)}), f32[16,32,128]{2,1,0:T(8,128)S(1)}, u32[]{:S(2)}, u32[]{:S(2)}) async-start(f32[16,32,128]{2,1,0:T(8,128)} %bitcast.10), calls=%async_computation | async-start | bytes 524288 | tf_op jit(solution)/shard_map/all_to_all | solution.py:346
  19.7 0.0 copy-start.8
  19.7 0.6 copy-done.8
  20.4 0.6 dynamic_slice.4
  21.6 16.0 %all-to-all-done.piece_ref = f32[16,32,128]{2,1,0:T(8,128)S(1)} async-done(((f32[16,32,128]{2,1,0:T(8,128)}), f32[16,32,128]{2,1,0:T(8,128)S(1)}, u32[]{:S(2)}, u32[]{:S(2)}) %all-to-all-start) | async-done | bytes 262176 | tf_op jit(solution)/shard_map/all_to_all | solution.py:346
  37.7 0.6 scan_total.2
  38.2 9.7 %all_to_all.30.total_ref = f32[4,32,128]{2,1,0:T(8,128)S(1)} all-to-all(f32[4,32,128]{2,1,0:T(8,128)S(1)} %scan_total.2), channel_id=1, replica_groups=mesh['ctx_0'=4,'ctx_1'=16,'row'=4,'core'=2] {'ctx_0'}, dimensions={0} | all-to-all | bytes 131072 | tf_op jit(solution)/shard_map/all_to_all | solution.py:347
  47.9 1.3 scan_prefix.2
  49.2 6.2 %all-to-all-start.2 = ((f32[16,32,128]{2,1,0:T(8,128)}), f32[16,32,128]{2,1,0:T(8,128)S(1)}, u32[]{:S(2)}, u32[]{:S(2)}) async-start(f32[16,32,128]{2,1,0:T(8,128)} %scan_prefix.2), calls=%async_computation.2 | async-start | bytes 524288 | tf_op jit(solution)/shard_map/all_to_all | solution.py:349
  55.5 0.0 copy-start
  55.5 0.0 copy-start.3
  55.5 0.0 copy-start.6
  55.5 3.6 %inside.1 = (bf16[4,2,256,256]{3,2,1,0:T(8,128)(2,1)}, f32[512,512]{1,0:T(8,128)}, f32[8,512]{1,0:T(8,128)S(1)}) custom-call(f32[4]{0:T(128)} %rates.7, bf16[512,512]{1,0:T(8,128)(2,1)} %queries.7, bf16[512,512]{1,0:T(8,128)(2,1)} %keys.7, bf16[512,512]{1,0:T(8,128)(2,1)} %values.7, f32[1,512]{1,0:T(1,128)} %bitcast.11), custom_call_target="tpu_custom_call" | custom-call | flops 400000000 | bytes 4000000 | tf_op jit(solution)/shard_map/inside/pallas_call | solution.py:268
  59.1 14.0 %all-to-all-done.2 = f32[16,32,128]{2,1,0:T(8,128)S(1)} async-done(((f32[16,32,128]{2,1,0:T(8,128)}), f32[16,32,128]{2,1,0:T(8,128)S(1)}, u32[]{:S(2)}, u32[]{:S(2)}) %all-to-all-start.2) | async-done | bytes 262176 | tf_op jit(solution)/shard_map/all_to_all | solution.py:349
  73.1 0.0 copy-done
  73.1 0.0 copy-done.3
  73.2 0.0 copy-done.6
  73.2 1.6 %carried.1 = (f32[512,512]{1,0:T(8,128)S(1)}, f32[8,128]{1,0:T(8,128)S(1)}) custom-call(f32[8,512]{1,0:T(8,128)S(1)} %get-tuple-element.21.table, bf16[512,512]{1,0:T(8,128)(2,1)S(1)} %copy-done, f32[4,128,128]{2,1,0:T(8,128)S(1)} %bitcast.6, f32[4,128,128]{2,1,0:T(8,128)S(1)} %copy-done.6, f32[512,512]{1,0:T(8,128)} %get-tuple-element.22.far_inside, ...), custom_call_target="tpu_custom_call" | custom-call | flops 400000000 | bytes 4000000 | tf_op jit(solution)/shard_map/carried/pallas_call | solution.py:268
  74.8 0.0 copy-start.4
  74.8 2.5 %psum.14 = f32[8,128]{1,0:T(8,128)S(1)} all-reduce(f32[8,128]{1,0:T(8,128)S(1)} %get-tuple-element.23), channel_id=1, replica_groups=mesh['ctx_0'=4,'ctx_1'=16,'row'=4,'core'=2] {'core'}, use_global_device_ids=true, to_apply=%region_0.1 | all-reduce | flops 1024 | bytes 8192 | tf_op jit(solution)/shard_map/psum | solution.py:398
  77.3 10.7 %psum.15.sums = f32[8,128]{1,0:T(8,128)S(1)} all-reduce(f32[8,128]{1,0:T(8,128)S(1)} %psum.14), channel_id=1, replica_groups=mesh['ctx_0'=4,'ctx_1'=16,'row'=4,'core'=2] {'row'}, use_global_device_ids=true, to_apply=%region_1.2 | all-reduce | flops 1024 | bytes 8192 | tf_op jit(solution)/shard_map/psum | solution.py:398
  88.0 0.9 grad.1
  88.9 0.0 copy-done.4
  88.9 0.0 copy-start.5
  88.9 22.4 %all_to_all.31.piece_ref = f32[16,32,128]{2,1,0:T(8,128)S(1)} all-to-all(f32[16,32,128]{2,1,0:T(8,128)S(1)} %bitcast.8), channel_id=1, replica_groups=mesh['ctx_0'=4,'ctx_1'=16,'row'=4,'core'=2] {'ctx_1'}, dimensions={0} | all-to-all | bytes 524288 | tf_op jit(solution)/shard_map/all_to_all | solution.py:346
  111.3 0.6 scan_total.3
  111.9 8.0 %all_to_all.32.total_ref = f32[4,32,128]{2,1,0:T(8,128)S(1)} all-to-all(f32[4,32,128]{2,1,0:T(8,128)S(1)} %scan_total.3), channel_id=1, replica_groups=mesh['ctx_0'=4,'ctx_1'=16,'row'=4,'core'=2] {'ctx_0'}, dimensions={0} | all-to-all | bytes 131072 | tf_op jit(solution)/shard_map/all_to_all | solution.py:347
  119.8 1.3 scan_prefix.3
  121.1 0.0 copy-start.7
  121.1 5.2 %all-to-all-start.5 = ((f32[16,32,128]{2,1,0:T(8,128)}), f32[16,32,128]{2,1,0:T(8,128)S(1)}, u32[]{:S(2)}, u32[]{:S(2)}) async-start(f32[16,32,128]{2,1,0:T(8,128)} %scan_prefix.3), calls=%async_computation.5 | async-start | bytes 524288 | tf_op jit(solution)/shard_map/all_to_all | solution.py:349
  126.3 0.0 copy-done.5
  126.3 0.0 copy-done.7
  126.3 0.0 copy-start.1
  126.3 0.0 copy-start.2
  126.3 6.0 %local.1 = (bf16[512,512]{1,0:T(8,128)(2,1)}, bf16[512,512]{1,0:T(8,128)(2,1)}, f32[512,512]{1,0:T(8,128)}, f32[512,512]{1,0:T(8,128)}, f32[4,128,128]{2,1,0:T(8,128)S(1)}) custom-call(f32[4]{0:T(128)} %rates.7, bf16[512,512]{1,0:T(8,128)(2,1)} %queries.7, bf16[512,512]{1,0:T(8,128)(2,1)} %keys.7, bf16[512,512]{1,0:T(8,128)(2,1)} %values.7, ...), custom_call_target="tpu_custom_call" | custom-call | flops 400000000 | bytes 4000000 | tf_op jit(solution)/shard_map/local/pallas_call | solution.py:268
  132.4 11.2 %all-to-all-done.5 = f32[16,32,128]{2,1,0:T(8,128)S(1)} async-done(((f32[16,32,128]{2,1,0:T(8,128)}), f32[16,32,128]{2,1,0:T(8,128)S(1)}, u32[]{:S(2)}, u32[]{:S(2)}) %all-to-all-start.5) | async-done | bytes 262176 | tf_op jit(solution)/shard_map/all_to_all | solution.py:349
  143.6 0.0 copy-done.1
  143.6 0.0 copy-done.2
  143.6 4.3 %finish.1 = (bf16[512,512]{1,0:T(8,128)(2,1)}, bf16[512,512]{1,0:T(8,128)(2,1)}) custom-call(f32[4]{0:T(128)} %rates.7, bf16[512,512]{1,0:T(8,128)(2,1)S(1)} %copy-done.1, bf16[512,512]{1,0:T(8,128)(2,1)S(1)} %copy-done.2, f32[512,512]{1,0:T(8,128)} %get-tuple-element.27.key_part, f32[512,512]{1,0:T(8,128)} %get-tuple-element.28.value_part, ...), custom_call_target="tpu_custom_call" | custom-call | tf_op jit(solution)/shard_map/finish/pallas_call | solution.py:428
  (1 shorter events, 0.0 us)
Async XLA Ops:
  4.5 33.1 %all-to-all-start = ((f32[16,32,128]{2,1,0:T(8,128)}), f32[16,32,128]{2,1,0:T(8,128)S(1)}, u32[]{:S(2)}, u32[]{:S(2)}) async-start(f32[16,32,128]{2,1,0:T(8,128)} %bitcast.10), calls=%async_computation | async-start | bytes 524288 | tf_op jit(solution)/shard_map/all_to_all | solution.py:346
  19.7 0.7 copy-start.8
  49.2 23.9 %all-to-all-start.2 = ((f32[16,32,128]{2,1,0:T(8,128)}), f32[16,32,128]{2,1,0:T(8,128)S(1)}, u32[]{:S(2)}, u32[]{:S(2)}) async-start(f32[16,32,128]{2,1,0:T(8,128)} %scan_prefix.2), calls=%async_computation.2 | async-start | bytes 524288 | tf_op jit(solution)/shard_map/all_to_all | solution.py:349
  55.5 17.7 %copy-start = (bf16[512,512]{1,0:T(8,128)(2,1)S(1)}, bf16[512,512]{1,0:T(8,128)(2,1)}, u32[]{:S(2)}) copy-start(bf16[512,512]{1,0:T(8,128)(2,1)} %queries.7) | copy-start | bytes 1572868
  55.5 17.7 %copy-start.3 = (bf16[512,512]{1,0:T(8,128)(2,1)S(1)}, bf16[512,512]{1,0:T(8,128)(2,1)}, u32[]{:S(2)}) copy-start(bf16[512,512]{1,0:T(8,128)(2,1)} %out_grad.5) | copy-start | bytes 1572868
  55.5 17.7 %copy-start.6 = (f32[4,128,128]{2,1,0:T(8,128)S(1)}, f32[4,128,128]{2,1,0:T(8,128)}, u32[]{:S(2)}) copy-start(f32[4,128,128]{2,1,0:T(8,128)} %get-tuple-element.20.first) | copy-start | bytes 786436
  74.8 14.1 %copy-start.4 = (f32[512,512]{1,0:T(8,128)}, f32[512,512]{1,0:T(8,128)S(1)}, u32[]{:S(2)}) copy-start(f32[512,512]{1,0:T(8,128)S(1)} %get-tuple-element.24.attention) | copy-start | bytes 3145732
  88.9 37.4 %copy-start.5 = (f32[512,512]{1,0:T(8,128)S(1)}, f32[512,512]{1,0:T(8,128)}, u32[]{:S(2)}) copy-start(f32[512,512]{1,0:T(8,128)} %copy-done.4) | copy-start | bytes 3145732
  121.1 5.2 %copy-start.7 = (f32[4,128,128]{2,1,0:T(8,128)S(1)}, f32[4,128,128]{2,1,0:T(8,128)}, u32[]{:S(2)}) copy-start(f32[4,128,128]{2,1,0:T(8,128)} %get-tuple-element.20.first) | copy-start | bytes 786436
  121.1 22.4 %all-to-all-start.5 = ((f32[16,32,128]{2,1,0:T(8,128)}), f32[16,32,128]{2,1,0:T(8,128)S(1)}, u32[]{:S(2)}, u32[]{:S(2)}) async-start(f32[16,32,128]{2,1,0:T(8,128)} %scan_prefix.3), calls=%async_computation.5 | async-start | bytes 524288 | tf_op jit(solution)/shard_map/all_to_all | solution.py:349
  126.3 17.3 %copy-start.1 = (bf16[512,512]{1,0:T(8,128)(2,1)S(1)}, bf16[512,512]{1,0:T(8,128)(2,1)}, u32[]{:S(2)}) copy-start(bf16[512,512]{1,0:T(8,128)(2,1)} %keys.7) | copy-start | bytes 1572868
  126.3 17.3 %copy-start.2 = (bf16[512,512]{1,0:T(8,128)(2,1)S(1)}, bf16[512,512]{1,0:T(8,128)(2,1)}, u32[]{:S(2)}) copy-start(bf16[512,512]{1,0:T(8,128)(2,1)} %values.7) | copy-start | bytes 1572868

commit v4 on v3

--- a/solution.py
+++ b/solution.py
@@ -32,13 +32,14 @@
 
 
 def dot_wide_right(left, right, left_dim, right_dim):
-    high, low = halves(right)
-    return dot(left, high, left_dim, right_dim) + dot(left, low, left_dim, right_dim)
-
-
-def dot_wide_left(left, right, left_dim, right_dim):
-    high, low = halves(left)
-    return dot(high, right, left_dim, right_dim) + dot(low, right, left_dim, right_dim)
+    twice = jnp.concatenate([left, left], axis=left_dim)
+    return dot(twice, jnp.concatenate(halves(right), axis=right_dim), left_dim, right_dim)
+
+
+def dot_wide_left(left, right):
+    both = dot(jnp.concatenate(halves(left), axis=1), right, 0, 0)
+    width = left.shape[1]
+    return both[:width] + both[width:]
 
 
 def rows_of(shape):
@@ -69,22 +70,41 @@
     return slice(head * 128, (head + 1) * 128)
 
 
-def memory_kernel(rates, keys, values, end, first):
-    block = pl.program_id(0)
+def start_copies(pairs, flags):
+    copies = []
+    for source, target in pairs:
+        copy = pltpu.make_async_copy(source, target, flags.at[len(copies)])
+        copy.start()
+        copies.append(copy)
+    return copies
+
+
+def wait_all(copies):
+    for copy in copies:
+        copy.wait()
+
+
+def memory_kernel(rates, far_keys, far_values, end, first, keys, values, ready):
+    loads = []
+    for block in range(2):
+        rows = block_rows(block)
+        pairs = ((far_keys, keys), (far_values, values))
+        loads.append(
+            start_copies([(f.at[rows, :], n.at[rows, :]) for f, n in pairs], ready.at[block])
+        )
     to_last = BLOCK - 1.0 - rows_of((BLOCK, 128))
-    for head in range(4):
-        cols = cols_of(head)
-        wide = keys[:, cols].astype(F32) * jnp.exp(-rates[head] * to_last)
-        update = dot_wide_left(wide, values[:, cols], 0, 0)
-        full = jnp.exp(jnp.full((128, 128), -BLOCK * rates[head], F32))
-
-        @pl.when(block == 0)
-        def _():
-            first[head] = update
-
-        @pl.when(block > 0)
-        def _():
-            end[head] = full * first[head] + update
+    for block in range(2):
+        rows = block_rows(block)
+        wait_all(loads[block])
+        for head in range(4):
+            cols = cols_of(head)
+            wide = keys[rows, cols].astype(F32) * jnp.exp(-rates[head] * to_last)
+            update = dot_wide_left(wide, values[rows, cols])
+            if block == 0:
+                first[head] = update
+            else:
+                full = jnp.exp(jnp.full((128, 128), -BLOCK * rates[head], F32))
+                end[head] = full * first[head] + update
 
 
 def rate_row(table, head):
@@ -176,7 +196,7 @@
                 attention[rows, cols], out_grad[rows, cols], table[0:1, cols], scale, coeff
             )
             start = jnp.exp(-rate_row(table, head) * from_start)
-            gathered = dot_wide_left(queries[rows, cols].astype(F32) * start, low, 0, 0)
+            gathered = dot_wide_left(queries[rows, cols].astype(F32) * start, low)
             if block == 1:
                 end[head] = gathered
             else:
@@ -225,24 +245,53 @@
             value_part[rows, cols] = dot(probs[head, block], grad, 0, 0)
             if block == 1:
                 start = jnp.exp(-rates[head] * (after_start - 1.0))
-                second[head] = dot_wide_left(queries[rows, cols].astype(F32) * start, grad, 0, 0)
+                second[head] = dot_wide_left(queries[rows, cols].astype(F32) * start, grad)
 
 
 def finish_kernel(
-    rates, keys, values, key_part, value_part, after, second, key_grad, value_grad
+    rates,
+    keys,
+    values,
+    far_key_part,
+    far_value_part,
+    after,
+    second,
+    far_key_grad,
+    far_value_grad,
+    key_part,
+    value_part,
+    key_more,
+    value_more,
+    key_grad,
+    value_grad,
+    ready,
+    done,
 ):
-    tile = pl.program_id(0)
-    rows = pl.ds(tile * 128, 128)
-    to_end = BLOCK - rows_of((128, 128)) - 128.0 * (tile % 2).astype(F32)
-    for head in range(4):
-        cols = cols_of(head)
-        ending = jnp.exp(-rates[head] * to_end)
-        full = jnp.exp(jnp.full((128, 128), -BLOCK * rates[head], F32))
-        backlog = jnp.where(tile < 2, full * after[head] + second[head], after[head])
-        key_more = dot_wide_right(values[rows, cols], backlog, 1, 1) * ending
-        value_more = dot_wide_right(keys[rows, cols], backlog, 1, 0) * ending
-        key_grad[:, cols] = (key_part[:, cols] + key_more).astype(BF16)
-        value_grad[:, cols] = (value_part[:, cols] + value_more).astype(BF16)
+    loads, stores = [], []
+    for block in range(2):
+        rows = block_rows(block)
+        pairs = ((far_key_part, key_part), (far_value_part, value_part))
+        loads.append(
+            start_copies([(f.at[rows, :], n.at[rows, :]) for f, n in pairs], ready.at[block])
+        )
+    to_end = BLOCK - rows_of((BLOCK, 128))
+    for block in range(2):
+        rows = block_rows(block)
+        for head in range(4):
+            cols = cols_of(head)
+            ending = jnp.exp(-rates[head] * to_end)
+            backlog = after[head]
+            if block == 0:
+                full = jnp.exp(jnp.full((128, 128), -BLOCK * rates[head], F32))
+                backlog = full * backlog + second[head]
+            key_more[:, cols] = dot_wide_right(values[rows, cols], backlog, 1, 1) * ending
+            value_more[:, cols] = dot_wide_right(keys[rows, cols], backlog, 1, 0) * ending
+        wait_all(loads[block])
+        key_grad[rows, :] = (key_part[rows, :] + key_more[...]).astype(BF16)
+        value_grad[rows, :] = (value_part[rows, :] + value_more[...]).astype(BF16)
+        pairs = ((key_grad, far_key_grad), (value_grad, far_value_grad))
+        stores += start_copies([(n.at[rows, :], f.at[rows, :]) for n, f in pairs], done.at[block])
+    wait_all(stores)
 
 
 def shape(*dims, dtype=F32):
@@ -304,22 +353,33 @@
 def scan_prefix(table, pieces, totals, reverse):
     count, rows, lanes = pieces.shape
     first = 5 if reverse else 1
-
-    def kernel(table_ref, piece_ref, total_ref, prefix_ref):
-        order = list(range(count - 1, -1, -1) if reverse else range(count))
+    stride = count // 4
+
+    def kernel(table_ref, piece_ref, total_ref, far_ref, prefix_ref, done):
         running = total_ref[0] * table_ref[first]
         for peer in range(1, total_ref.shape[0]):
             running = running + total_ref[peer] * table_ref[first + peer]
-        for k in order:
-            prefix_ref[k] = running
-            if k != order[-1]:
-                running = running * table_ref[0] + piece_ref[k]
+        stores = []
+        for part in range(4):
+            order = range(part * stride, (part + 1) * stride)
+            for step in order:
+                k = count - 1 - step if reverse else step
+                prefix_ref[k] = running
+                if step != count - 1:
+                    running = running * table_ref[0] + piece_ref[k]
+            low = count - (part + 1) * stride if reverse else part * stride
+            span = slice(low, low + stride)
+            store = pltpu.make_async_copy(prefix_ref.at[span], far_ref.at[span], done.at[part])
+            store.start()
+            stores.append(store)
+        wait_all(stores)
 
     return pl.pallas_call(
         kernel,
         in_specs=[SMEM, VMEM, VMEM],
-        out_specs=VMEM,
-        out_shape=pltpu.VMEM((count, rows, lanes), F32),
+        out_specs=pl.BlockSpec(memory_space=pltpu.HBM),
+        out_shape=shape(count, rows, lanes),
+        scratch_shapes=(pltpu.VMEM((count, rows, lanes), F32), pltpu.SemaphoreType.DMA((4,))),
         name="scan_prefix",
         compiler_params=pltpu.CompilerParams(vmem_limit_bytes=GRANT),
     )(table, near(pieces), near(totals))
@@ -360,16 +420,17 @@
     tables = shape(heads, 2, BLOCK, BLOCK, dtype=BF16)
     state_near, wide_near = pltpu.VMEM(state.shape, F32), pltpu.VMEM(wide.shape, F32)
     far_q, far_k, far_v, far_grad = map(Streamed, (queries, key_rows, value_rows, out_grad))
-    block_rows_spec = pl.BlockSpec((BLOCK, width), lambda block: (block, 0))
-    states = pl.BlockSpec(state.shape, lambda block: (0, 0, 0))
-    memory_end, memory_first = pl.pallas_call(
+    narrow_near, flags = pltpu.VMEM(narrow.shape, BF16), pltpu.SemaphoreType.DMA((2, 2))
+    memory_end, memory_first = call(
         memory_kernel,
-        grid=(tokens // BLOCK,),
-        in_specs=[SMEM, block_rows_spec, block_rows_spec],
-        out_specs=(states, states),
-        out_shape=(state, state),
-        name="memory",
-    )(decay_rates, key_rows, value_rows)
+        "memory",
+        (Streamed(state), state_near),
+        Far(key_rows),
+        Far(value_rows),
+        grant=None,
+        rates=decay_rates,
+        scratch=(narrow_near, narrow_near, flags),
+    )
     probs, inside, aux = call(
         inside_kernel,
         "inside",
@@ -424,22 +485,20 @@
         rates=decay_rates,
     )
     after = along_context(table, backlog_end, True)
-    tile_rows = pl.BlockSpec((128, width), lambda tile: (tile, 0))
-    key_grad, value_grad = pl.pallas_call(
+    more = pltpu.VMEM((BLOCK, width), F32)
+    key_grad, value_grad = call(
         finish_kernel,
-        grid=(tokens // 128,),
-        in_specs=[SMEM] + [VMEM] * 2 + [tile_rows] * 2 + [VMEM] * 2,
-        out_specs=(tile_rows, tile_rows),
-        out_shape=(narrow, narrow),
-        name="finish",
-    )(
-        decay_rates,
+        "finish",
+        (Far(narrow), Far(narrow)),
         near(key_rows),
         near(value_rows),
-        key_part,
-        value_part,
+        Far(key_part),
+        Far(value_part),
         near(after),
         near(backlog_second),
+        grant=None,
+        rates=decay_rates,
+        scratch=(wide_near, wide_near, more, more, narrow_near, narrow_near, flags, flags),
     )
     return (normed_out, query_grad, key_grad, value_grad)
 

time: 149 us -> 147 us (0.987)
  Pallas kernels: 24.1 us -> 22.5 us
    pallas_call x4 -> x2, Pallas kernels: 10.8 us -> 2.57 us  [scan_prefix(): pl.pallas_call(kernel, in_specs=[SMEM, VMEM, VMEM], out_specs=pl.BlockSpe...]
    pallas_call x4 -> x6, Pallas kernels: 12.2 us -> 18.8 us  [call(): pl.pallas_call(kernel, in_specs=[SMEM] * len(small) + [place_of(item) for...]
where the time goes in v4:
time: 147 us; the launch traced here: 146 us
  blocking collectives  53.2 us (36%)
  waiting for transfers between devices  41.3 us (28%)
  starting transfers between devices  26.7 us (18%)
  Pallas kernels  22.5 us (15%)
    all_to_all x2, waiting for transfers between devices, along_context(): return lax.all_to_all(prefix, LINE[1], 0, 0).reshape(state.shape)  25.3 us
    all_to_all x1, blocking collectives, along_context(): pieces = lax.all_to_all(state.reshape(near_size, -1, lanes), LINE[1], 0, 0)  22.4 us
    pallas_call x6, Pallas kernels, call(): pl.pallas_call(kernel, in_specs=[SMEM] * len(small) + [place_of(item) for...  18.8 us
    all_to_all x2, blocking collectives, along_context(): totals = lax.all_to_all(scan_total(table, pieces, reverse), LINE[0], 0, 0)  17.7 us
    all_to_all x1, waiting for transfers between devices, along_context(): pieces = lax.all_to_all(state.reshape(near_size, -1, lanes), LINE[1], 0, 0)  16 us
    all_to_all x1, starting transfers between devices, along_context(): pieces = lax.all_to_all(state.reshape(near_size, -1, lanes), LINE[1], 0, 0)  15.2 us
    psum x2, blocking collectives, on_device(): sums = lax.psum(lax.psum(sums, 'core'), 'row')  13.2 us
    all_to_all x2, starting transfers between devices, along_context(): return lax.all_to_all(prefix, LINE[1], 0, 0).reshape(state.shape)  11.4 us
  transfers between devices with their start and end apart: 3, of which 3 were waited for; matrix products, arithmetic and copies ran while one was open for 0% of the time, Pallas kernels for 7%

profile of v4, /device:TPU:32, one launch (start us, length us, event | category | flops | bytes accessed | tf_op | source)
XLA Modules:
  0.0 146.4 jit_solution(15459077669389834416)
XLA Ops:
  0.6 3.2 %memory.1 = (f32[4,128,128]{2,1,0:T(8,128)}, f32[4,128,128]{2,1,0:T(8,128)S(1)}) custom-call(f32[4]{0:T(128)} %rates.7, bf16[512,512]{1,0:T(8,128)(2,1)} %keys.5, bf16[512,512]{1,0:T(8,128)(2,1)} %values.5), custom_call_target="tpu_custom_call" | custom-call | flops 400000000 | bytes 4000000 | tf_op jit(solution)/shard_map/memory/pallas_call | solution.py:317
  3.8 0.0 copy-start.6
  3.8 15.2 %all-to-all-start = ((f32[16,32,128]{2,1,0:T(8,128)}), f32[16,32,128]{2,1,0:T(8,128)S(1)}, u32[]{:S(2)}, u32[]{:S(2)}) async-start(f32[16,32,128]{2,1,0:T(8,128)} %bitcast.10), calls=%async_computation | async-start | bytes 524288 | tf_op jit(solution)/shard_map/all_to_all | solution.py:406
  19.0 0.0 copy-start.8
  19.1 0.6 copy-done.8
  19.7 0.6 dynamic_slice.4
  21.0 16.0 %all-to-all-done.piece_ref = f32[16,32,128]{2,1,0:T(8,128)S(1)} async-done(((f32[16,32,128]{2,1,0:T(8,128)}), f32[16,32,128]{2,1,0:T(8,128)S(1)}, u32[]{:S(2)}, u32[]{:S(2)}) %all-to-all-start) | async-done | bytes 262176 | tf_op jit(solution)/shard_map/all_to_all | solution.py:406
  37.0 0.6 scan_total.2
  37.5 9.7 %all_to_all.30.total_ref = f32[4,32,128]{2,1,0:T(8,128)S(1)} all-to-all(f32[4,32,128]{2,1,0:T(8,128)S(1)} %scan_total.2), channel_id=1, replica_groups=mesh['ctx_0'=4,'ctx_1'=16,'row'=4,'core'=2] {'ctx_0'}, dimensions={0} | all-to-all | bytes 131072 | tf_op jit(solution)/shard_map/all_to_all | solution.py:407
  47.3 1.3 scan_prefix.2
  48.5 6.3 %all-to-all-start.2 = ((f32[16,32,128]{2,1,0:T(8,128)}), f32[16,32,128]{2,1,0:T(8,128)S(1)}, u32[]{:S(2)}, u32[]{:S(2)}) async-start(f32[16,32,128]{2,1,0:T(8,128)} %scan_prefix.2), calls=%async_computation.2 | async-start | bytes 524288 | tf_op jit(solution)/shard_map/all_to_all | solution.py:409
  54.8 0.0 copy-start
  54.8 0.0 copy-start.1
  54.8 3.6 %inside.1 = (bf16[4,2,256,256]{3,2,1,0:T(8,128)(2,1)}, f32[512,512]{1,0:T(8,128)}, f32[8,512]{1,0:T(8,128)S(1)}) custom-call(f32[4]{0:T(128)} %rates.7, bf16[512,512]{1,0:T(8,128)(2,1)} %queries.7, bf16[512,512]{1,0:T(8,128)(2,1)} %keys.5, bf16[512,512]{1,0:T(8,128)(2,1)} %values.5, f32[1,512]{1,0:T(1,128)} %bitcast.11), custom_call_target="tpu_custom_call" | custom-call | flops 400000000 | bytes 4000000 | tf_op jit(solution)/shard_map/inside/pallas_call | solution.py:317
  58.4 14.0 %all-to-all-done.2 = f32[16,32,128]{2,1,0:T(8,128)S(1)} async-done(((f32[16,32,128]{2,1,0:T(8,128)}), f32[16,32,128]{2,1,0:T(8,128)S(1)}, u32[]{:S(2)}, u32[]{:S(2)}) %all-to-all-start.2) | async-done | bytes 262176 | tf_op jit(solution)/shard_map/all_to_all | solution.py:409
  72.5 0.0 copy-done.6
  72.5 0.0 copy-done
  72.5 0.0 copy-done.1
  72.5 1.6 %carried.1 = (f32[512,512]{1,0:T(8,128)S(1)}, f32[8,128]{1,0:T(8,128)S(1)}) custom-call(f32[8,512]{1,0:T(8,128)S(1)} %get-tuple-element.21.table, bf16[512,512]{1,0:T(8,128)(2,1)S(1)} %copy-done, f32[4,128,128]{2,1,0:T(8,128)S(1)} %bitcast.6, f32[4,128,128]{2,1,0:T(8,128)S(1)} %get-tuple-element.20.first, f32[512,512]{1,0:T(8,128)} %get-tuple-element.22.far_inside, ...), custom_call_target="tpu_custom_call" | custom-call | flops 400000000 | bytes 4000000 | tf_op jit(solution)/shard_map/carried/pallas_call | solution.py:317
  74.1 0.0 copy-start.4
  74.2 2.5 %psum.14 = f32[8,128]{1,0:T(8,128)S(1)} all-reduce(f32[8,128]{1,0:T(8,128)S(1)} %get-tuple-element.23), channel_id=1, replica_groups=mesh['ctx_0'=4,'ctx_1'=16,'row'=4,'core'=2] {'core'}, use_global_device_ids=true, to_apply=%region_0.1 | all-reduce | flops 1024 | bytes 8192 | tf_op jit(solution)/shard_map/psum | solution.py:459
  76.6 10.7 %psum.15.sums = f32[8,128]{1,0:T(8,128)S(1)} all-reduce(f32[8,128]{1,0:T(8,128)S(1)} %psum.14), channel_id=1, replica_groups=mesh['ctx_0'=4,'ctx_1'=16,'row'=4,'core'=2] {'row'}, use_global_device_ids=true, to_apply=%region_1.2 | all-reduce | flops 1024 | bytes 8192 | tf_op jit(solution)/shard_map/psum | solution.py:459
  87.3 1.0 grad.1
  88.3 0.0 copy-done.4
  88.4 0.0 copy-start.5
  88.4 22.4 %all_to_all.31.piece_ref = f32[16,32,128]{2,1,0:T(8,128)S(1)} all-to-all(f32[16,32,128]{2,1,0:T(8,128)S(1)} %bitcast.8), channel_id=1, replica_groups=mesh['ctx_0'=4,'ctx_1'=16,'row'=4,'core'=2] {'ctx_1'}, dimensions={0} | all-to-all | bytes 524288 | tf_op jit(solution)/shard_map/all_to_all | solution.py:406
  110.7 0.6 scan_total.3
  111.3 8.0 %all_to_all.32.total_ref = f32[4,32,128]{2,1,0:T(8,128)S(1)} all-to-all(f32[4,32,128]{2,1,0:T(8,128)S(1)} %scan_total.3), channel_id=1, replica_groups=mesh['ctx_0'=4,'ctx_1'=16,'row'=4,'core'=2] {'ctx_0'}, dimensions={0} | all-to-all | bytes 131072 | tf_op jit(solution)/shard_map/all_to_all | solution.py:407
  119.3 1.3 scan_prefix.3
  120.6 0.0 copy-start.7
  120.6 5.2 %all-to-all-start.5 = ((f32[16,32,128]{2,1,0:T(8,128)}), f32[16,32,128]{2,1,0:T(8,128)S(1)}, u32[]{:S(2)}, u32[]{:S(2)}) async-start(f32[16,32,128]{2,1,0:T(8,128)} %scan_prefix.3), calls=%async_computation.5 | async-start | bytes 524288 | tf_op jit(solution)/shard_map/all_to_all | solution.py:409
  125.8 0.0 copy-done.5
  125.8 0.0 copy-done.7
  125.8 0.0 copy-start.2
  125.8 0.0 copy-start.3
  125.8 6.0 %local.1 = (bf16[512,512]{1,0:T(8,128)(2,1)}, bf16[512,512]{1,0:T(8,128)(2,1)}, f32[512,512]{1,0:T(8,128)}, f32[512,512]{1,0:T(8,128)}, f32[4,128,128]{2,1,0:T(8,128)S(1)}) custom-call(f32[4]{0:T(128)} %rates.7, bf16[512,512]{1,0:T(8,128)(2,1)} %queries.7, bf16[512,512]{1,0:T(8,128)(2,1)} %keys.5, bf16[512,512]{1,0:T(8,128)(2,1)} %values.5, ...), custom_call_target="tpu_custom_call" | custom-call | flops 400000000 | bytes 4000000 | tf_op jit(solution)/shard_map/local/pallas_call | solution.py:317
  131.8 11.2 %all-to-all-done.5 = f32[16,32,128]{2,1,0:T(8,128)S(1)} async-done(((f32[16,32,128]{2,1,0:T(8,128)}), f32[16,32,128]{2,1,0:T(8,128)S(1)}, u32[]{:S(2)}, u32[]{:S(2)}) %all-to-all-start.5) | async-done | bytes 262176 | tf_op jit(solution)/shard_map/all_to_all | solution.py:409
  143.0 0.0 copy-done.2
  143.0 0.0 copy-done.3
  143.1 3.3 %finish.1 = (bf16[512,512]{1,0:T(8,128)(2,1)}, bf16[512,512]{1,0:T(8,128)(2,1)}) custom-call(f32[4]{0:T(128)} %rates.7, bf16[512,512]{1,0:T(8,128)(2,1)S(1)} %copy-done.2, bf16[512,512]{1,0:T(8,128)(2,1)S(1)} %copy-done.3, f32[512,512]{1,0:T(8,128)} %get-tuple-element.27.far_key_part, f32[512,512]{1,0:T(8,128)} %get-tuple-element.28.far_value_part, ...), custom_call_target="tpu_custom_call" | custom-call | flops 400000000 | bytes 4000000 | tf_op jit(solution)/shard_map/finish/pallas_call | solution.py:317
  (1 shorter events, 0.0 us)
Async XLA Ops:
  3.8 68.7 %copy-start.6 = (f32[4,128,128]{2,1,0:T(8,128)}, f32[4,128,128]{2,1,0:T(8,128)S(1)}, u32[]{:S(2)}) copy-start(f32[4,128,128]{2,1,0:T(8,128)S(1)} %get-tuple-element.20.first) | copy-start | bytes 786436
  3.8 33.1 %all-to-all-start = ((f32[16,32,128]{2,1,0:T(8,128)}), f32[16,32,128]{2,1,0:T(8,128)S(1)}, u32[]{:S(2)}, u32[]{:S(2)}) async-start(f32[16,32,128]{2,1,0:T(8,128)} %bitcast.10), calls=%async_computation | async-start | bytes 524288 | tf_op jit(solution)/shard_map/all_to_all | solution.py:406
  19.0 0.7 copy-start.8
  48.5 23.9 %all-to-all-start.2 = ((f32[16,32,128]{2,1,0:T(8,128)}), f32[16,32,128]{2,1,0:T(8,128)S(1)}, u32[]{:S(2)}, u32[]{:S(2)}) async-start(f32[16,32,128]{2,1,0:T(8,128)} %scan_prefix.2), calls=%async_computation.2 | async-start | bytes 524288 | tf_op jit(solution)/shard_map/all_to_all | solution.py:409
  54.8 17.7 %copy-start = (bf16[512,512]{1,0:T(8,128)(2,1)S(1)}, bf16[512,512]{1,0:T(8,128)(2,1)}, u32[]{:S(2)}) copy-start(bf16[512,512]{1,0:T(8,128)(2,1)} %queries.7) | copy-start | bytes 1572868
  54.8 17.7 %copy-start.1 = (bf16[512,512]{1,0:T(8,128)(2,1)S(1)}, bf16[512,512]{1,0:T(8,128)(2,1)}, u32[]{:S(2)}) copy-start(bf16[512,512]{1,0:T(8,128)(2,1)} %out_grad.5) | copy-start | bytes 1572868
  74.1 14.2 %copy-start.4 = (f32[512,512]{1,0:T(8,128)}, f32[512,512]{1,0:T(8,128)S(1)}, u32[]{:S(2)}) copy-start(f32[512,512]{1,0:T(8,128)S(1)} %get-tuple-element.24.attention) | copy-start | bytes 3145732
  88.4 37.4 %copy-start.5 = (f32[512,512]{1,0:T(8,128)S(1)}, f32[512,512]{1,0:T(8,128)}, u32[]{:S(2)}) copy-start(f32[512,512]{1,0:T(8,128)} %copy-done.4) | copy-start | bytes 3145732
  120.6 5.2 %copy-start.7 = (f32[4,128,128]{2,1,0:T(8,128)S(1)}, f32[4,128,128]{2,1,0:T(8,128)}, u32[]{:S(2)}) copy-start(f32[4,128,128]{2,1,0:T(8,128)} %copy-done.6) | copy-start | bytes 786436
  120.6 22.4 %all-to-all-start.5 = ((f32[16,32,128]{2,1,0:T(8,128)}), f32[16,32,128]{2,1,0:T(8,128)S(1)}, u32[]{:S(2)}, u32[]{:S(2)}) async-start(f32[16,32,128]{2,1,0:T(8,128)} %scan_prefix.3), calls=%async_computation.5 | async-start | bytes 524288 | tf_op jit(solution)/shard_map/all_to_all | solution.py:409
  125.8 17.3 %copy-start.2 = (bf16[512,512]{1,0:T(8,128)(2,1)S(1)}, bf16[512,512]{1,0:T(8,128)(2,1)}, u32[]{:S(2)}) copy-start(bf16[512,512]{1,0:T(8,128)(2,1)} %keys.5) | copy-start | bytes 1572868
  125.8 17.3 %copy-start.3 = (bf16[512,512]{1,0:T(8,128)(2,1)S(1)}, bf16[512,512]{1,0:T(8,128)(2,1)}, u32[]{:S(2)}) copy-start(bf16[512,512]{1,0:T(8,128)(2,1)} %values.5) | copy-start | bytes 1572868

commit v5 on v4

--- a/solution.py
+++ b/solution.py
@@ -84,7 +84,10 @@
         copy.wait()
 
 
-def memory_kernel(rates, far_keys, far_values, end, first, keys, values, ready):
+def memory_kernel(
+    rates, far_keys, far_values, far_end, first, keys, values, end, ready, done
+):
+    stores = []
     loads = []
     for block in range(2):
         rows = block_rows(block)
@@ -105,6 +108,10 @@
             else:
                 full = jnp.exp(jnp.full((128, 128), -BLOCK * rates[head], F32))
                 end[head] = full * first[head] + update
+                store = pltpu.make_async_copy(end.at[head], far_end.at[head], done.at[head])
+                store.start()
+                stores.append(store)
+    wait_all(stores)
 
 
 def rate_row(table, head):
@@ -287,10 +294,15 @@
             key_more[:, cols] = dot_wide_right(values[rows, cols], backlog, 1, 1) * ending
             value_more[:, cols] = dot_wide_right(keys[rows, cols], backlog, 1, 0) * ending
         wait_all(loads[block])
-        key_grad[rows, :] = (key_part[rows, :] + key_more[...]).astype(BF16)
-        value_grad[rows, :] = (value_part[rows, :] + value_more[...]).astype(BF16)
-        pairs = ((key_grad, far_key_grad), (value_grad, far_value_grad))
-        stores += start_copies([(n.at[rows, :], f.at[rows, :]) for n, f in pairs], done.at[block])
+        for half in range(4):
+            span = slice(block * BLOCK + half * 64, block * BLOCK + half * 64 + 64)
+            own = slice(half * 64, half * 64 + 64)
+            key_grad[span, :] = (key_part[span, :] + key_more[own, :]).astype(BF16)
+            value_grad[span, :] = (value_part[span, :] + value_more[own, :]).astype(BF16)
+            pairs = ((key_grad, far_key_grad), (value_grad, far_value_grad))
+            stores += start_copies(
+                [(n.at[span, :], f.at[span, :]) for n, f in pairs], done.at[4 * block + half]
+            )
     wait_all(stores)
 
 
@@ -328,10 +340,10 @@
     )(*small, *map(bare, operands))
 
 
-def scan_total(table, pieces, reverse):
+def scan_total(table, pieces, reverse, filled):
     count, rows, lanes = pieces.shape
 
-    def kernel(table_ref, piece_ref, total_ref):
+    def kernel(table_ref, piece_ref, _, total_ref):
         order = range(count - 1, -1, -1) if reverse else range(count)
         running = None
         for k in order:
@@ -342,44 +354,33 @@
 
     return pl.pallas_call(
         kernel,
-        in_specs=[SMEM, VMEM],
+        in_specs=[SMEM, VMEM, VMEM],
         out_specs=VMEM,
         out_shape=pltpu.VMEM((lax.axis_size(LINE[0]), rows, lanes), F32),
         name="scan_total",
         compiler_params=pltpu.CompilerParams(vmem_limit_bytes=GRANT),
-    )(table, near(pieces))
+    )(table, near(pieces), near(filled))
 
 
 def scan_prefix(table, pieces, totals, reverse):
     count, rows, lanes = pieces.shape
     first = 5 if reverse else 1
-    stride = count // 4
-
-    def kernel(table_ref, piece_ref, total_ref, far_ref, prefix_ref, done):
+
+    def kernel(table_ref, piece_ref, total_ref, prefix_ref):
+        order = list(range(count - 1, -1, -1) if reverse else range(count))
         running = total_ref[0] * table_ref[first]
         for peer in range(1, total_ref.shape[0]):
             running = running + total_ref[peer] * table_ref[first + peer]
-        stores = []
-        for part in range(4):
-            order = range(part * stride, (part + 1) * stride)
-            for step in order:
-                k = count - 1 - step if reverse else step
-                prefix_ref[k] = running
-                if step != count - 1:
-                    running = running * table_ref[0] + piece_ref[k]
-            low = count - (part + 1) * stride if reverse else part * stride
-            span = slice(low, low + stride)
-            store = pltpu.make_async_copy(prefix_ref.at[span], far_ref.at[span], done.at[part])
-            store.start()
-            stores.append(store)
-        wait_all(stores)
+        for k in order:
+            prefix_ref[k] = running
+            if k != order[-1]:
+                running = running * table_ref[0] + piece_ref[k]
 
     return pl.pallas_call(
         kernel,
         in_specs=[SMEM, VMEM, VMEM],
-        out_specs=pl.BlockSpec(memory_space=pltpu.HBM),
-        out_shape=shape(count, rows, lanes),
-        scratch_shapes=(pltpu.VMEM((count, rows, lanes), F32), pltpu.SemaphoreType.DMA((4,))),
+        out_specs=VMEM,
+        out_shape=pltpu.VMEM((count, rows, lanes), F32),
         name="scan_prefix",
         compiler_params=pltpu.CompilerParams(vmem_limit_bytes=GRANT),
     )(table, near(pieces), near(totals))
@@ -400,11 +401,11 @@
     return jnp.where(steps >= 0, weights, 0.0)
 
 
-def along_context(table, state, reverse):
+def along_context(table, state, reverse, filled):
     near_size, far_size = lax.axis_size(LINE[1]), lax.axis_size(LINE[0])
     lanes = state.shape[-1]
     pieces = lax.all_to_all(state.reshape(near_size, -1, lanes), LINE[1], 0, 0)
-    totals = lax.all_to_all(scan_total(table, pieces, reverse), LINE[0], 0, 0)
+    totals = lax.all_to_all(scan_total(table, pieces, reverse, filled), LINE[0], 0, 0)
     prefix = scan_prefix(table, pieces, totals, reverse)
     return lax.all_to_all(prefix, LINE[1], 0, 0).reshape(state.shape)
 
@@ -424,12 +425,12 @@
     memory_end, memory_first = call(
         memory_kernel,
         "memory",
-        (Streamed(state), state_near),
+        (Far(state), state_near),
         Far(key_rows),
         Far(value_rows),
         grant=None,
         rates=decay_rates,
-        scratch=(narrow_near, narrow_near, flags),
+        scratch=(narrow_near, narrow_near, state_near, flags, pltpu.SemaphoreType.DMA((4,))),
     )
     probs, inside, aux = call(
         inside_kernel,
@@ -442,7 +443,7 @@
         grant=None,
         rates=decay_rates,
     )
-    entering = along_context(table, memory_end, False)
+    entering = along_context(table, memory_end, False, aux)
     attention, sums = call(
         carried_kernel,
         "carried",
@@ -484,7 +485,7 @@
         grant=None,
         rates=decay_rates,
     )
-    after = along_context(table, backlog_end, True)
+    after = along_context(table, backlog_end, True, backlog_second)
     more = pltpu.VMEM((BLOCK, width), F32)
     key_grad, value_grad = call(
         finish_kernel,
@@ -498,7 +499,7 @@
         near(backlog_second),
         grant=None,
         rates=decay_rates,
-        scratch=(wide_near, wide_near, more, more, narrow_near, narrow_near, flags, flags),
+        scratch=(wide_near, wide_near, more, more, narrow_near, narrow_near, flags, pltpu.SemaphoreType.DMA((8, 2))),
     )
     return (normed_out, query_grad, key_grad, value_grad)
 

time: 147 us -> 146 us (level)
  blocking collectives: 53.2 us -> 76.7 us
  waiting for transfers between devices: 41.3 us -> 22.8 us
  starting transfers between devices: 26.7 us -> 20.2 us
    all_to_all x2 -> x0, waiting for transfers between devices: 25.3 us -> none  [along_context(): return lax.all_to_all(prefix, LINE[1], 0, 0).reshape(state.shape)]
    all_to_all x3 -> x4, blocking collectives: 40 us -> 63.5 us  [the longest x2 45.8 us: along_context(): return lax.all_to_all(prefix, LINE[1], 0, 0).reshape(state.shape)]
    all_to_all x2 -> x0, starting transfers between devices: 11.4 us -> none  [along_context(): return lax.all_to_all(prefix, LINE[1], 0, 0).reshape(state.shape)]
    all_to_all x1 -> x2, waiting for transfers between devices: 16 us -> 22.8 us  [along_context(): pieces = lax.all_to_all(state.reshape(near_size, -1, lanes), LINE[1], 0, 0)]
    all_to_all x1 -> x2, starting transfers between devices: 15.2 us -> 20.2 us  [along_context(): pieces = lax.all_to_all(state.reshape(near_size, -1, lanes), LINE[1], 0, 0)]
  transfers between devices with their start and end apart: 3 -> 2, of which waited for: 3 -> 2; matrix products, arithmetic and copies ran while one was open for 0% -> 0% of each run, Pallas kernels for 7% -> 7%
where the time goes in v5:
time: 146 us; the launch traced here: 145 us
  blocking collectives  76.7 us (53%)
  waiting for transfers between devices  22.8 us (16%)
  Pallas kernels  21.7 us (15%)
  starting transfers between devices  20.2 us (14%)
  local copies, waits for them, and re-layouts  2.47 us (2%)
    all_to_all x2, blocking collectives, along_context(): return lax.all_to_all(prefix, LINE[1], 0, 0).reshape(state.shape)  45.8 us
    all_to_all x2, waiting for transfers between devices, along_context(): pieces = lax.all_to_all(state.reshape(near_size, -1, lanes), LINE[1], 0, 0)  22.8 us
    all_to_all x2, starting transfers between devices, along_context(): pieces = lax.all_to_all(state.reshape(near_size, -1, lanes), LINE[1], 0, 0)  20.2 us
    pallas_call x6, Pallas kernels, call(): pl.pallas_call(kernel, in_specs=[SMEM] * len(small) + [place_of(item) for...  19.3 us
    all_to_all x2, blocking collectives, along_context(): lax.all_to_all(scan_total(table, pieces, reverse, filled), LINE[0], 0, 0)  17.7 us
    psum x2, blocking collectives, on_device(): sums = lax.psum(lax.psum(sums, 'core'), 'row')  13.2 us
  transfers between devices with their start and end apart: 2, of which 2 were waited for; matrix products, arithmetic and copies ran while one was open for 0% of the time, Pallas kernels for 7%

profile of v5, /device:TPU:32, one launch (start us, length us, event | category | flops | bytes accessed | tf_op | source)
XLA Modules:
  0.0 145.2 jit_solution(1665563697933158525)
XLA Ops:
  0.6 3.1 %memory.1 = (f32[4,128,128]{2,1,0:T(8,128)}, f32[4,128,128]{2,1,0:T(8,128)S(1)}) custom-call(f32[4]{0:T(128)} %rates.7, bf16[512,512]{1,0:T(8,128)(2,1)} %keys.5, bf16[512,512]{1,0:T(8,128)(2,1)} %values.5), custom_call_target="tpu_custom_call" | custom-call | flops 400000000 | bytes 4000000 | tf_op jit(solution)/shard_map/memory/pallas_call | solution.py:329
  3.8 15.2 %all-to-all-start = ((f32[16,32,128]{2,1,0:T(8,128)}), f32[16,32,128]{2,1,0:T(8,128)S(1)}, u32[]{:S(2)}, u32[]{:S(2)}) async-start(f32[16,32,128]{2,1,0:T(8,128)} %bitcast.9), calls=%async_computation | async-start | bytes 524288 | tf_op jit(solution)/shard_map/all_to_all | solution.py:407
  19.0 0.0 copy-start.6
  19.0 0.6 copy-done.6
  19.6 0.6 dynamic_slice.4
  20.9 3.5 %inside.1 = (bf16[4,2,256,256]{3,2,1,0:T(8,128)(2,1)}, f32[512,512]{1,0:T(8,128)}, f32[8,512]{1,0:T(8,128)S(1)}) custom-call(f32[4]{0:T(128)} %rates.7, bf16[512,512]{1,0:T(8,128)(2,1)} %queries.7, bf16[512,512]{1,0:T(8,128)(2,1)} %keys.5, bf16[512,512]{1,0:T(8,128)(2,1)} %values.5, f32[1,512]{1,0:T(1,128)} %bitcast.10), custom_call_target="tpu_custom_call" | custom-call | flops 400000000 | bytes 4000000 | tf_op jit(solution)/shard_map/inside/pallas_call | solution.py:329
  24.4 12.5 %all-to-all-done.piece_ref = f32[16,32,128]{2,1,0:T(8,128)S(1)} async-done(((f32[16,32,128]{2,1,0:T(8,128)}), f32[16,32,128]{2,1,0:T(8,128)S(1)}, u32[]{:S(2)}, u32[]{:S(2)}) %all-to-all-start) | async-done | bytes 262176 | tf_op jit(solution)/shard_map/all_to_all | solution.py:407
  36.9 0.6 scan_total.2
  37.5 9.7 %all_to_all.30.total_ref = f32[4,32,128]{2,1,0:T(8,128)S(1)} all-to-all(f32[4,32,128]{2,1,0:T(8,128)S(1)} %scan_total.2), channel_id=1, replica_groups=mesh['ctx_0'=4,'ctx_1'=16,'row'=4,'core'=2] {'ctx_0'}, dimensions={0} | all-to-all | bytes 131072 | tf_op jit(solution)/shard_map/all_to_all | solution.py:408
  47.2 0.0 copy-start
  47.2 0.0 copy-start.1
  47.2 0.6 scan_prefix.2
  47.8 23.7 %all_to_all.31 = f32[16,32,128]{2,1,0:T(8,128)S(1)} all-to-all(f32[16,32,128]{2,1,0:T(8,128)S(1)} %scan_prefix.2), channel_id=1, replica_groups=mesh['ctx_0'=4,'ctx_1'=16,'row'=4,'core'=2] {'ctx_1'}, dimensions={0} | all-to-all | bytes 524288 | tf_op jit(solution)/shard_map/all_to_all | solution.py:410
  71.5 0.0 copy-done
  71.5 0.0 copy-done.1
  71.5 1.6 %carried.1 = (f32[512,512]{1,0:T(8,128)S(1)}, f32[8,128]{1,0:T(8,128)S(1)}) custom-call(f32[8,512]{1,0:T(8,128)S(1)} %get-tuple-element.20._.table, bf16[512,512]{1,0:T(8,128)(2,1)S(1)} %copy-done, f32[4,128,128]{2,1,0:T(8,128)S(1)} %bitcast.6, f32[4,128,128]{2,1,0:T(8,128)S(1)} %get-tuple-element.21.first, f32[512,512]{1,0:T(8,128)} %get-tuple-element.22.far_inside, ...), custom_call_target="tpu_custom_call" | custom-call | flops 400000000 | bytes 4000000 | tf_op jit(solution)/shard_map/carried/pallas_call | solution.py:329
  73.2 0.0 copy-start.4
  73.2 2.5 %psum.14 = f32[8,128]{1,0:T(8,128)S(1)} all-reduce(f32[8,128]{1,0:T(8,128)S(1)} %get-tuple-element.23), channel_id=1, replica_groups=mesh['ctx_0'=4,'ctx_1'=16,'row'=4,'core'=2] {'core'}, use_global_device_ids=true, to_apply=%region_0.1 | all-reduce | flops 1024 | bytes 8192 | tf_op jit(solution)/shard_map/psum | solution.py:460
  75.7 10.7 %psum.15.sums = f32[8,128]{1,0:T(8,128)S(1)} all-reduce(f32[8,128]{1,0:T(8,128)S(1)} %psum.14), channel_id=1, replica_groups=mesh['ctx_0'=4,'ctx_1'=16,'row'=4,'core'=2] {'row'}, use_global_device_ids=true, to_apply=%region_1.2 | all-reduce | flops 1024 | bytes 8192 | tf_op jit(solution)/shard_map/psum | solution.py:460
  86.4 1.7 %grad.1 = f32[4,128,128]{2,1,0:T(8,128)} custom-call(f32[8,512]{1,0:T(8,128)S(1)} %get-tuple-element.20._.table, f32[8,128]{1,0:T(8,128)S(1)} %psum.15.sums, bf16[512,512]{1,0:T(8,128)(2,1)S(1)} %copy-done, f32[512,512]{1,0:T(8,128)S(1)} %get-tuple-element.24.attention, bf16[512,512]{1,0:T(8,128)(2,1)S(1)} %copy-done.1), custom_call_target="tpu_custom_call" | custom-call | flops 400000000 | bytes 4000000 | tf_op jit(solution)/shard_map/grad/pallas_call | solution.py:329
  88.1 0.0 copy-done.4
  88.1 5.0 %all-to-all-start.3 = ((f32[16,32,128]{2,1,0:T(8,128)}), f32[16,32,128]{2,1,0:T(8,128)S(1)}, u32[]{:S(2)}, u32[]{:S(2)}) async-start(f32[16,32,128]{2,1,0:T(8,128)} %bitcast.4), calls=%async_computation.3 | async-start | bytes 524288 | tf_op jit(solution)/shard_map/all_to_all | solution.py:407
  93.1 0.0 copy-start.5
  93.1 1.2 copy-done.5
  94.3 5.9 %local.1 = (bf16[512,512]{1,0:T(8,128)(2,1)}, bf16[512,512]{1,0:T(8,128)(2,1)}, f32[512,512]{1,0:T(8,128)}, f32[512,512]{1,0:T(8,128)}, f32[4,128,128]{2,1,0:T(8,128)S(1)}) custom-call(f32[4]{0:T(128)} %rates.7, bf16[512,512]{1,0:T(8,128)(2,1)} %queries.7, bf16[512,512]{1,0:T(8,128)(2,1)} %keys.5, bf16[512,512]{1,0:T(8,128)(2,1)} %values.5, ...), custom_call_target="tpu_custom_call" | custom-call | flops 400000000 | bytes 4000000 | tf_op jit(solution)/shard_map/local/pallas_call | solution.py:329
  100.2 10.3 %all-to-all-done.3.piece_ref = f32[16,32,128]{2,1,0:T(8,128)S(1)} async-done(((f32[16,32,128]{2,1,0:T(8,128)}), f32[16,32,128]{2,1,0:T(8,128)S(1)}, u32[]{:S(2)}, u32[]{:S(2)}) %all-to-all-start.3) | async-done | bytes 262176 | tf_op jit(solution)/shard_map/all_to_all | solution.py:407
  110.5 0.6 scan_total.3
  111.1 8.0 %all_to_all.32.total_ref = f32[4,32,128]{2,1,0:T(8,128)S(1)} all-to-all(f32[4,32,128]{2,1,0:T(8,128)S(1)} %scan_total.3), channel_id=1, replica_groups=mesh['ctx_0'=4,'ctx_1'=16,'row'=4,'core'=2] {'ctx_0'}, dimensions={0} | all-to-all | bytes 131072 | tf_op jit(solution)/shard_map/all_to_all | solution.py:408
  119.1 0.0 copy-start.2
  119.1 0.0 copy-start.3
  119.1 0.6 scan_prefix.3
  119.7 22.1 %all_to_all.33 = f32[16,32,128]{2,1,0:T(8,128)S(1)} all-to-all(f32[16,32,128]{2,1,0:T(8,128)S(1)} %scan_prefix.3), channel_id=1, replica_groups=mesh['ctx_0'=4,'ctx_1'=16,'row'=4,'core'=2] {'ctx_1'}, dimensions={0} | all-to-all | bytes 524288 | tf_op jit(solution)/shard_map/all_to_all | solution.py:410
  141.8 0.0 copy-done.2
  141.8 0.0 copy-done.3
  141.8 3.4 %finish.1 = (bf16[512,512]{1,0:T(8,128)(2,1)}, bf16[512,512]{1,0:T(8,128)(2,1)}) custom-call(f32[4]{0:T(128)} %rates.7, bf16[512,512]{1,0:T(8,128)(2,1)S(1)} %copy-done.2, bf16[512,512]{1,0:T(8,128)(2,1)S(1)} %copy-done.3, f32[512,512]{1,0:T(8,128)} %get-tuple-element.27.far_key_part, f32[512,512]{1,0:T(8,128)} %get-tuple-element.28.far_value_part, ...), custom_call_target="tpu_custom_call" | custom-call | flops 400000000 | bytes 4000000 | tf_op jit(solution)/shard_map/finish/pallas_call | solution.py:329
  (1 shorter events, 0.0 us)
Async XLA Ops:
  3.8 33.1 %all-to-all-start = ((f32[16,32,128]{2,1,0:T(8,128)}), f32[16,32,128]{2,1,0:T(8,128)S(1)}, u32[]{:S(2)}, u32[]{:S(2)}) async-start(f32[16,32,128]{2,1,0:T(8,128)} %bitcast.9), calls=%async_computation | async-start | bytes 524288 | tf_op jit(solution)/shard_map/all_to_all | solution.py:407
  19.0 0.7 copy-start.6
  47.2 24.3 %copy-start = (bf16[512,512]{1,0:T(8,128)(2,1)S(1)}, bf16[512,512]{1,0:T(8,128)(2,1)}, u32[]{:S(2)}) copy-start(bf16[512,512]{1,0:T(8,128)(2,1)} %queries.7) | copy-start | bytes 1572868
  47.2 24.3 %copy-start.1 = (bf16[512,512]{1,0:T(8,128)(2,1)S(1)}, bf16[512,512]{1,0:T(8,128)(2,1)}, u32[]{:S(2)}) copy-start(bf16[512,512]{1,0:T(8,128)(2,1)} %out_grad.5) | copy-start | bytes 1572868
  73.2 14.9 %copy-start.4 = (f32[512,512]{1,0:T(8,128)}, f32[512,512]{1,0:T(8,128)S(1)}, u32[]{:S(2)}) copy-start(f32[512,512]{1,0:T(8,128)S(1)} %get-tuple-element.24.attention) | copy-start | bytes 3145732
  88.1 22.4 %all-to-all-start.3 = ((f32[16,32,128]{2,1,0:T(8,128)}), f32[16,32,128]{2,1,0:T(8,128)S(1)}, u32[]{:S(2)}, u32[]{:S(2)}) async-start(f32[16,32,128]{2,1,0:T(8,128)} %bitcast.4), calls=%async_computation.3 | async-start | bytes 524288 | tf_op jit(solution)/shard_map/all_to_all | solution.py:407
  93.1 1.2 copy-start.5
  119.1 22.7 %copy-start.2 = (bf16[512,512]{1,0:T(8,128)(2,1)S(1)}, bf16[512,512]{1,0:T(8,128)(2,1)}, u32[]{:S(2)}) copy-start(bf16[512,512]{1,0:T(8,128)(2,1)} %keys.5) | copy-start | bytes 1572868
  119.1 22.7 %copy-start.3 = (bf16[512,512]{1,0:T(8,128)(2,1)S(1)}, bf16[512,512]{1,0:T(8,128)(2,1)}, u32[]{:S(2)}) copy-start(bf16[512,512]{1,0:T(8,128)(2,1)} %values.5) | copy-start | bytes 1572868

commit v6 on v5

--- a/solution.py
+++ b/solution.py
@@ -169,7 +169,9 @@
             for tile in range(2):
                 turned = part[tile * 128 : (tile + 1) * 128, :].T
                 flat.append(jnp.sum(turned, axis=0, keepdims=True))
-    sums[...] = jnp.concatenate(squares + products, axis=0)
+    both = jnp.concatenate(squares + products, axis=0)
+    for peer in range(sums.shape[0]):
+        sums[peer] = both
 
 
 def per_token(row):
@@ -177,8 +179,11 @@
 
 
 def scales_of(features, sums, block):
-    scale = lax.rsqrt(sums[0:4] / features + EPSILON)
-    coeff = scale * sums[4:8] / features
+    total = sums[0]
+    for peer in range(1, sums.shape[0]):
+        total = total + sums[peer]
+    scale = lax.rsqrt(total[0:4] / features + EPSILON)
+    coeff = scale * total[4:8] / features
     tiles = (2 * block, 2 * block + 1)
     return tuple(
         jnp.concatenate([per_token(part[tile : tile + 1]) for tile in tiles], axis=0)
@@ -192,7 +197,10 @@
     return normed, (scale * (grad - normed * coeff)).astype(BF16)
 
 
-def grad_kernel(features, table, sums, queries, attention, out_grad, end):
+def grad_kernel(
+    features, table, sums, queries, attention, out_grad, far_end, end, done
+):
+    stores = []
     from_start = rows_of((BLOCK, 128))
     for block in (1, 0):
         rows = block_rows(block)
@@ -208,6 +216,10 @@
                 end[head] = gathered
             else:
                 end[head] = jnp.exp(-BLOCK * rate_row(table, head)) * end[head] + gathered
+                store = pltpu.make_async_copy(end.at[head], far_end.at[head], done.at[head])
+                store.start()
+                stores.append(store)
+    wait_all(stores)
 
 
 def local_kernel(
@@ -447,7 +459,7 @@
     attention, sums = call(
         carried_kernel,
         "carried",
-        (wide_near, pltpu.VMEM((8, 128), F32)),
+        (wide_near, pltpu.VMEM((lax.axis_size(SIDE), 8, 128), F32)),
         near(aux),
         near(queries),
         near(entering),
@@ -457,16 +469,18 @@
         grant=None,
         scratch=(wide_near, pltpu.SemaphoreType.DMA((2,))),
     )
-    sums = lax.psum(lax.psum(sums, "core"), "row")
+    sums = lax.all_to_all(sums, SIDE, 0, 0)
     (backlog_end,) = call(
         functools.partial(grad_kernel, features),
         "grad",
-        (state_near,),
+        (Far(state),),
         near(aux),
         near(sums),
         near(queries),
         near(attention),
         near(out_grad),
+        grant=None,
+        scratch=(state_near, pltpu.SemaphoreType.DMA((4,))),
     )
     query_grad, normed_out, key_part, value_part, backlog_second = call(
         functools.partial(local_kernel, features),

time: 146 us -> 144 us (0.986)
  blocking collectives: 76.7 us -> 75 us
    psum x2 -> x0, blocking collectives: 13.2 us -> none  [on_device(): sums = lax.psum(lax.psum(sums, 'core'), 'row')]
    all_to_all x0 -> x1, blocking collectives: none -> 9.71 us  [on_device(): sums = lax.all_to_all(sums, SIDE, 0, 0)]
    all_to_all x2, blocking collectives: 45.8 us -> 47.6 us  [along_context(): return lax.all_to_all(prefix, LINE[1], 0, 0).reshape(state.shape)]
where the time goes in v6:
time: 144 us
  blocking collectives  75 us (52%)
  waiting for transfers between devices  22.9 us (16%)
  Pallas kernels  21.5 us (15%)
  starting transfers between devices  20.2 us (14%)
  local copies, waits for them, and re-layouts  2.47 us (2%)
    all_to_all x2, blocking collectives, along_context(): return lax.all_to_all(prefix, LINE[1], 0, 0).reshape(state.shape)  47.6 us
    all_to_all x2, waiting for transfers between devices, along_context(): pieces = lax.all_to_all(state.reshape(near_size, -1, lanes), LINE[1], 0, 0)  22.9 us
    all_to_all x2, starting transfers between devices, along_context(): pieces = lax.all_to_all(state.reshape(near_size, -1, lanes), LINE[1], 0, 0)  20.2 us
    pallas_call x6, Pallas kernels, call(): pl.pallas_call(kernel, in_specs=[SMEM] * len(small) + [place_of(item) for...  19.2 us
    all_to_all x2, blocking collectives, along_context(): lax.all_to_all(scan_total(table, pieces, reverse, filled), LINE[0], 0, 0)  17.7 us
    all_to_all x1, blocking collectives, on_device(): sums = lax.all_to_all(sums, SIDE, 0, 0)  9.71 us
  transfers between devices with their start and end apart: 2, of which 2 were waited for; matrix products, arithmetic and copies ran while one was open for 0% of the time, Pallas kernels for 7%

profile of v6, /device:TPU:32, one launch (start us, length us, event | category | flops | bytes accessed | tf_op | source)
XLA Modules:
  0.0 143.6 jit_solution(11485557923384169882)
XLA Ops:
  0.6 3.1 %memory.1 = (f32[4,128,128]{2,1,0:T(8,128)}, f32[4,128,128]{2,1,0:T(8,128)S(1)}) custom-call(f32[4]{0:T(128)} %rates.7, bf16[512,512]{1,0:T(8,128)(2,1)} %keys.5, bf16[512,512]{1,0:T(8,128)(2,1)} %values.5), custom_call_target="tpu_custom_call" | custom-call | flops 400000000 | bytes 4000000 | tf_op jit(solution)/shard_map/memory/pallas_call | solution.py:341
  3.8 15.2 %all-to-all-start = ((f32[16,32,128]{2,1,0:T(8,128)}), f32[16,32,128]{2,1,0:T(8,128)S(1)}, u32[]{:S(2)}, u32[]{:S(2)}) async-start(f32[16,32,128]{2,1,0:T(8,128)} %bitcast.10), calls=%async_computation | async-start | bytes 524288 | tf_op jit(solution)/shard_map/all_to_all | solution.py:419
  19.0 0.0 copy-start.6
  19.0 0.6 copy-done.6
  19.6 0.6 dynamic_slice.4
  20.9 3.5 %inside.1 = (bf16[4,2,256,256]{3,2,1,0:T(8,128)(2,1)}, f32[512,512]{1,0:T(8,128)}, f32[8,512]{1,0:T(8,128)S(1)}) custom-call(f32[4]{0:T(128)} %rates.7, bf16[512,512]{1,0:T(8,128)(2,1)} %queries.7, bf16[512,512]{1,0:T(8,128)(2,1)} %keys.5, bf16[512,512]{1,0:T(8,128)(2,1)} %values.5, f32[1,512]{1,0:T(1,128)} %bitcast.11), custom_call_target="tpu_custom_call" | custom-call | flops 400000000 | bytes 4000000 | tf_op jit(solution)/shard_map/inside/pallas_call | solution.py:341
  24.4 12.5 %all-to-all-done.piece_ref = f32[16,32,128]{2,1,0:T(8,128)S(1)} async-done(((f32[16,32,128]{2,1,0:T(8,128)}), f32[16,32,128]{2,1,0:T(8,128)S(1)}, u32[]{:S(2)}, u32[]{:S(2)}) %all-to-all-start) | async-done | bytes 262176 | tf_op jit(solution)/shard_map/all_to_all | solution.py:419
  36.9 0.6 scan_total.2
  37.5 9.7 %all_to_all.35.total_ref = f32[4,32,128]{2,1,0:T(8,128)S(1)} all-to-all(f32[4,32,128]{2,1,0:T(8,128)S(1)} %scan_total.2), channel_id=1, replica_groups=mesh['ctx_0'=4,'ctx_1'=16,'row'=4,'core'=2] {'ctx_0'}, dimensions={0} | all-to-all | bytes 131072 | tf_op jit(solution)/shard_map/all_to_all | solution.py:420
  47.2 0.0 copy-start
  47.2 0.0 copy-start.1
  47.2 0.6 scan_prefix.2
  47.8 23.7 %all_to_all.36 = f32[16,32,128]{2,1,0:T(8,128)S(1)} all-to-all(f32[16,32,128]{2,1,0:T(8,128)S(1)} %scan_prefix.2), channel_id=1, replica_groups=mesh['ctx_0'=4,'ctx_1'=16,'row'=4,'core'=2] {'ctx_1'}, dimensions={0} | all-to-all | bytes 524288 | tf_op jit(solution)/shard_map/all_to_all | solution.py:422
  71.5 0.0 copy-done
  71.5 0.0 copy-done.1
  71.5 1.6 %carried.1 = (f32[512,512]{1,0:T(8,128)S(1)}, f32[8,8,128]{2,1,0:T(8,128)S(1)}) custom-call(f32[8,512]{1,0:T(8,128)S(1)} %get-tuple-element.20._.table, bf16[512,512]{1,0:T(8,128)(2,1)S(1)} %copy-done, f32[4,128,128]{2,1,0:T(8,128)S(1)} %bitcast.6, f32[4,128,128]{2,1,0:T(8,128)S(1)} %get-tuple-element.21.first, f32[512,512]{1,0:T(8,128)} %get-tuple-element.22.far_inside, ...), custom_call_target="tpu_custom_call" | custom-call | flops 400000000 | bytes 4000000 | tf_op jit(solution)/shard_map/carried/pallas_call | solution.py:341
  73.2 0.0 copy-start.4
  73.2 9.7 %all_to_all.37.sums = f32[8,8,128]{2,1,0:T(8,128)S(1)} all-to-all(f32[8,8,128]{2,1,0:T(8,128)S(1)} %get-tuple-element.23), channel_id=1, replica_groups=mesh['ctx_0'=4,'ctx_1'=16,'row'=4,'core'=2] {'row','core'}, dimensions={0} | all-to-all | bytes 65536 | tf_op jit(solution)/shard_map/all_to_all | solution.py:472
  82.9 1.6 %grad.1 = f32[4,128,128]{2,1,0:T(8,128)} custom-call(f32[8,512]{1,0:T(8,128)S(1)} %get-tuple-element.20._.table, f32[8,8,128]{2,1,0:T(8,128)S(1)} %all_to_all.37.sums, bf16[512,512]{1,0:T(8,128)(2,1)S(1)} %copy-done, f32[512,512]{1,0:T(8,128)S(1)} %get-tuple-element.24.attention, bf16[512,512]{1,0:T(8,128)(2,1)S(1)} %copy-done.1), custom_call_target="tpu_custom_call" | custom-call | flops 400000000 | bytes 4000000 | tf_op jit(solution)/shard_map/grad/pallas_call | solution.py:341
  84.5 0.0 copy-done.4
  84.5 5.0 %all-to-all-start.4 = ((f32[16,32,128]{2,1,0:T(8,128)}), f32[16,32,128]{2,1,0:T(8,128)S(1)}, u32[]{:S(2)}, u32[]{:S(2)}) async-start(f32[16,32,128]{2,1,0:T(8,128)} %bitcast.9), calls=%async_computation.4 | async-start | bytes 524288 | tf_op jit(solution)/shard_map/all_to_all | solution.py:419
  89.5 0.0 copy-start.5
  89.5 1.2 copy-done.5
  90.7 5.9 %local.1 = (bf16[512,512]{1,0:T(8,128)(2,1)}, bf16[512,512]{1,0:T(8,128)(2,1)}, f32[512,512]{1,0:T(8,128)}, f32[512,512]{1,0:T(8,128)}, f32[4,128,128]{2,1,0:T(8,128)S(1)}) custom-call(f32[4]{0:T(128)} %rates.7, bf16[512,512]{1,0:T(8,128)(2,1)} %queries.7, bf16[512,512]{1,0:T(8,128)(2,1)} %keys.5, bf16[512,512]{1,0:T(8,128)(2,1)} %values.5, ...), custom_call_target="tpu_custom_call" | custom-call | flops 400000000 | bytes 4000000 | tf_op jit(solution)/shard_map/local/pallas_call | solution.py:341
  96.6 10.4 %all-to-all-done.4.piece_ref = f32[16,32,128]{2,1,0:T(8,128)S(1)} async-done(((f32[16,32,128]{2,1,0:T(8,128)}), f32[16,32,128]{2,1,0:T(8,128)S(1)}, u32[]{:S(2)}, u32[]{:S(2)}) %all-to-all-start.4) | async-done | bytes 262176 | tf_op jit(solution)/shard_map/all_to_all | solution.py:419
  107.1 0.6 scan_total.3
  107.7 8.0 %all_to_all.38.total_ref = f32[4,32,128]{2,1,0:T(8,128)S(1)} all-to-all(f32[4,32,128]{2,1,0:T(8,128)S(1)} %scan_total.3), channel_id=1, replica_groups=mesh['ctx_0'=4,'ctx_1'=16,'row'=4,'core'=2] {'ctx_0'}, dimensions={0} | all-to-all | bytes 131072 | tf_op jit(solution)/shard_map/all_to_all | solution.py:420
  115.7 0.0 copy-start.2
  115.7 0.0 copy-start.3
  115.7 0.6 scan_prefix.3
  116.2 23.9 %all_to_all.39 = f32[16,32,128]{2,1,0:T(8,128)S(1)} all-to-all(f32[16,32,128]{2,1,0:T(8,128)S(1)} %scan_prefix.3), channel_id=1, replica_groups=mesh['ctx_0'=4,'ctx_1'=16,'row'=4,'core'=2] {'ctx_1'}, dimensions={0} | all-to-all | bytes 524288 | tf_op jit(solution)/shard_map/all_to_all | solution.py:422
  140.2 0.0 copy-done.2
  140.2 0.0 copy-done.3
  140.2 3.4 %finish.1 = (bf16[512,512]{1,0:T(8,128)(2,1)}, bf16[512,512]{1,0:T(8,128)(2,1)}) custom-call(f32[4]{0:T(128)} %rates.7, bf16[512,512]{1,0:T(8,128)(2,1)S(1)} %copy-done.2, bf16[512,512]{1,0:T(8,128)(2,1)S(1)} %copy-done.3, f32[512,512]{1,0:T(8,128)} %get-tuple-element.27.far_key_part, f32[512,512]{1,0:T(8,128)} %get-tuple-element.28.far_value_part, ...), custom_call_target="tpu_custom_call" | custom-call | flops 400000000 | bytes 4000000 | tf_op jit(solution)/shard_map/finish/pallas_call | solution.py:341
  (1 shorter events, 0.0 us)
Async XLA Ops:
  3.8 33.1 %all-to-all-start = ((f32[16,32,128]{2,1,0:T(8,128)}), f32[16,32,128]{2,1,0:T(8,128)S(1)}, u32[]{:S(2)}, u32[]{:S(2)}) async-start(f32[16,32,128]{2,1,0:T(8,128)} %bitcast.10), calls=%async_computation | async-start | bytes 524288 | tf_op jit(solution)/shard_map/all_to_all | solution.py:419
  19.0 0.7 copy-start.6
  47.2 24.3 %copy-start = (bf16[512,512]{1,0:T(8,128)(2,1)S(1)}, bf16[512,512]{1,0:T(8,128)(2,1)}, u32[]{:S(2)}) copy-start(bf16[512,512]{1,0:T(8,128)(2,1)} %queries.7) | copy-start | bytes 1572868
  47.2 24.3 %copy-start.1 = (bf16[512,512]{1,0:T(8,128)(2,1)S(1)}, bf16[512,512]{1,0:T(8,128)(2,1)}, u32[]{:S(2)}) copy-start(bf16[512,512]{1,0:T(8,128)(2,1)} %out_grad.5) | copy-start | bytes 1572868
  73.2 11.3 %copy-start.4 = (f32[512,512]{1,0:T(8,128)}, f32[512,512]{1,0:T(8,128)S(1)}, u32[]{:S(2)}) copy-start(f32[512,512]{1,0:T(8,128)S(1)} %get-tuple-element.24.attention) | copy-start | bytes 3145732
  84.5 22.6 %all-to-all-start.4 = ((f32[16,32,128]{2,1,0:T(8,128)}), f32[16,32,128]{2,1,0:T(8,128)S(1)}, u32[]{:S(2)}, u32[]{:S(2)}) async-start(f32[16,32,128]{2,1,0:T(8,128)} %bitcast.9), calls=%async_computation.4 | async-start | bytes 524288 | tf_op jit(solution)/shard_map/all_to_all | solution.py:419
  89.5 1.2 copy-start.5
  115.7 24.5 %copy-start.2 = (bf16[512,512]{1,0:T(8,128)(2,1)S(1)}, bf16[512,512]{1,0:T(8,128)(2,1)}, u32[]{:S(2)}) copy-start(bf16[512,512]{1,0:T(8,128)(2,1)} %keys.5) | copy-start | bytes 1572868
  115.7 24.5 %copy-start.3 = (bf16[512,512]{1,0:T(8,128)(2,1)S(1)}, bf16[512,512]{1,0:T(8,128)(2,1)}, u32[]{:S(2)}) copy-start(bf16[512,512]{1,0:T(8,128)(2,1)} %values.5) | copy-start | bytes 1572868

commit v7 on v6

--- a/solution.py
+++ b/solution.py
@@ -267,53 +267,43 @@
                 second[head] = dot_wide_left(queries[rows, cols].astype(F32) * start, grad)
 
 
+def settle_kernel(key_part, value_part, second, settled):
+    settled[...] = key_part[0:8, 0:128] + value_part[0:8, 0:128] + second[0, 0:8, :]
+
+
 def finish_kernel(
-    rates,
+    table,
     keys,
     values,
-    far_key_part,
-    far_value_part,
+    key_part,
+    value_part,
     after,
     second,
     far_key_grad,
     far_value_grad,
-    key_part,
-    value_part,
-    key_more,
-    value_more,
     key_grad,
     value_grad,
-    ready,
     done,
 ):
-    loads, stores = [], []
-    for block in range(2):
-        rows = block_rows(block)
-        pairs = ((far_key_part, key_part), (far_value_part, value_part))
-        loads.append(
-            start_copies([(f.at[rows, :], n.at[rows, :]) for f, n in pairs], ready.at[block])
-        )
+    stores = []
     to_end = BLOCK - rows_of((BLOCK, 128))
     for block in range(2):
         rows = block_rows(block)
         for head in range(4):
             cols = cols_of(head)
-            ending = jnp.exp(-rates[head] * to_end)
+            ending = jnp.exp(-rate_row(table, head) * to_end)
             backlog = after[head]
             if block == 0:
-                full = jnp.exp(jnp.full((128, 128), -BLOCK * rates[head], F32))
+                full = jnp.exp(-BLOCK * rate_row(table, head))
                 backlog = full * backlog + second[head]
-            key_more[:, cols] = dot_wide_right(values[rows, cols], backlog, 1, 1) * ending
-            value_more[:, cols] = dot_wide_right(keys[rows, cols], backlog, 1, 0) * ending
-        wait_all(loads[block])
-        for half in range(4):
-            span = slice(block * BLOCK + half * 64, block * BLOCK + half * 64 + 64)
-            own = slice(half * 64, half * 64 + 64)
-            key_grad[span, :] = (key_part[span, :] + key_more[own, :]).astype(BF16)
-            value_grad[span, :] = (value_part[span, :] + value_more[own, :]).astype(BF16)
+            key_more = dot_wide_right(values[rows, cols], backlog, 1, 1) * ending
+            value_more = dot_wide_right(keys[rows, cols], backlog, 1, 0) * ending
+            key_grad[rows, cols] = (key_part[rows, cols] + key_more).astype(BF16)
+            value_grad[rows, cols] = (value_part[rows, cols] + value_more).astype(BF16)
             pairs = ((key_grad, far_key_grad), (value_grad, far_value_grad))
             stores += start_copies(
-                [(n.at[span, :], f.at[span, :]) for n, f in pairs], done.at[4 * block + half]
+                [(n.at[rows, cols], f.at[rows, cols]) for n, f in pairs],
+                done.at[4 * block + head],
             )
     wait_all(stores)
 
@@ -499,21 +489,27 @@
         grant=None,
         rates=decay_rates,
     )
-    after = along_context(table, backlog_end, True, backlog_second)
-    more = pltpu.VMEM((BLOCK, width), F32)
+    (settled,) = call(
+        settle_kernel,
+        "settle",
+        (pltpu.VMEM((8, 128), F32),),
+        near(key_part),
+        near(value_part),
+        near(backlog_second),
+    )
+    after = along_context(table, backlog_end, True, settled)
     key_grad, value_grad = call(
         finish_kernel,
         "finish",
         (Far(narrow), Far(narrow)),
+        near(aux),
         near(key_rows),
         near(value_rows),
-        Far(key_part),
-        Far(value_part),
+        near(key_part),
+        near(value_part),
         near(after),
         near(backlog_second),
-        grant=None,
-        rates=decay_rates,
-        scratch=(wide_near, wide_near, more, more, narrow_near, narrow_near, flags, pltpu.SemaphoreType.DMA((8, 2))),
+        scratch=(narrow_near, narrow_near, pltpu.SemaphoreType.DMA((8, 2))),
     )
     return (normed_out, query_grad, key_grad, value_grad)
 

time: 144 us -> 142 us (0.986)
  local copies, waits for them, and re-layouts: 2.47 us -> 4.93 us
  waiting for transfers between devices: 22.9 us -> 20.5 us
  Pallas kernels: 21.5 us -> 19.7 us
    all_to_all x2, waiting for transfers between devices: 22.9 us -> 20.5 us  [along_context(): pieces = lax.all_to_all(state.reshape(near_size, -1, lanes), LINE[1], 0, 0)]
    unnamed x14 -> x22, local copies, waits for them, and re-layouts: 1.89 us -> 4.34 us
    pallas_call x6 -> x7, Pallas kernels: 19.2 us -> 17.4 us  [call(): pl.pallas_call(kernel, in_specs=[SMEM] * len(small) + [place_of(item) for...]
where the time goes in v7:
time: 142 us
  blocking collectives  75 us (53%)
  waiting for transfers between devices  20.5 us (14%)
  starting transfers between devices  20.2 us (14%)
  Pallas kernels  19.7 us (14%)
  local copies, waits for them, and re-layouts  4.93 us (3%)
    all_to_all x2, blocking collectives, along_context(): return lax.all_to_all(prefix, LINE[1], 0, 0).reshape(state.shape)  47.6 us
    all_to_all x2, waiting for transfers between devices, along_context(): pieces = lax.all_to_all(state.reshape(near_size, -1, lanes), LINE[1], 0, 0)  20.5 us
    all_to_all x2, starting transfers between devices, along_context(): pieces = lax.all_to_all(state.reshape(near_size, -1, lanes), LINE[1], 0, 0)  20.2 us
    all_to_all x2, blocking collectives, along_context(): lax.all_to_all(scan_total(table, pieces, reverse, filled), LINE[0], 0, 0)  17.7 us
    pallas_call x7, Pallas kernels, call(): pl.pallas_call(kernel, in_specs=[SMEM] * len(small) + [place_of(item) for...  17.4 us
    all_to_all x1, blocking collectives, on_device(): sums = lax.all_to_all(sums, SIDE, 0, 0)  9.71 us
    unnamed x22, local copies, waits for them, and re-layouts  4.34 us
  transfers between devices with their start and end apart: 2, of which 2 were waited for; matrix products, arithmetic and copies ran while one was open for 0% of the time, Pallas kernels for 7%

profile of v7, /device:TPU:32, one launch (start us, length us, event | category | flops | bytes accessed | tf_op | source)
XLA Modules:
  0.0 141.7 jit_solution(17727409642593031742)
XLA Ops:
  0.6 3.1 %memory.1 = (f32[4,128,128]{2,1,0:T(8,128)}, f32[4,128,128]{2,1,0:T(8,128)S(1)}) custom-call(f32[4]{0:T(128)} %rates.5, bf16[512,512]{1,0:T(8,128)(2,1)} %keys.5, bf16[512,512]{1,0:T(8,128)(2,1)} %values.5), custom_call_target="tpu_custom_call" | custom-call | flops 400000000 | bytes 4000000 | tf_op jit(solution)/shard_map/memory/pallas_call | solution.py:331
  3.8 15.2 %all-to-all-start = ((f32[16,32,128]{2,1,0:T(8,128)}), f32[16,32,128]{2,1,0:T(8,128)S(1)}, u32[]{:S(2)}, u32[]{:S(2)}) async-start(f32[16,32,128]{2,1,0:T(8,128)} %bitcast.10), calls=%async_computation | async-start | bytes 524288 | tf_op jit(solution)/shard_map/all_to_all | solution.py:409
  19.0 0.0 copy-start.10
  19.0 0.6 copy-done.10
  19.6 0.6 dynamic_slice.4
  20.9 3.5 %inside.1 = (bf16[4,2,256,256]{3,2,1,0:T(8,128)(2,1)}, f32[512,512]{1,0:T(8,128)}, f32[8,512]{1,0:T(8,128)S(1)}) custom-call(f32[4]{0:T(128)} %rates.5, bf16[512,512]{1,0:T(8,128)(2,1)} %queries.7, bf16[512,512]{1,0:T(8,128)(2,1)} %keys.5, bf16[512,512]{1,0:T(8,128)(2,1)} %values.5, f32[1,512]{1,0:T(1,128)} %bitcast.11), custom_call_target="tpu_custom_call" | custom-call | flops 400000000 | bytes 4000000 | tf_op jit(solution)/shard_map/inside/pallas_call | solution.py:331
  24.4 12.5 %all-to-all-done.piece_ref = f32[16,32,128]{2,1,0:T(8,128)S(1)} async-done(((f32[16,32,128]{2,1,0:T(8,128)}), f32[16,32,128]{2,1,0:T(8,128)S(1)}, u32[]{:S(2)}, u32[]{:S(2)}) %all-to-all-start) | async-done | bytes 262176 | tf_op jit(solution)/shard_map/all_to_all | solution.py:409
  36.9 0.6 scan_total.2
  37.5 9.7 %all_to_all.35.total_ref = f32[4,32,128]{2,1,0:T(8,128)S(1)} all-to-all(f32[4,32,128]{2,1,0:T(8,128)S(1)} %scan_total.2), channel_id=1, replica_groups=mesh['ctx_0'=4,'ctx_1'=16,'row'=4,'core'=2] {'ctx_0'}, dimensions={0} | all-to-all | bytes 131072 | tf_op jit(solution)/shard_map/all_to_all | solution.py:410
  47.2 0.0 copy-start
  47.2 0.0 copy-start.3
  47.2 0.6 scan_prefix.2
  47.8 23.7 %all_to_all.36 = f32[16,32,128]{2,1,0:T(8,128)S(1)} all-to-all(f32[16,32,128]{2,1,0:T(8,128)S(1)} %scan_prefix.2), channel_id=1, replica_groups=mesh['ctx_0'=4,'ctx_1'=16,'row'=4,'core'=2] {'ctx_1'}, dimensions={0} | all-to-all | bytes 524288 | tf_op jit(solution)/shard_map/all_to_all | solution.py:412
  71.5 0.0 copy-done
  71.5 0.0 copy-done.3
  71.5 1.6 %carried.1 = (f32[512,512]{1,0:T(8,128)S(1)}, f32[8,8,128]{2,1,0:T(8,128)S(1)}) custom-call(f32[8,512]{1,0:T(8,128)S(1)} %get-tuple-element.20._.table, bf16[512,512]{1,0:T(8,128)(2,1)S(1)} %copy-done, f32[4,128,128]{2,1,0:T(8,128)S(1)} %bitcast.6, f32[4,128,128]{2,1,0:T(8,128)S(1)} %get-tuple-element.21.first, f32[512,512]{1,0:T(8,128)} %get-tuple-element.22.far_inside, ...), custom_call_target="tpu_custom_call" | custom-call | flops 400000000 | bytes 4000000 | tf_op jit(solution)/shard_map/carried/pallas_call | solution.py:331
  73.2 0.0 copy-start.8
  73.2 9.7 %all_to_all.37.sums = f32[8,8,128]{2,1,0:T(8,128)S(1)} all-to-all(f32[8,8,128]{2,1,0:T(8,128)S(1)} %get-tuple-element.23), channel_id=1, replica_groups=mesh['ctx_0'=4,'ctx_1'=16,'row'=4,'core'=2] {'row','core'}, dimensions={0} | all-to-all | bytes 65536 | tf_op jit(solution)/shard_map/all_to_all | solution.py:462
  82.9 1.6 %grad.1 = f32[4,128,128]{2,1,0:T(8,128)} custom-call(f32[8,512]{1,0:T(8,128)S(1)} %get-tuple-element.20._.table, f32[8,8,128]{2,1,0:T(8,128)S(1)} %all_to_all.37.sums, bf16[512,512]{1,0:T(8,128)(2,1)S(1)} %copy-done, f32[512,512]{1,0:T(8,128)S(1)} %get-tuple-element.24.attention, bf16[512,512]{1,0:T(8,128)(2,1)S(1)} %copy-done.3), custom_call_target="tpu_custom_call" | custom-call | flops 400000000 | bytes 4000000 | tf_op jit(solution)/shard_map/grad/pallas_call | solution.py:331
  84.5 0.0 copy-done.8
  84.5 5.0 %all-to-all-start.4 = ((f32[16,32,128]{2,1,0:T(8,128)}), f32[16,32,128]{2,1,0:T(8,128)S(1)}, u32[]{:S(2)}, u32[]{:S(2)}) async-start(f32[16,32,128]{2,1,0:T(8,128)} %bitcast.9), calls=%async_computation.4 | async-start | bytes 524288 | tf_op jit(solution)/shard_map/all_to_all | solution.py:409
  89.5 0.0 copy-start.9
  89.5 1.2 copy-done.9
  90.7 5.9 %local.1 = (bf16[512,512]{1,0:T(8,128)(2,1)}, bf16[512,512]{1,0:T(8,128)(2,1)}, f32[512,512]{1,0:T(8,128)}, f32[512,512]{1,0:T(8,128)}, f32[4,128,128]{2,1,0:T(8,128)S(1)}) custom-call(f32[4]{0:T(128)} %rates.5, bf16[512,512]{1,0:T(8,128)(2,1)} %queries.7, bf16[512,512]{1,0:T(8,128)(2,1)} %keys.5, bf16[512,512]{1,0:T(8,128)(2,1)} %values.5, ...), custom_call_target="tpu_custom_call" | custom-call | flops 400000000 | bytes 4000000 | tf_op jit(solution)/shard_map/local/pallas_call | solution.py:331
  96.6 0.0 copy-start.4
  96.6 1.2 copy-done.4
  97.9 0.0 copy-start.6
  97.9 1.2 copy-done.6
  99.1 0.0 copy-start.5
  99.1 0.0 copy-start.7
  99.1 8.0 %all-to-all-done.4.piece_ref = f32[16,32,128]{2,1,0:T(8,128)S(1)} async-done(((f32[16,32,128]{2,1,0:T(8,128)}), f32[16,32,128]{2,1,0:T(8,128)S(1)}, u32[]{:S(2)}, u32[]{:S(2)}) %all-to-all-start.4) | async-done | bytes 262176 | tf_op jit(solution)/shard_map/all_to_all | solution.py:409
  107.1 0.6 scan_total.3
  107.7 8.0 %all_to_all.38.total_ref = f32[4,32,128]{2,1,0:T(8,128)S(1)} all-to-all(f32[4,32,128]{2,1,0:T(8,128)S(1)} %scan_total.3), channel_id=1, replica_groups=mesh['ctx_0'=4,'ctx_1'=16,'row'=4,'core'=2] {'ctx_0'}, dimensions={0} | all-to-all | bytes 131072 | tf_op jit(solution)/shard_map/all_to_all | solution.py:410
  115.7 0.0 copy-start.1
  115.7 0.0 copy-start.2
  115.7 0.6 scan_prefix.3
  116.3 23.9 %all_to_all.39 = f32[16,32,128]{2,1,0:T(8,128)S(1)} all-to-all(f32[16,32,128]{2,1,0:T(8,128)S(1)} %scan_prefix.3), channel_id=1, replica_groups=mesh['ctx_0'=4,'ctx_1'=16,'row'=4,'core'=2] {'ctx_1'}, dimensions={0} | all-to-all | bytes 524288 | tf_op jit(solution)/shard_map/all_to_all | solution.py:412
  140.2 0.0 copy-done.5
  140.2 0.0 copy-done.7
  140.2 0.0 copy-done.1
  140.2 0.0 copy-done.2
  140.2 1.5 %finish.1 = (bf16[512,512]{1,0:T(8,128)(2,1)}, bf16[512,512]{1,0:T(8,128)(2,1)}) custom-call(f32[8,512]{1,0:T(8,128)S(1)} %get-tuple-element.20._.table, bf16[512,512]{1,0:T(8,128)(2,1)S(1)} %copy-done.1, bf16[512,512]{1,0:T(8,128)(2,1)S(1)} %copy-done.2, f32[512,512]{1,0:T(8,128)S(1)} %copy-done.5, f32[512,512]{1,0:T(8,128)S(1)} %copy-done.7, ...), custom_call_target="tpu_custom_call" | custom-call | flops 400000000 | bytes 4000000 | tf_op jit(solution)/shard_map/finish/pallas_call | solution.py:331
  (2 shorter events, 0.0 us)
Async XLA Ops:
  3.8 33.1 %all-to-all-start = ((f32[16,32,128]{2,1,0:T(8,128)}), f32[16,32,128]{2,1,0:T(8,128)S(1)}, u32[]{:S(2)}, u32[]{:S(2)}) async-start(f32[16,32,128]{2,1,0:T(8,128)} %bitcast.10), calls=%async_computation | async-start | bytes 524288 | tf_op jit(solution)/shard_map/all_to_all | solution.py:409
  19.0 0.7 copy-start.10
  47.2 24.3 %copy-start = (bf16[512,512]{1,0:T(8,128)(2,1)S(1)}, bf16[512,512]{1,0:T(8,128)(2,1)}, u32[]{:S(2)}) copy-start(bf16[512,512]{1,0:T(8,128)(2,1)} %queries.7) | copy-start | bytes 1572868
  47.2 24.3 %copy-start.3 = (bf16[512,512]{1,0:T(8,128)(2,1)S(1)}, bf16[512,512]{1,0:T(8,128)(2,1)}, u32[]{:S(2)}) copy-start(bf16[512,512]{1,0:T(8,128)(2,1)} %out_grad.5) | copy-start | bytes 1572868
  73.2 11.3 %copy-start.8 = (f32[512,512]{1,0:T(8,128)}, f32[512,512]{1,0:T(8,128)S(1)}, u32[]{:S(2)}) copy-start(f32[512,512]{1,0:T(8,128)S(1)} %get-tuple-element.24.attention) | copy-start | bytes 3145732
  84.5 22.6 %all-to-all-start.4 = ((f32[16,32,128]{2,1,0:T(8,128)}), f32[16,32,128]{2,1,0:T(8,128)S(1)}, u32[]{:S(2)}, u32[]{:S(2)}) async-start(f32[16,32,128]{2,1,0:T(8,128)} %bitcast.9), calls=%async_computation.4 | async-start | bytes 524288 | tf_op jit(solution)/shard_map/all_to_all | solution.py:409
  89.5 1.2 copy-start.9
  96.6 1.2 copy-start.4
  97.9 1.2 copy-start.6
  99.1 41.1 %copy-start.5 = (f32[512,512]{1,0:T(8,128)S(1)}, f32[512,512]{1,0:T(8,128)}, u32[]{:S(2)}) copy-start(f32[512,512]{1,0:T(8,128)} %get-tuple-element.27.key_part) | copy-start | bytes 3145732
  99.1 41.1 %copy-start.7 = (f32[512,512]{1,0:T(8,128)S(1)}, f32[512,512]{1,0:T(8,128)}, u32[]{:S(2)}) copy-start(f32[512,512]{1,0:T(8,128)} %get-tuple-element.28.value_part) | copy-start | bytes 3145732
  115.7 24.5 %copy-start.1 = (bf16[512,512]{1,0:T(8,128)(2,1)S(1)}, bf16[512,512]{1,0:T(8,128)(2,1)}, u32[]{:S(2)}) copy-start(bf16[512,512]{1,0:T(8,128)(2,1)} %keys.5) | copy-start | bytes 1572868
  115.7 24.5 %copy-start.2 = (bf16[512,512]{1,0:T(8,128)(2,1)S(1)}, bf16[512,512]{1,0:T(8,128)(2,1)}, u32[]{:S(2)}) copy-start(bf16[512,512]{1,0:T(8,128)(2,1)} %values.5) | copy-start | bytes 1572868

commit v8 on v7

--- a/solution.py
+++ b/solution.py
@@ -156,6 +156,8 @@
             leading = jnp.exp(-rate_row(table, head) * after_start)
             carried = dot_wide_right(queries[rows, cols], memory, 1, 0)
             attention[rows, cols] = carried * leading
+    for block in range(2):
+        rows = block_rows(block)
         loads[block].wait()
         square = product = None
         for head in range(4):
@@ -202,23 +204,22 @@
 ):
     stores = []
     from_start = rows_of((BLOCK, 128))
-    for block in (1, 0):
-        rows = block_rows(block)
-        scale, coeff = scales_of(features, sums, block)
-        for head in range(4):
-            cols = cols_of(head)
+    scales = [scales_of(features, sums, block) for block in range(2)]
+    for head in range(4):
+        cols = cols_of(head)
+        start = jnp.exp(-rate_row(table, head) * from_start)
+        gathered = []
+        for block in range(2):
+            rows = block_rows(block)
+            scale, coeff = scales[block]
             _, low = attention_grad(
                 attention[rows, cols], out_grad[rows, cols], table[0:1, cols], scale, coeff
             )
-            start = jnp.exp(-rate_row(table, head) * from_start)
-            gathered = dot_wide_left(queries[rows, cols].astype(F32) * start, low)
-            if block == 1:
-                end[head] = gathered
-            else:
-                end[head] = jnp.exp(-BLOCK * rate_row(table, head)) * end[head] + gathered
-                store = pltpu.make_async_copy(end.at[head], far_end.at[head], done.at[head])
-                store.start()
-                stores.append(store)
+            gathered.append(dot_wide_left(queries[rows, cols].astype(F32) * start, low))
+        end[head] = jnp.exp(-BLOCK * rate_row(table, head)) * gathered[1] + gathered[0]
+        store = pltpu.make_async_copy(end.at[head], far_end.at[head], done.at[head])
+        store.start()
+        stores.append(store)
     wait_all(stores)
 
 

time: 142 us -> 142 us (level)
  no operation moved by 1% of the time
where the time goes in v8:
time: 142 us
  blocking collectives  75 us (53%)
  waiting for transfers between devices  20.5 us (14%)
  starting transfers between devices  20.2 us (14%)
  Pallas kernels  19.5 us (14%)
  local copies, waits for them, and re-layouts  4.93 us (3%)
    all_to_all x2, blocking collectives, along_context(): return lax.all_to_all(prefix, LINE[1], 0, 0).reshape(state.shape)  47.6 us
    all_to_all x2, waiting for transfers between devices, along_context(): pieces = lax.all_to_all(state.reshape(near_size, -1, lanes), LINE[1], 0, 0)  20.5 us
    all_to_all x2, starting transfers between devices, along_context(): pieces = lax.all_to_all(state.reshape(near_size, -1, lanes), LINE[1], 0, 0)  20.2 us
    all_to_all x2, blocking collectives, along_context(): lax.all_to_all(scan_total(table, pieces, reverse, filled), LINE[0], 0, 0)  17.7 us
    pallas_call x7, Pallas kernels, call(): pl.pallas_call(kernel, in_specs=[SMEM] * len(small) + [place_of(item) for...  17.2 us
    all_to_all x1, blocking collectives, on_device(): sums = lax.all_to_all(sums, SIDE, 0, 0)  9.71 us
    unnamed x22, local copies, waits for them, and re-layouts  4.34 us
  transfers between devices with their start and end apart: 2, of which 2 were waited for; matrix products, arithmetic and copies ran while one was open for 0% of the time, Pallas kernels for 7%

profile of v8, /device:TPU:32, one launch (start us, length us, event | category | flops | bytes accessed | tf_op | source)
XLA Modules:
  0.0 141.6 jit_solution(16757662741651799511)
XLA Ops:
  0.6 3.1 %memory.1 = (f32[4,128,128]{2,1,0:T(8,128)}, f32[4,128,128]{2,1,0:T(8,128)S(1)}) custom-call(f32[4]{0:T(128)} %rates.5, bf16[512,512]{1,0:T(8,128)(2,1)} %keys.5, bf16[512,512]{1,0:T(8,128)(2,1)} %values.5), custom_call_target="tpu_custom_call" | custom-call | flops 400000000 | bytes 4000000 | tf_op jit(solution)/shard_map/memory/pallas_call | solution.py:332
  3.8 15.2 %all-to-all-start = ((f32[16,32,128]{2,1,0:T(8,128)}), f32[16,32,128]{2,1,0:T(8,128)S(1)}, u32[]{:S(2)}, u32[]{:S(2)}) async-start(f32[16,32,128]{2,1,0:T(8,128)} %bitcast.10), calls=%async_computation | async-start | bytes 524288 | tf_op jit(solution)/shard_map/all_to_all | solution.py:410
  19.0 0.0 copy-start.10
  19.0 0.6 copy-done.10
  19.6 0.6 dynamic_slice.4
  20.9 3.5 %inside.1 = (bf16[4,2,256,256]{3,2,1,0:T(8,128)(2,1)}, f32[512,512]{1,0:T(8,128)}, f32[8,512]{1,0:T(8,128)S(1)}) custom-call(f32[4]{0:T(128)} %rates.5, bf16[512,512]{1,0:T(8,128)(2,1)} %queries.7, bf16[512,512]{1,0:T(8,128)(2,1)} %keys.5, bf16[512,512]{1,0:T(8,128)(2,1)} %values.5, f32[1,512]{1,0:T(1,128)} %bitcast.11), custom_call_target="tpu_custom_call" | custom-call | flops 400000000 | bytes 4000000 | tf_op jit(solution)/shard_map/inside/pallas_call | solution.py:332
  24.4 12.5 %all-to-all-done.piece_ref = f32[16,32,128]{2,1,0:T(8,128)S(1)} async-done(((f32[16,32,128]{2,1,0:T(8,128)}), f32[16,32,128]{2,1,0:T(8,128)S(1)}, u32[]{:S(2)}, u32[]{:S(2)}) %all-to-all-start) | async-done | bytes 262176 | tf_op jit(solution)/shard_map/all_to_all | solution.py:410
  36.9 0.6 scan_total.2
  37.5 9.7 %all_to_all.35.total_ref = f32[4,32,128]{2,1,0:T(8,128)S(1)} all-to-all(f32[4,32,128]{2,1,0:T(8,128)S(1)} %scan_total.2), channel_id=1, replica_groups=mesh['ctx_0'=4,'ctx_1'=16,'row'=4,'core'=2] {'ctx_0'}, dimensions={0} | all-to-all | bytes 131072 | tf_op jit(solution)/shard_map/all_to_all | solution.py:411
  47.2 0.0 copy-start
  47.2 0.0 copy-start.3
  47.2 0.6 scan_prefix.2
  47.8 23.7 %all_to_all.36 = f32[16,32,128]{2,1,0:T(8,128)S(1)} all-to-all(f32[16,32,128]{2,1,0:T(8,128)S(1)} %scan_prefix.2), channel_id=1, replica_groups=mesh['ctx_0'=4,'ctx_1'=16,'row'=4,'core'=2] {'ctx_1'}, dimensions={0} | all-to-all | bytes 524288 | tf_op jit(solution)/shard_map/all_to_all | solution.py:413
  71.5 0.0 copy-done
  71.5 0.0 copy-done.3
  71.5 1.5 %carried.1 = (f32[512,512]{1,0:T(8,128)S(1)}, f32[8,8,128]{2,1,0:T(8,128)S(1)}) custom-call(f32[8,512]{1,0:T(8,128)S(1)} %get-tuple-element.20._.table, bf16[512,512]{1,0:T(8,128)(2,1)S(1)} %copy-done, f32[4,128,128]{2,1,0:T(8,128)S(1)} %bitcast.6, f32[4,128,128]{2,1,0:T(8,128)S(1)} %get-tuple-element.21.first, f32[512,512]{1,0:T(8,128)} %get-tuple-element.22.far_inside, ...), custom_call_target="tpu_custom_call" | custom-call | flops 400000000 | bytes 4000000 | tf_op jit(solution)/shard_map/carried/pallas_call | solution.py:332
  73.1 0.0 copy-start.8
  73.1 9.7 %all_to_all.37.sums = f32[8,8,128]{2,1,0:T(8,128)S(1)} all-to-all(f32[8,8,128]{2,1,0:T(8,128)S(1)} %get-tuple-element.23), channel_id=1, replica_groups=mesh['ctx_0'=4,'ctx_1'=16,'row'=4,'core'=2] {'row','core'}, dimensions={0} | all-to-all | bytes 65536 | tf_op jit(solution)/shard_map/all_to_all | solution.py:463
  82.8 1.6 %grad.1 = f32[4,128,128]{2,1,0:T(8,128)} custom-call(f32[8,512]{1,0:T(8,128)S(1)} %get-tuple-element.20._.table, f32[8,8,128]{2,1,0:T(8,128)S(1)} %all_to_all.37.sums, bf16[512,512]{1,0:T(8,128)(2,1)S(1)} %copy-done, f32[512,512]{1,0:T(8,128)S(1)} %get-tuple-element.24.attention, bf16[512,512]{1,0:T(8,128)(2,1)S(1)} %copy-done.3), custom_call_target="tpu_custom_call" | custom-call | flops 400000000 | bytes 4000000 | tf_op jit(solution)/shard_map/grad/pallas_call | solution.py:332
  84.4 0.0 copy-done.8
  84.4 5.0 %all-to-all-start.4 = ((f32[16,32,128]{2,1,0:T(8,128)}), f32[16,32,128]{2,1,0:T(8,128)S(1)}, u32[]{:S(2)}, u32[]{:S(2)}) async-start(f32[16,32,128]{2,1,0:T(8,128)} %bitcast.9), calls=%async_computation.4 | async-start | bytes 524288 | tf_op jit(solution)/shard_map/all_to_all | solution.py:410
  89.4 0.0 copy-start.9
  89.4 1.2 copy-done.9
  90.6 5.9 %local.1 = (bf16[512,512]{1,0:T(8,128)(2,1)}, bf16[512,512]{1,0:T(8,128)(2,1)}, f32[512,512]{1,0:T(8,128)}, f32[512,512]{1,0:T(8,128)}, f32[4,128,128]{2,1,0:T(8,128)S(1)}) custom-call(f32[4]{0:T(128)} %rates.5, bf16[512,512]{1,0:T(8,128)(2,1)} %queries.7, bf16[512,512]{1,0:T(8,128)(2,1)} %keys.5, bf16[512,512]{1,0:T(8,128)(2,1)} %values.5, ...), custom_call_target="tpu_custom_call" | custom-call | flops 400000000 | bytes 4000000 | tf_op jit(solution)/shard_map/local/pallas_call | solution.py:332
  96.5 0.0 copy-start.4
  96.5 1.2 copy-done.4
  97.7 0.0 copy-start.6
  97.7 1.2 copy-done.6
  99.0 0.0 copy-start.5
  99.0 0.0 copy-start.7
  99.0 8.0 %all-to-all-done.4.piece_ref = f32[16,32,128]{2,1,0:T(8,128)S(1)} async-done(((f32[16,32,128]{2,1,0:T(8,128)}), f32[16,32,128]{2,1,0:T(8,128)S(1)}, u32[]{:S(2)}, u32[]{:S(2)}) %all-to-all-start.4) | async-done | bytes 262176 | tf_op jit(solution)/shard_map/all_to_all | solution.py:410
  106.9 0.6 scan_total.3
  107.5 8.0 %all_to_all.38.total_ref = f32[4,32,128]{2,1,0:T(8,128)S(1)} all-to-all(f32[4,32,128]{2,1,0:T(8,128)S(1)} %scan_total.3), channel_id=1, replica_groups=mesh['ctx_0'=4,'ctx_1'=16,'row'=4,'core'=2] {'ctx_0'}, dimensions={0} | all-to-all | bytes 131072 | tf_op jit(solution)/shard_map/all_to_all | solution.py:411
  115.5 0.0 copy-start.1
  115.5 0.0 copy-start.2
  115.5 0.6 scan_prefix.3
  116.1 23.9 %all_to_all.39 = f32[16,32,128]{2,1,0:T(8,128)S(1)} all-to-all(f32[16,32,128]{2,1,0:T(8,128)S(1)} %scan_prefix.3), channel_id=1, replica_groups=mesh['ctx_0'=4,'ctx_1'=16,'row'=4,'core'=2] {'ctx_1'}, dimensions={0} | all-to-all | bytes 524288 | tf_op jit(solution)/shard_map/all_to_all | solution.py:413
  140.0 0.0 copy-done.5
  140.0 0.0 copy-done.7
  140.0 0.0 copy-done.1
  140.0 0.0 copy-done.2
  140.0 1.5 %finish.1 = (bf16[512,512]{1,0:T(8,128)(2,1)}, bf16[512,512]{1,0:T(8,128)(2,1)}) custom-call(f32[8,512]{1,0:T(8,128)S(1)} %get-tuple-element.20._.table, bf16[512,512]{1,0:T(8,128)(2,1)S(1)} %copy-done.1, bf16[512,512]{1,0:T(8,128)(2,1)S(1)} %copy-done.2, f32[512,512]{1,0:T(8,128)S(1)} %copy-done.5, f32[512,512]{1,0:T(8,128)S(1)} %copy-done.7, ...), custom_call_target="tpu_custom_call" | custom-call | flops 400000000 | bytes 4000000 | tf_op jit(solution)/shard_map/finish/pallas_call | solution.py:332
  (2 shorter events, 0.0 us)
Async XLA Ops:
  3.8 33.1 %all-to-all-start = ((f32[16,32,128]{2,1,0:T(8,128)}), f32[16,32,128]{2,1,0:T(8,128)S(1)}, u32[]{:S(2)}, u32[]{:S(2)}) async-start(f32[16,32,128]{2,1,0:T(8,128)} %bitcast.10), calls=%async_computation | async-start | bytes 524288 | tf_op jit(solution)/shard_map/all_to_all | solution.py:410
  19.0 0.7 copy-start.10
  47.2 24.3 %copy-start = (bf16[512,512]{1,0:T(8,128)(2,1)S(1)}, bf16[512,512]{1,0:T(8,128)(2,1)}, u32[]{:S(2)}) copy-start(bf16[512,512]{1,0:T(8,128)(2,1)} %queries.7) | copy-start | bytes 1572868
  47.2 24.3 %copy-start.3 = (bf16[512,512]{1,0:T(8,128)(2,1)S(1)}, bf16[512,512]{1,0:T(8,128)(2,1)}, u32[]{:S(2)}) copy-start(bf16[512,512]{1,0:T(8,128)(2,1)} %out_grad.5) | copy-start | bytes 1572868
  73.1 11.3 %copy-start.8 = (f32[512,512]{1,0:T(8,128)}, f32[512,512]{1,0:T(8,128)S(1)}, u32[]{:S(2)}) copy-start(f32[512,512]{1,0:T(8,128)S(1)} %get-tuple-element.24.attention) | copy-start | bytes 3145732
  84.4 22.6 %all-to-all-start.4 = ((f32[16,32,128]{2,1,0:T(8,128)}), f32[16,32,128]{2,1,0:T(8,128)S(1)}, u32[]{:S(2)}, u32[]{:S(2)}) async-start(f32[16,32,128]{2,1,0:T(8,128)} %bitcast.9), calls=%async_computation.4 | async-start | bytes 524288 | tf_op jit(solution)/shard_map/all_to_all | solution.py:410
  89.4 1.2 copy-start.9
  96.5 1.2 copy-start.4
  97.7 1.2 copy-start.6
  99.0 41.1 %copy-start.5 = (f32[512,512]{1,0:T(8,128)S(1)}, f32[512,512]{1,0:T(8,128)}, u32[]{:S(2)}) copy-start(f32[512,512]{1,0:T(8,128)} %get-tuple-element.27.key_part) | copy-start | bytes 3145732
  99.0 41.1 %copy-start.7 = (f32[512,512]{1,0:T(8,128)S(1)}, f32[512,512]{1,0:T(8,128)}, u32[]{:S(2)}) copy-start(f32[512,512]{1,0:T(8,128)} %get-tuple-element.28.value_part) | copy-start | bytes 3145732
  115.5 24.5 %copy-start.1 = (bf16[512,512]{1,0:T(8,128)(2,1)S(1)}, bf16[512,512]{1,0:T(8,128)(2,1)}, u32[]{:S(2)}) copy-start(bf16[512,512]{1,0:T(8,128)(2,1)} %keys.5) | copy-start | bytes 1572868
  115.5 24.5 %copy-start.2 = (bf16[512,512]{1,0:T(8,128)(2,1)S(1)}, bf16[512,512]{1,0:T(8,128)(2,1)}, u32[]{:S(2)}) copy-start(bf16[512,512]{1,0:T(8,128)(2,1)} %values.5) | copy-start | bytes 1572868
